TPU v7x, 256 devices: a whole 4x4x8 slice. The times are simulated.
256 devices in a mesh: beam: 4 (over y), row: 4 (over x), col: 16 (over z, core).
Axes of the slice: x: 4, y: 4, z: 8, core: 2. Of those that a mesh axis runs over, the one named last changes fastest.
Arguments:
- phase_volume: bfloat16 [64, 1024, 2048], P('beam', 'row', 'col'), may hold values from -0.75 to 0.75
- absorb_volume: bfloat16 [64, 1024, 2048], P('beam', 'row', 'col'), may hold values from -0.375 to 0.375
- probe: float32 [2, 256, 256], replicated, may hold values from -6 to 6
- amplitudes: bfloat16 [4, 16, 32, 256, 256], P('row', 'col', 'beam'), may hold values from 0.19921875 to 2.5
- scan_rows: int32 [4, 16, 32], P('row', 'col', 'beam'), may hold values from 0 to 255
- scan_cols: int32 [4, 16, 32], P('row', 'col', 'beam'), may hold values from 0 to 127
Outputs:
- object_step: float32 [2, 1024, 2048], P(None, 'row', 'col')
- probe_gradient: float32 [2, 256, 256], replicated
- loss: float32 [], replicated
All inputs are finite; a program needn't handle non-finite values.
Results may differ from a plain program's by a relative error of at most 0.00055.
The roundings to bfloat16 on the way count: a program that leaves them out, or rounds other values in their place, can miss the bound.
Values sent between devices are 32-bit elements; how exact they have to be, the bound alone decides.
A program may use at most 64 MiB of HBM per device.

v0:
```python
import math

import jax
import jax.numpy as jnp
from jax import lax
from jax.sharding import Mesh
from jax.sharding import PartitionSpec as P

COL = ("col_0", "col_1")
ROW_COL = ("row", "col_0", "col_1")


def from_behind(value, axis, steps):
    count = lax.axis_size(axis)
    first, last = (max(0, -steps), min(count, count - steps))
    return lax.ppermute(value, axis, [(source, source + steps) for source in range(first, last)])


def sent_to_all(x, axis):
    copies = jnp.broadcast_to(x, (lax.axis_size(axis), *x.shape))
    return lax.all_to_all(copies, axis, split_axis=0, concat_axis=0, tiled=True)


def over_copies(x, axis):
    return sent_to_all(x, axis).sum(axis=0)


def in_one(arrays, axis):
    line, at, finished = (jnp.concatenate([a.reshape(-1) for a in arrays]), 0, [])
    so_far = over_copies(line, axis)
    for a in arrays:
        finished.append(so_far[at : at + a.size].reshape(a.shape))
        at += a.size
    return tuple(finished)


def extended(cells, sides, width):
    for axis, dim in sides:
        count = lax.axis_size(axis)
        ends = count - 1
        head = lax.slice_in_dim(cells, 0, width, axis=dim)
        tail = lax.slice_in_dim(cells, cells.shape[dim] - width, cells.shape[dim], axis=dim)
        cells = jnp.concatenate(
            [
                lax.ppermute(tail, axis, [(i, (i + 1) % count) for i in range(ends)]),
                cells,
                lax.ppermute(head, axis, [((i + 1) % count, i) for i in range(ends)]),
            ],
            axis=dim,
        )
    return cells


def rows_for(lines, length):
    spare = -lines.shape[0] % length
    if not spare:
        return lines
    return jnp.concatenate([lines, jnp.zeros((spare, *lines.shape[1:]), lines.dtype)])


def joined_along(parts, dim):
    parts = jnp.moveaxis(parts, 0, dim)
    dims = parts.shape
    return parts.reshape(*dims[:dim], dims[dim] * dims[dim + 1], *dims[dim + 2 :])


def gather_axes(x, axes, dim):
    far, near = axes
    parts = sent_to_all(sent_to_all(x, far), near)
    return joined_along(parts.swapaxes(0, 1).reshape(-1, *x.shape), dim)


def cut_along(x, dim, length):
    before, after = (x.shape[:dim], x.shape[dim + 1 :])
    return jnp.moveaxis(x.reshape(*before, length, -1, *after), dim, 0)


def summed_on_arrival(x, axis, dim):
    length = lax.axis_size(axis)
    parts = lax.all_to_all(cut_along(x, dim, length), axis, 0, 0, tiled=True)
    return jnp.sum(parts, axis=0)


def summed_rows(x, axes, dim):
    far, near = axes
    own = summed_on_arrival(cut_along(x, dim, lax.axis_size(far)), near, dim + 1)
    return jnp.sum(lax.all_to_all(own, far, 0, 0, tiled=True), axis=0)


def sum_by_parts(x, axes):
    padded = rows_for(x, lax.axis_size(axes[0]) * lax.axis_size(axes[1]))
    whole = gather_axes(summed_rows(padded, axes, 0), axes, 0)
    return lax.slice_in_dim(whole, 0, len(x)).reshape(x.shape)


def packed_total(arrays, axis):
    ends = [0]
    for a in arrays:
        ends.append(ends[-1] + a.size)
    so_far = sum_by_parts(jnp.concatenate([a.ravel() for a in arrays]), axis)
    return tuple((so_far[b:e].reshape(a.shape) for a, b, e in zip(arrays, ends, ends[1:])))


def dft_tables(length):
    indices = jnp.arange(length, dtype=jnp.int32)
    product = indices[:, None] * indices[None, :] % length
    angles = product.astype(jnp.float32) * (2.0 * math.pi / length)
    factor = 1.0 / math.sqrt(length)
    return (
        (jnp.cos(angles) * factor).astype(jnp.bfloat16),
        (-jnp.sin(angles) * factor).astype(jnp.bfloat16),
    )


def fold_rims(canvas, half):
    rows_inner = canvas.shape[1] - 2 * half
    cols_inner = canvas.shape[2] - 2 * half
    middle = canvas[:, :, half : half + cols_inner]
    from_right = from_behind(canvas[:, :, :half], COL, -1)
    from_left = from_behind(canvas[:, :, half + cols_inner :], COL, 1)
    middle = middle + from_right
    middle = middle + from_left
    center = middle[:, half : half + rows_inner, :]
    from_below = from_behind(middle[:, :half, :], "row", -1)
    from_above = from_behind(middle[:, half + rows_inner :, :], "row", 1)
    center = center + jnp.pad(from_below, ((0, 0), (rows_inner - half, 0), (0, 0)))
    return center + jnp.pad(from_above, ((0, 0), (0, rows_inner - half), (0, 0)))


def local(phase_volume, absorb_volume, probe, amplitudes, scan_rows, scan_cols):
    length = probe.shape[1]
    half = length // 2
    count = scan_rows.shape[2]
    rows_local = phase_volume.shape[1]
    cols_local = phase_volume.shape[2]
    phase_part = jnp.sum(phase_volume, axis=0, dtype=jnp.float32)
    absorb_part = jnp.sum(absorb_volume, axis=0, dtype=jnp.float32)
    phase_sum, absorb_sum = in_one((phase_part, absorb_part), "beam")
    padded = extended(jnp.stack([phase_sum, absorb_sum]), (("row", 1), (COL, 2)), half)
    row_begin = scan_rows.reshape(count)
    col_begin = scan_cols.reshape(count)
    zero_index = jnp.zeros((), jnp.int32)
    windows = jax.vmap(
        lambda row_at, col_at: lax.dynamic_slice(
            padded, (zero_index, row_at, col_at), (2, length, length)
        )
    )(row_begin, col_begin)
    table_real, table_imag = dft_tables(length)
    negated = -table_imag
    forward_left = jnp.stack(
        [jnp.stack([table_real, negated]), jnp.stack([table_imag, table_real])]
    )
    forward_right = jnp.stack(
        [
            jnp.concatenate([table_real, table_imag], axis=1),
            jnp.concatenate([negated, table_real], axis=1),
        ]
    )
    backward_left = jnp.stack(
        [jnp.stack([table_real, table_imag]), jnp.stack([negated, table_real])]
    )
    backward_right = jnp.stack(
        [
            jnp.concatenate([table_real, negated], axis=1),
            jnp.concatenate([table_imag, table_real], axis=1),
        ]
    )
    damping = jnp.exp(-windows[:, 1])
    trans_real = damping * jnp.cos(windows[:, 0])
    trans_imag = damping * jnp.sin(windows[:, 0])
    wave_real = probe[0] * trans_real - probe[1] * trans_imag
    wave_imag = probe[0] * trans_imag + probe[1] * trans_real
    outgoing = jnp.stack([wave_real, wave_imag], axis=1).astype(jnp.bfloat16)
    half_wave = jnp.einsum(
        "yxab,sxbc->syac", forward_left, outgoing, preferred_element_type=jnp.float32
    ).astype(jnp.bfloat16)
    far_field = jnp.einsum(
        "sxab,xbd->sad", half_wave, forward_right, preferred_element_type=jnp.float32
    )
    far_real = far_field[:, :, :length]
    far_imag = far_field[:, :, length:]
    amplitude = amplitudes.reshape(count, length, length).astype(jnp.float32)
    modulus = jnp.sqrt(far_real * far_real + far_imag * far_imag)
    misfit = jnp.sum((modulus - amplitude) * (modulus - amplitude))
    ratio = 1.0 - amplitude / jnp.maximum(modulus, 0.5)
    residual = (far_field * jnp.concatenate([ratio, ratio], axis=2)).astype(jnp.bfloat16)
    back_half = jnp.einsum(
        "yxab,sbxc->syac",
        backward_left,
        residual.reshape(count, length, 2, length),
        preferred_element_type=jnp.float32,
    ).astype(jnp.bfloat16)
    near_field = jnp.einsum(
        "syab,ybd->sad", back_half, backward_right, preferred_element_type=jnp.float32
    )
    grad_real = near_field[:, :, :length]
    grad_imag = near_field[:, :, length:]
    object_real = wave_real * grad_real + wave_imag * grad_imag
    object_imag = wave_real * grad_imag - wave_imag * grad_real
    cells = jnp.stack([object_imag, -object_real], axis=1)
    probe_term = jnp.stack(
        [
            jnp.sum(trans_real * grad_real + trans_imag * grad_imag, axis=0),
            jnp.sum(trans_real * grad_imag - trans_imag * grad_real, axis=0),
        ]
    )

    def add_window(index, canvas_now):
        where = (zero_index, row_begin[index], col_begin[index])
        piece = lax.dynamic_slice(canvas_now, where, (2, length, length))
        return lax.dynamic_update_slice(canvas_now, piece + cells[index], where)

    canvas = jnp.zeros((2, rows_local + length, cols_local + length), jnp.float32)
    canvas = lax.fori_loop(0, count, add_window, canvas)
    summed = over_copies(canvas, "beam")
    probe_total, misfit_total = packed_total(
        (probe_term, misfit), ("beam", ("row", "col_0", "col_1"))
    )
    gradient = fold_rims(summed, half)
    square_sum = over_copies(jnp.sum(gradient * gradient), ROW_COL)
    plane_devices = lax.axis_size("row") * lax.axis_size(COL)
    mean_square = square_sum / (2 * rows_local * cols_local * plane_devices)
    factor = jnp.minimum(1.0, 0.5 / jnp.sqrt(mean_square + 1e-06))
    total = plane_devices * lax.axis_size("beam") * count
    return (gradient * factor, probe_total / total, misfit_total / (total * length * length))


def solution(mesh):
    split = Mesh(
        mesh.devices.reshape(mesh.shape["beam"], mesh.shape["row"], 8, 2),
        ("beam", "row", "col_0", "col_1"),
    )
    in_specs = (
        P("beam", "row", COL),
        P("beam", "row", COL),
        P(),
        P("row", COL, "beam", None, None),
        P("row", COL, "beam"),
        P("row", COL, "beam"),
    )
    out_specs = (P(None, "row", COL), P(), P())
    return jax.shard_map(local, mesh=split, in_specs=in_specs, out_specs=out_specs, check_vma=False)
```

profile of v0, /device:TPU:1, one launch (start us, length us, event | category | flops | bytes accessed | tf_op | source)
XLA Modules:
  0.0 407.6 jit_solution(17198867959797655671)
XLA Ops:
  3.4 1.5 broadcast_in_dim.26
  5.0 5.0 %all-to-all-start = ((f32[4,1,65536]{2,1,0:T(1,128)}), f32[4,1,65536]{2,1,0:T(1,128)S(1)}, u32[]{:S(2)}, u32[]{:S(2)}) async-start(f32[4,1,65536]{2,1,0:T(1,128)} %broadcast_in_dim.26), calls=%async_computation | async-start | bytes 2097152 | tf_op jit(solution)/shard_map/all_to_all | solution.py:21
  10.0 13.4 %all-to-all-done = f32[4,1,65536]{2,1,0:T(1,128)S(1)} async-done(((f32[4,1,65536]{2,1,0:T(1,128)}), f32[4,1,65536]{2,1,0:T(1,128)S(1)}, u32[]{:S(2)}, u32[]{:S(2)}) %all-to-all-start) | async-done | bytes 1048608 | tf_op jit(solution)/shard_map/all_to_all | solution.py:21
  24.5 3.9 collective-permute-start
  31.7 2.4 collective-permute-done.1
  34.1 6.7 %collective-permute-start.2 = (f32[2,512,128]{2,1,0:T(8,128)S(1)}, f32[2,512,128]{2,1,0:T(8,128)S(1)}, u32[]{:S(2)}, u32[]{:S(2)}) collective-permute-start(f32[2,512,128]{2,1,0:T(8,128)S(1)} %pad_maximum_fusion.2), channel_id=1, source_target_pairs={{0,1},{1,2},{2,3},{3,4},{4,5},{5,6},{6,7},{7,8},{8,9},{9,10},{10,1... | collective-permute-start | bytes 1572872 | tf_op jit(solution)/shard_map/ppermute | solution.py:45
  40.8 1.9 collective-permute-start.3
  48.3 3.1 collective-permute-done.3
  52.7 24.4 %while.15 = (s32[]{:T(128)}, f32[2,512,384]{2,1,0:T(8,128)S(1)}, s32[8,3]{0,1:T(4,128)S(1)}, f32[8,2,256,256]{2,3,1,0:T(8,128)}, s32[]{:T(128)}) while((s32[]{:T(128)}, f32[2,512,384]{2,1,0:T(8,128)S(1)}, s32[8,3]{0,1:T(4,128)S(1)}, f32[8,2,256,256]{2,3,1,0:T(8,128)}, s32[]{:T(128)}) %tuple.77), condition=%wide.while_cond, body=%wide.while_body.sunk | while | flops 2 | bytes 3146353 | solution.py:144
  53.3 1.4 dynamic-slice_bitcast_fusion.2
  56.3 1.4 dynamic-slice_bitcast_fusion.2
  65.5 1.4 dynamic-slice_bitcast_fusion.2
  68.5 1.4 dynamic-slice_bitcast_fusion.2
  71.6 1.4 dynamic-slice_bitcast_fusion.2
  74.6 1.4 dynamic-slice_bitcast_fusion.2
  77.1 9.9 %subtract_convert_fusion = (bf16[8,1,256,256]{2,3,1,0:T(8,128)(2,1)}, f32[8,1,256,256]{2,3,1,0:T(8,128)S(1)}, f32[8,1,256,256]{2,3,1,0:T(8,128)S(1)}) fusion(f32[256,256]{0,1:T(8,128)S(1)} %copy.90, f32[256,256]{0,1:T(8,128)S(1)} %copy.86, f32[8,2,256,256]{2,3,1,0:T(8,128)} %get-tuple-element.105), kind=kLoop, calls=%fused_computation.43 | loop fusion | flops 3670016 | bytes 9961472 | tf_op jit(solution)/shard_map/convert.1
  87.0 1.4 add_convert_fusion
  88.7 5.9 %convolution_bitcast_fusion.1 = f32[8,256,512]{2,1,0:T(8,128)} fusion(bf16[8,1,256,256]{2,3,1,0:T(8,128)(2,1)} %add_convert_fusion, bf16[8,1,256,256]{2,3,1,0:T(8,128)(2,1)} %get-tuple-element.166, bf16[1,2,256,256]{3,2,1,0:T(8,128)(2,1)S(1)} %copy-done.10, bf16[1,2,256,256]{3,2,1,0:T(8,128)(2,1)} %get-tuple-element.197, ...), kind=kOutput, calls=%fused_computation.13 | convolution fusion | flops 2154037248 | bytes 7340032 | tf_op jit(solution)/shard_map/sxab,xbd->sad/dot_general | solution.py:177
  94.6 4.5 %fusion.3 = (f32[]{:T(128)}, f32[8,256,256]{2,1,0:T(8,128)S(1)}) fusion(bf16[1,1,8,256,256]{4,3,2,1,0:T(8,128)(2,1)} %param.11, f32[8,256,512]{2,1,0:T(8,128)} %convolution_bitcast_fusion.1), kind=kLoop, calls=%fused_computation.16 | loop fusion | flops 5242879 | bytes 7340036 | tf_op jit(solution)/shard_map/reduce_sum | solution.py:184
  99.1 1.9 fusion
  101.0 4.0 copy.111
  105.0 5.9 %convolution_bitcast_fusion = f32[8,256,512]{1,2,0:T(8,128)} fusion(bf16[8,256,2,256,1]{1,3,2,4,0:T(8,128)(2,1)} %bitcast.175, bf16[1,2,256,256]{3,2,1,0:T(8,128)(2,1)} %get-tuple-element.198, bf16[1,2,256,256]{3,2,1,0:T(8,128)(2,1)S(1)} %copy-done.7, bf16[1,256,512]{2,1,0:T(8,128)(2,1)S(1)} %copy-done.6, bf16[1,256,512]{2,1,0:T(8,128)(2,1)S(1)} %copy-done.5), kind=kOutput, calls=%fused_computation.12 | convolution fusion | flops 2149842944 | bytes 7340032 | tf_op jit(solution)/shard_map/syab,ybd->sad/dot_general | solution.py:193
  111.0 5.1 %fusion.13 = (f32[256,256]{0,1:T(8,128)S(1)}, f32[256,256]{0,1:T(8,128)}, f32[8,1,256,256]{2,3,0,1:T(8,128)S(1)}, f32[8,1,256,256]{2,3,0,1:T(8,128)S(1)}) fusion(f32[8,1,256,256]{2,3,1,0:T(8,128)S(1)} %get-tuple-element.167, f32[8,1,256,256]{2,3,1,0:T(8,128)} %copy-done, f32[8,256,512]{1,2,0:T(8,128)} %convolution_bitcast_fusion, f32[256,256]{0,1:T(8,128)S(1)} %copy.90, ...), kind=kLoop, calls=%fused_computation.33 | loop fusion | flops 10878976 | bytes 13631488 | tf_op jit(solution)/shard_map/reduce_sum | solution.py:203
  116.0 2.2 pad_maximum_fusion
  118.4 115.5 %while.14 = (s32[]{:T(128)}, f32[2,512,384]{2,1,0:T(8,128)S(1)}, s32[8]{0:T(128)S(1)}, s32[8]{0:T(128)S(1)}, f32[8,2,256,256]{2,3,0,1:T(8,128)}, /*index=5*/s32[]{:T(128)}, s32[]{:T(128)}, s32[]{:T(128)}, s32[]{:T(128)}) while((s32[]{:T(128)}, f32[2,512,384]{2,1,0:T(8,128)S(1)}, s32[8]{0:T(128)S(1)}, s32[8]{0:T(128)S(1)}, ...), condition=%wide.region_4.5_spmd, body=%wide.region_3.4_spmd.sunk | while | flops 131080 | bytes 4718793 | solution.py:214
  124.5 8.9 %dynamic_update_slice.8 = f32[2,512,384]{2,1,0:T(8,128)S(1)} dynamic-update-slice(f32[2,512,384]{2,1,0:T(8,128)S(1)} %get-tuple-element.290, f32[2,256,256]{2,1,0:T(8,128)S(1)} %bitcast_add_fusion.2, s32[]{:T(128)} %constant.71.clone.1..sunk, s32[]{:T(128)S(6)} %select_n.125, s32[]{:T(128)S(6)} %select_n.126) | dynamic-update-slice | bytes 1048580 | tf_op jit(solution)/shard_map/while/body/eval_jaxpr/dynamic_update_slice | solution.py:211
  139.4 8.8 %dynamic_update_slice.8 = f32[2,512,384]{2,1,0:T(8,128)S(1)} dynamic-update-slice(f32[2,512,384]{2,1,0:T(8,128)S(1)} %get-tuple-element.290, f32[2,256,256]{2,1,0:T(8,128)S(1)} %bitcast_add_fusion.2, s32[]{:T(128)} %constant.71.clone.1..sunk, s32[]{:T(128)S(6)} %select_n.125, s32[]{:T(128)S(6)} %select_n.126) | dynamic-update-slice | bytes 1048580 | tf_op jit(solution)/shard_map/while/body/eval_jaxpr/dynamic_update_slice | solution.py:211
  154.2 8.7 %dynamic_update_slice.8 = f32[2,512,384]{2,1,0:T(8,128)S(1)} dynamic-update-slice(f32[2,512,384]{2,1,0:T(8,128)S(1)} %get-tuple-element.290, f32[2,256,256]{2,1,0:T(8,128)S(1)} %bitcast_add_fusion.2, s32[]{:T(128)} %constant.71.clone.1..sunk, s32[]{:T(128)S(6)} %select_n.125, s32[]{:T(128)S(6)} %select_n.126) | dynamic-update-slice | bytes 1048580 | tf_op jit(solution)/shard_map/while/body/eval_jaxpr/dynamic_update_slice | solution.py:211
  168.9 7.8 %dynamic_update_slice.8 = f32[2,512,384]{2,1,0:T(8,128)S(1)} dynamic-update-slice(f32[2,512,384]{2,1,0:T(8,128)S(1)} %get-tuple-element.290, f32[2,256,256]{2,1,0:T(8,128)S(1)} %bitcast_add_fusion.2, s32[]{:T(128)} %constant.71.clone.1..sunk, s32[]{:T(128)S(6)} %select_n.125, s32[]{:T(128)S(6)} %select_n.126) | dynamic-update-slice | bytes 1048580 | tf_op jit(solution)/shard_map/while/body/eval_jaxpr/dynamic_update_slice | solution.py:211
  182.6 8.9 %dynamic_update_slice.8 = f32[2,512,384]{2,1,0:T(8,128)S(1)} dynamic-update-slice(f32[2,512,384]{2,1,0:T(8,128)S(1)} %get-tuple-element.290, f32[2,256,256]{2,1,0:T(8,128)S(1)} %bitcast_add_fusion.2, s32[]{:T(128)} %constant.71.clone.1..sunk, s32[]{:T(128)S(6)} %select_n.125, s32[]{:T(128)S(6)} %select_n.126) | dynamic-update-slice | bytes 1048580 | tf_op jit(solution)/shard_map/while/body/eval_jaxpr/dynamic_update_slice | solution.py:211
  197.5 8.4 %dynamic_update_slice.8 = f32[2,512,384]{2,1,0:T(8,128)S(1)} dynamic-update-slice(f32[2,512,384]{2,1,0:T(8,128)S(1)} %get-tuple-element.290, f32[2,256,256]{2,1,0:T(8,128)S(1)} %bitcast_add_fusion.2, s32[]{:T(128)} %constant.71.clone.1..sunk, s32[]{:T(128)S(6)} %select_n.125, s32[]{:T(128)S(6)} %select_n.126) | dynamic-update-slice | bytes 1048580 | tf_op jit(solution)/shard_map/while/body/eval_jaxpr/dynamic_update_slice | solution.py:211
  211.8 8.9 %dynamic_update_slice.8 = f32[2,512,384]{2,1,0:T(8,128)S(1)} dynamic-update-slice(f32[2,512,384]{2,1,0:T(8,128)S(1)} %get-tuple-element.290, f32[2,256,256]{2,1,0:T(8,128)S(1)} %bitcast_add_fusion.2, s32[]{:T(128)} %constant.71.clone.1..sunk, s32[]{:T(128)S(6)} %select_n.125, s32[]{:T(128)S(6)} %select_n.126) | dynamic-update-slice | bytes 1048580 | tf_op jit(solution)/shard_map/while/body/eval_jaxpr/dynamic_update_slice | solution.py:211
  226.7 7.1 %dynamic_update_slice.8 = f32[2,512,384]{2,1,0:T(8,128)S(1)} dynamic-update-slice(f32[2,512,384]{2,1,0:T(8,128)S(1)} %get-tuple-element.290, f32[2,256,256]{2,1,0:T(8,128)S(1)} %bitcast_add_fusion.2, s32[]{:T(128)} %constant.71.clone.1..sunk, s32[]{:T(128)S(6)} %select_n.125, s32[]{:T(128)S(6)} %select_n.126) | dynamic-update-slice | bytes 1048580 | tf_op jit(solution)/shard_map/while/body/eval_jaxpr/dynamic_update_slice | solution.py:211
  233.8 3.1 broadcast_in_dim.27
  236.9 5.4 %all-to-all-start.1 = ((f32[4,2,512,384]{3,2,1,0:T(8,128)}), f32[4,2,512,384]{3,2,1,0:T(8,128)}, u32[]{:S(2)}, u32[]{:S(2)}) async-start(f32[4,2,512,384]{3,2,1,0:T(8,128)} %broadcast_in_dim.27), calls=%async_computation.1 | async-start | bytes 12582912 | tf_op jit(solution)/shard_map/all_to_all | solution.py:21
  245.6 59.3 %all-to-all-done.1 = f32[4,2,512,384]{3,2,1,0:T(8,128)} async-done(((f32[4,2,512,384]{3,2,1,0:T(8,128)}), f32[4,2,512,384]{3,2,1,0:T(8,128)}, u32[]{:S(2)}, u32[]{:S(2)}) %all-to-all-start.1) | async-done | bytes 6291488 | tf_op jit(solution)/shard_map/all_to_all | solution.py:21
  304.9 18.4 %all-to-all-start.3 = ((f32[64,4,513]{2,1,0:T(4,128)}), f32[64,4,513]{2,1,0:T(4,128)S(1)}, u32[]{:S(2)}, u32[]{:S(2)}) async-start(f32[64,4,513]{2,1,0:T(4,128)} %copy.101), calls=%async_computation.3 | async-start | bytes 1310720 | tf_op jit(solution)/shard_map/all_to_all | solution.py:80
  323.4 3.3 reduce_sum.102
  327.7 2.4 collective-permute-start.4
  330.1 3.2 collective-permute-start.5
  333.3 10.4 %all-to-all-done.3 = f32[64,4,513]{2,1,0:T(4,128)S(1)} async-done(((f32[64,4,513]{2,1,0:T(4,128)}), f32[64,4,513]{2,1,0:T(4,128)S(1)}, u32[]{:S(2)}, u32[]{:S(2)}) %all-to-all-start.3) | async-done | bytes 525344 | tf_op jit(solution)/shard_map/all_to_all | solution.py:80
  343.9 6.5 %all_to_all.45 = f32[4,1,513]{2,1,0:T(1,128)S(1)} all-to-all(f32[4,1,513]{2,1,0:T(1,128)S(1)} %all_to_all.33), channel_id=1, replica_groups=mesh['beam'=4,'row'=4,'col_0'=8,'col_1'=2] {'beam'}, dimensions={0} | all-to-all | bytes 16416 | tf_op jit(solution)/shard_map/all_to_all | solution.py:87
  350.4 6.5 %all_to_all.46 = f32[4,1,513]{2,1,0:T(1,128)S(1)} all-to-all(f32[4,1,513]{2,1,0:T(1,128)S(1)} %broadcast_in_dim.30), channel_id=1, replica_groups=mesh['beam'=4,'row'=4,'col_0'=8,'col_1'=2] {'beam'}, dimensions={0} | all-to-all | bytes 16416 | tf_op jit(solution)/shard_map/all_to_all | solution.py:21
  357.9 8.3 %all-to-all-start.6 = ((f32[64,4,513]{2,1,0:T(4,128)}), f32[64,4,513]{2,1,0:T(4,128)S(1)}, u32[]{:S(2)}, u32[]{:S(2)}) async-start(f32[64,4,513]{2,1,0:T(4,128)} %broadcast_in_dim.31), calls=%async_computation.6 | async-start | bytes 1310720 | tf_op jit(solution)/shard_map/all_to_all | solution.py:21
  368.7 4.0 collective-permute-start.7
  372.7 13.6 %all-to-all-done.6 = f32[64,4,513]{2,1,0:T(4,128)S(1)} async-done(((f32[64,4,513]{2,1,0:T(4,128)}), f32[64,4,513]{2,1,0:T(4,128)S(1)}, u32[]{:S(2)}, u32[]{:S(2)}) %all-to-all-start.6) | async-done | bytes 525344 | tf_op jit(solution)/shard_map/all_to_all | solution.py:21
  388.8 6.3 %all-to-all-start.2 = ((f32[64,1,1]{2,1,0:T(1,128)}), f32[64,1,1]{2,1,0:T(1,128)S(1)}, u32[]{:S(2)}, u32[]{:S(2)}) async-start(f32[64,1,1]{2,1,0:T(1,128)} %broadcast_in_dim.28), calls=%async_computation.2 | async-start | bytes 65536 | tf_op jit(solution)/shard_map/all_to_all | solution.py:21
  397.2 7.1 %all-to-all-done.2 = f32[64,1,1]{2,1,0:T(1,128)S(1)} async-done(((f32[64,1,1]{2,1,0:T(1,128)}), f32[64,1,1]{2,1,0:T(1,128)S(1)}, u32[]{:S(2)}, u32[]{:S(2)}) %all-to-all-start.2) | async-done | bytes 288 | tf_op jit(solution)/shard_map/all_to_all | solution.py:21
  (155 shorter events, 64.4 us)
Async XLA Ops:
  3.4 6.6 %copy-start.11 = (s32[1,1,8]{2,1,0:T(1,128)S(1)}, s32[1,1,8]{2,1,0:T(1,128)}, u32[]{:S(2)}) copy-start(s32[1,1,8]{2,1,0:T(1,128)} %param.12) | copy-start | bytes 100
  3.4 6.6 %copy-start.12 = (s32[1,1,8]{2,1,0:T(1,128)S(1)}, s32[1,1,8]{2,1,0:T(1,128)}, u32[]{:S(2)}) copy-start(s32[1,1,8]{2,1,0:T(1,128)} %param.13) | copy-start | bytes 100
  3.4 6.6 %copy-start.3 = (f32[2,256,256]{2,1,0:T(8,128)S(1)}, f32[2,256,256]{2,1,0:T(8,128)}, u32[]{:S(2)}) copy-start(f32[2,256,256]{2,1,0:T(8,128)} %param.10) | copy-start | bytes 1572868
  5.0 18.5 %all-to-all-start = ((f32[4,1,65536]{2,1,0:T(1,128)}), f32[4,1,65536]{2,1,0:T(1,128)S(1)}, u32[]{:S(2)}, u32[]{:S(2)}) async-start(f32[4,1,65536]{2,1,0:T(1,128)} %broadcast_in_dim.26), calls=%async_computation | async-start | bytes 2097152 | tf_op jit(solution)/shard_map/all_to_all | solution.py:21
  24.5 7.2 %collective-permute-start = (f32[2,128,128]{2,1,0:T(8,128)S(1)}, f32[2,128,128]{2,1,0:T(8,128)S(1)}, u32[]{:S(2)}, u32[]{:S(2)}) collective-permute-start(f32[2,128,128]{2,1,0:T(8,128)S(1)} %get-tuple-element.191), channel_id=1, source_target_pairs={{0,16},{16,32},{32,48},{1,17},{17,33},{33,49},{2,18},{18,34},{34,5... | collective-permute-start | bytes 393224 | tf_op jit(solution)/shard_map/ppermute | solution.py:45
  28.4 5.7 %collective-permute-start.1 = (f32[2,128,128]{2,1,0:T(8,128)S(1)}, f32[2,128,128]{2,1,0:T(8,128)S(1)}, u32[]{:S(2)}, u32[]{:S(2)}) collective-permute-start(f32[2,128,128]{2,1,0:T(8,128)S(1)} %get-tuple-element.192), channel_id=1, source_target_pairs={{16,0},{32,16},{48,32},{17,1},{33,17},{49,33},{18,2},{34,18},{50,3... | collective-permute-start | bytes 393224 | tf_op jit(solution)/shard_map/ppermute | solution.py:47
  34.1 13.4 %collective-permute-start.2 = (f32[2,512,128]{2,1,0:T(8,128)S(1)}, f32[2,512,128]{2,1,0:T(8,128)S(1)}, u32[]{:S(2)}, u32[]{:S(2)}) collective-permute-start(f32[2,512,128]{2,1,0:T(8,128)S(1)} %pad_maximum_fusion.2), channel_id=1, source_target_pairs={{0,1},{1,2},{2,3},{3,4},{4,5},{5,6},{6,7},{7,8},{8,9},{9,10},{10,1... | collective-permute-start | bytes 1572872 | tf_op jit(solution)/shard_map/ppermute | solution.py:45
  40.8 10.6 %collective-permute-start.3 = (f32[2,512,128]{2,1,0:T(8,128)S(1)}, f32[2,512,128]{2,1,0:T(8,128)}, u32[]{:S(2)}, u32[]{:S(2)}) collective-permute-start(f32[2,512,128]{2,1,0:T(8,128)S(1)} %pad_maximum_fusion.2), channel_id=1, source_target_pairs={{1,0},{2,1},{3,2},{4,3},{5,4},{6,5},{7,6},{8,7},{9,8},{10,9},{11,1... | collective-permute-start | bytes 1572872 | tf_op jit(solution)/shard_map/ppermute | solution.py:47
  47.5 0.8 copy-start.4
  87.0 1.7 copy-start
  87.0 1.7 copy-start.8
  87.0 1.7 copy-start.9
  87.0 1.7 copy-start.10
  94.6 4.5 %copy-start.1 = (f32[8,256,512]{2,1,0:T(8,128)S(1)}, f32[8,256,512]{2,1,0:T(8,128)}, u32[]{:S(2)}) copy-start(f32[8,256,512]{2,1,0:T(8,128)} %convolution_bitcast_fusion.1) | copy-start | bytes 12582916
  101.0 4.0 copy-start.5
  101.0 4.0 copy-start.6
  101.0 4.0 copy-start.7
  236.9 5.4 %copy-start.2 = (f32[256,256]{0,1:T(8,128)S(1)}, f32[256,256]{0,1:T(8,128)}, u32[]{:S(2)}) copy-start(f32[256,256]{0,1:T(8,128)} %get-tuple-element.147) | copy-start | bytes 786436
  236.9 68.0 %all-to-all-start.1 = ((f32[4,2,512,384]{3,2,1,0:T(8,128)}), f32[4,2,512,384]{3,2,1,0:T(8,128)}, u32[]{:S(2)}, u32[]{:S(2)}) async-start(f32[4,2,512,384]{3,2,1,0:T(8,128)} %broadcast_in_dim.27), calls=%async_computation.1 | async-start | bytes 12582912 | tf_op jit(solution)/shard_map/all_to_all | solution.py:21
  304.9 38.8 %all-to-all-start.3 = ((f32[64,4,513]{2,1,0:T(4,128)}), f32[64,4,513]{2,1,0:T(4,128)S(1)}, u32[]{:S(2)}, u32[]{:S(2)}) async-start(f32[64,4,513]{2,1,0:T(4,128)} %copy.101), calls=%async_computation.3 | async-start | bytes 1310720 | tf_op jit(solution)/shard_map/all_to_all | solution.py:80
  327.7 38.5 %collective-permute-start.4 = (f32[2,512,128]{2,1,0:T(8,128)}, f32[2,512,128]{2,1,0:T(8,128)S(1)}, u32[]{:S(2)}, u32[]{:S(2)}) collective-permute-start(f32[2,512,128]{2,1,0:T(8,128)} %get-tuple-element.177), channel_id=1, source_target_pairs={{1,0},{2,1},{3,2},{4,3},{5,4},{6,5},{7,6},{8,7},{9,8},{10,9},{11,1... | collective-permute-start | bytes 1572872 | tf_op jit(solution)/shard_map/ppermute | solution.py:16
  330.1 36.1 %collective-permute-start.5 = (f32[2,512,128]{2,1,0:T(8,128)}, f32[2,512,128]{2,1,0:T(8,128)}, u32[]{:S(2)}, u32[]{:S(2)}) collective-permute-start(f32[2,512,128]{2,1,0:T(8,128)} %get-tuple-element.178), channel_id=1, source_target_pairs={{0,1},{1,2},{2,3},{3,4},{4,5},{5,6},{6,7},{7,8},{8,9},{9,10},{10,1... | collective-permute-start | bytes 1572872 | tf_op jit(solution)/shard_map/ppermute | solution.py:16
  357.9 28.4 %all-to-all-start.6 = ((f32[64,4,513]{2,1,0:T(4,128)}), f32[64,4,513]{2,1,0:T(4,128)S(1)}, u32[]{:S(2)}, u32[]{:S(2)}) async-start(f32[64,4,513]{2,1,0:T(4,128)} %broadcast_in_dim.31), calls=%async_computation.6 | async-start | bytes 1310720 | tf_op jit(solution)/shard_map/all_to_all | solution.py:21
  367.4 19.5 %collective-permute-start.6 = (f32[2,128,128]{2,1,0:T(8,128)S(1)}, f32[2,128,128]{2,1,0:T(8,128)S(1)}, u32[]{:S(2)}, u32[]{:S(2)}) collective-permute-start(f32[2,128,128]{2,1,0:T(8,128)S(1)} %get-tuple-element.179), channel_id=1, source_target_pairs={{16,0},{32,16},{48,32},{17,1},{33,17},{49,33},{18,2},{34,18},{50,3... | collective-permute-start | bytes 393224 | tf_op jit(solution)/shard_map/ppermute | solution.py:16
  368.7 18.2 %collective-permute-start.7 = (f32[2,128,128]{2,1,0:T(8,128)S(1)}, f32[2,128,128]{2,1,0:T(8,128)S(1)}, u32[]{:S(2)}, u32[]{:S(2)}) collective-permute-start(f32[2,128,128]{2,1,0:T(8,128)S(1)} %get-tuple-element.180), channel_id=1, source_target_pairs={{0,16},{16,32},{32,48},{1,17},{17,33},{33,49},{2,18},{18,34},{34,5... | collective-permute-start | bytes 393224 | tf_op jit(solution)/shard_map/ppermute | solution.py:16
  388.8 15.5 %all-to-all-start.2 = ((f32[64,1,1]{2,1,0:T(1,128)}), f32[64,1,1]{2,1,0:T(1,128)S(1)}, u32[]{:S(2)}, u32[]{:S(2)}) async-start(f32[64,1,1]{2,1,0:T(1,128)} %broadcast_in_dim.28), calls=%async_computation.2 | async-start | bytes 65536 | tf_op jit(solution)/shard_map/all_to_all | solution.py:21
where the time goes:
time: 410 us; the launch traced here: 408 us
  local copies, waits for them, and re-layouts  130 us (32%)
  waiting for transfers between devices  109 us (27%)
  starting transfers between devices  68 us (17%)
  other arithmetic  45 us (11%)
  loops' own time  27 us (7%)
  blocking collectives  13 us (3%)
  matrix products  11.8 us (3%)
    all_to_all x4, waiting for transfers between devices, sent_to_all(): return lax.all_to_all(copies, axis, split_axis=0, concat_axis=0, tiled=True)  93.4 us
    dynamic_update_slice x8, local copies, waits for them, and re-layouts, add_window(): return lax.dynamic_update_slice(canvas_now, piece + cells[index], where)  67.6 us
    another operation x1, loops' own time, local(): canvas = lax.fori_loop(0, count, add_window, canvas)  26.9 us
    all_to_all x4, starting transfers between devices, sent_to_all(): return lax.all_to_all(copies, axis, split_axis=0, concat_axis=0, tiled=True)  25 us
    gather x40, local copies, waits for them, and re-layouts  24.3 us
    all_to_all x1, starting transfers between devices, summed_on_arrival(): parts = lax.all_to_all(cut_along(x, dim, length), axis, 0, 0, tiled=True)  18.4 us
    another operation x2, other arithmetic  11.4 us
    ppermute x4, starting transfers between devices, from_behind(): lax.ppermute(value, axis, [(source, source + steps) for source in range(f...  10.8 us
  transfers between devices with their start and end apart: 13, of which 7 were waited for; matrix products, arithmetic and copies ran while one was open for 5% of the time, Pallas kernels for 0%

commit v1 on v0

v1 whole, which is shorter than its diff:
```python
import math

import jax
import jax.numpy as jnp
import numpy as np
from jax import lax
from jax.experimental import pallas as pl
from jax.experimental.pallas import tpu as pltpu
from jax.sharding import Mesh
from jax.sharding import PartitionSpec as P

COL = ("col_0", "col_1")
ROW_COL = ("row", "col_0", "col_1")
LANES = 128
CHUNK = 128


def dft_tables(length):
    indices = np.arange(length, dtype=np.int32)
    product = indices[:, None] * indices[None, :] % length
    angles = product.astype(np.float32) * np.float32(2.0 * math.pi / length)
    factor = np.float32(1.0 / math.sqrt(length))
    return (
        jnp.asarray(np.cos(angles) * factor).astype(jnp.bfloat16),
        jnp.asarray(-np.sin(angles) * factor).astype(jnp.bfloat16),
    )


def window_kernel(
    rows_ref, cols_ref, t_ref, probe_ref, amp_ref, table_ref,
    canvas_ref, probe_sum_ref, misfit_ref,
    fwd, bwd, cut, psi, half, chi, back,
):
    step = pl.program_id(0)
    n = probe_ref.shape[1]

    @pl.when(step == 0)
    def _():
        real, imag = table_ref[0], table_ref[1]
        minus = -imag
        fwd[:n, :n] = real
        fwd[:n, n:] = minus
        fwd[n:, :n] = imag
        fwd[n:, n:] = real
        bwd[:n, :n] = real
        bwd[:n, n:] = imag
        bwd[n:, :n] = minus
        bwd[n:, n:] = real
        canvas_ref[...] = jnp.zeros_like(canvas_ref)
        probe_sum_ref[...] = jnp.zeros_like(probe_sum_ref)
        misfit_ref[...] = jnp.zeros_like(misfit_ref)

    row = rows_ref[step]
    col = cols_ref[step]
    turn = lax.rem(LANES - col, LANES)
    lane = lax.broadcasted_iota(jnp.int32, (32, LANES), 1)
    near = lane < LANES - col
    for at in range(0, n, 32):
        here = pl.ds(at, 32)
        pieces = []
        for part in range(2):
            turned = [
                pltpu.roll(t_ref[part, k, pl.ds(row + at, 32), :], turn, 1) for k in range(3)
            ]
            pieces.append([jnp.where(near, turned[k], turned[k + 1]) for k in range(2)])
        for k in range(2):
            lanes = pl.ds(k * LANES, LANES)
            tr, ti = pieces[0][k], pieces[1][k]
            cut[0, here, lanes] = tr
            cut[1, here, lanes] = ti
            pr = probe_ref[0, here, lanes]
            pi = probe_ref[1, here, lanes]
            psi[here, lanes] = (pr * tr - pi * ti).astype(jnp.bfloat16)
            psi[pl.ds(n + at, 32), lanes] = (pr * ti + pi * tr).astype(jnp.bfloat16)
    for part in range(2):
        half[:, part * n : (part + 1) * n] = jnp.dot(
            fwd[part * n : (part + 1) * n, :], psi[...], preferred_element_type=jnp.float32
        ).astype(jnp.bfloat16)
    total = jnp.zeros((8, LANES), jnp.float32)
    for at in range(0, n, CHUNK):
        here = pl.ds(at, CHUNK)
        far = jnp.dot(half[here, :], bwd[...], preferred_element_type=jnp.float32)
        fr, fi = far[:, :n], far[:, n:]
        amp = amp_ref[0, here, :].astype(jnp.float32)
        power = fr * fr + fi * fi
        inverse = lax.rsqrt(power)
        modulus = jnp.where(power > 0.0, power * inverse, 0.0)
        off = modulus - amp
        square = off * off
        total = total + jnp.sum(
            (square[:, :LANES] + square[:, LANES:]).reshape(CHUNK // 8, 8, LANES), axis=0
        )
        ratio = 1.0 - amp * jnp.minimum(inverse, 2.0)
        chi[here, :] = (fr * ratio).astype(jnp.bfloat16)
        chi[pl.ds(n + at, CHUNK), :] = (fi * ratio).astype(jnp.bfloat16)
    misfit_ref[...] += total
    for part in range(2):
        back[:, part * n : (part + 1) * n] = jnp.dot(
            bwd[part * n : (part + 1) * n, :], chi[...], preferred_element_type=jnp.float32
        ).astype(jnp.bfloat16)
    far_side = lax.broadcasted_iota(jnp.int32, (CHUNK, LANES), 1) >= col
    for at in range(0, n, CHUNK):
        here = pl.ds(at, CHUNK)
        grad = jnp.dot(back[here, :], fwd[...], preferred_element_type=jnp.float32)
        gr, gi = grad[:, :n], grad[:, n:]
        tr, ti = cut[0, here, :], cut[1, here, :]
        probe_sum_ref[0, here, :] += tr * gr + ti * gi
        probe_sum_ref[1, here, :] += tr * gi - ti * gr
        pr, pi = probe_ref[0, here, :], probe_ref[1, here, :]
        for part, value in enumerate((pr * gr + pi * gi, pr * gi - pi * gr)):
            first = pltpu.roll(value[:, :LANES], col, 1)
            second = pltpu.roll(value[:, LANES:], col, 1)
            there = pl.ds(row + at, CHUNK)
            canvas_ref[part, 0, there, :] += jnp.where(far_side, first, 0.0)
            canvas_ref[part, 1, there, :] += jnp.where(far_side, second, first)
            canvas_ref[part, 2, there, :] += jnp.where(far_side, 0.0, second)


def window_terms(t, probe, amplitudes, rows, cols):
    count, n, _ = amplitudes.shape
    grid_spec = pltpu.PrefetchScalarGridSpec(
        num_scalar_prefetch=2,
        grid=(count,),
        in_specs=[
            pl.BlockSpec(t.shape, lambda s, *_: (0, 0, 0, 0)),
            pl.BlockSpec(probe.shape, lambda s, *_: (0, 0, 0)),
            pl.BlockSpec((1, n, n), lambda s, *_: (s, 0, 0)),
            pl.BlockSpec((2, n, n), lambda s, *_: (0, 0, 0)),
        ],
        out_specs=[
            pl.BlockSpec(t.shape, lambda s, *_: (0, 0, 0, 0)),
            pl.BlockSpec(probe.shape, lambda s, *_: (0, 0, 0)),
            pl.BlockSpec((8, LANES), lambda s, *_: (0, 0)),
        ],
        scratch_shapes=[
            pltpu.VMEM((2 * n, 2 * n), jnp.bfloat16),
            pltpu.VMEM((2 * n, 2 * n), jnp.bfloat16),
            pltpu.VMEM((2, n, n), jnp.float32),
            pltpu.VMEM((2 * n, n), jnp.bfloat16),
            pltpu.VMEM((n, 2 * n), jnp.bfloat16),
            pltpu.VMEM((2 * n, n), jnp.bfloat16),
            pltpu.VMEM((n, 2 * n), jnp.bfloat16),
        ],
    )
    return pl.pallas_call(
        window_kernel,
        grid_spec=grid_spec,
        out_shape=[
            jax.ShapeDtypeStruct(t.shape, jnp.float32),
            jax.ShapeDtypeStruct(probe.shape, jnp.float32),
            jax.ShapeDtypeStruct((8, LANES), jnp.float32),
        ],
        compiler_params=pltpu.CompilerParams(dimension_semantics=("arbitrary",)),
        name="windows",
    )(rows, cols, t, probe, amplitudes, jnp.stack(dft_tables(n)))


def from_behind(value, axis, steps):
    count = lax.axis_size(axis)
    first, last = (max(0, -steps), min(count, count - steps))
    return lax.ppermute(value, axis, [(source, source + steps) for source in range(first, last)])


def sent_to_all(x, axis):
    copies = jnp.broadcast_to(x, (lax.axis_size(axis), *x.shape))
    return lax.all_to_all(copies, axis, split_axis=0, concat_axis=0, tiled=True)


def over_copies(x, axis):
    return sent_to_all(x, axis).sum(axis=0)


def extended(cells, sides, width):
    for axis, dim in sides:
        head = lax.slice_in_dim(cells, 0, width, axis=dim)
        tail = lax.slice_in_dim(cells, cells.shape[dim] - width, cells.shape[dim], axis=dim)
        cells = jnp.concatenate(
            [from_behind(tail, axis, 1), cells, from_behind(head, axis, -1)], axis=dim
        )
    return cells


def rows_for(lines, length):
    spare = -lines.shape[0] % length
    if not spare:
        return lines
    return jnp.concatenate([lines, jnp.zeros((spare, *lines.shape[1:]), lines.dtype)])


def joined_along(parts, dim):
    parts = jnp.moveaxis(parts, 0, dim)
    dims = parts.shape
    return parts.reshape(*dims[:dim], dims[dim] * dims[dim + 1], *dims[dim + 2 :])


def gather_axes(x, axes, dim):
    far, near = axes
    parts = sent_to_all(sent_to_all(x, far), near)
    return joined_along(parts.swapaxes(0, 1).reshape(-1, *x.shape), dim)


def cut_along(x, dim, length):
    before, after = (x.shape[:dim], x.shape[dim + 1 :])
    return jnp.moveaxis(x.reshape(*before, length, -1, *after), dim, 0)


def summed_on_arrival(x, axis, dim):
    length = lax.axis_size(axis)
    parts = lax.all_to_all(cut_along(x, dim, length), axis, 0, 0, tiled=True)
    return jnp.sum(parts, axis=0)


def summed_rows(x, axes, dim):
    far, near = axes
    own = summed_on_arrival(cut_along(x, dim, lax.axis_size(far)), near, dim + 1)
    return jnp.sum(lax.all_to_all(own, far, 0, 0, tiled=True), axis=0)


def sum_by_parts(x, axes):
    padded = rows_for(x, lax.axis_size(axes[0]) * lax.axis_size(axes[1]))
    whole = gather_axes(summed_rows(padded, axes, 0), axes, 0)
    return lax.slice_in_dim(whole, 0, len(x)).reshape(x.shape)


def packed_total(arrays, axis):
    ends = [0]
    for a in arrays:
        ends.append(ends[-1] + a.size)
    so_far = sum_by_parts(jnp.concatenate([a.ravel() for a in arrays]), axis)
    return tuple((so_far[b:e].reshape(a.shape) for a, b, e in zip(arrays, ends, ends[1:])))


def local(phase_volume, absorb_volume, probe, amplitudes, scan_rows, scan_cols):
    length = probe.shape[1]
    half = length // 2
    count = scan_rows.shape[2]
    rows_local = phase_volume.shape[1]
    cols_local = phase_volume.shape[2]
    part = jnp.stack(
        [
            jnp.sum(phase_volume, axis=0, dtype=jnp.float32),
            jnp.sum(absorb_volume, axis=0, dtype=jnp.float32),
        ]
    )
    summed = over_copies(part, "beam")
    tall = extended(summed, (("row", 1),), half)
    wide = jnp.stack([from_behind(tall, COL, 1), tall, from_behind(tall, COL, -1)], axis=1)
    damping = jnp.exp(-wide[1])
    t = jnp.stack([damping * jnp.cos(wide[0]), damping * jnp.sin(wide[0])])
    canvas, probe_term, misfit = window_terms(
        t,
        probe,
        amplitudes.reshape(count, length, length),
        scan_rows.reshape(count),
        scan_cols.reshape(count),
    )
    middle = canvas[:, 1] + from_behind(canvas[:, 0], COL, -1) + from_behind(canvas[:, 2], COL, 1)
    center = middle[:, half : half + rows_local]
    below = from_behind(middle[:, :half], "row", -1)
    above = from_behind(middle[:, half + rows_local :], "row", 1)
    center = center + jnp.pad(below, ((0, 0), (rows_local - half, 0), (0, 0)))
    center = center + jnp.pad(above, ((0, 0), (0, rows_local - half), (0, 0)))
    center = over_copies(center, "beam")
    tr = t[0, 1, half : half + rows_local]
    ti = t[1, 1, half : half + rows_local]
    gradient = jnp.stack(
        [tr * center[1] - ti * center[0], -(tr * center[0] + ti * center[1])]
    )
    probe_total, misfit_total = packed_total(
        (probe_term, jnp.sum(misfit)), ("beam", ("row", "col_0", "col_1"))
    )
    square_sum = over_copies(jnp.sum(gradient * gradient), ROW_COL)
    plane_devices = lax.axis_size("row") * lax.axis_size(COL)
    mean_square = square_sum / (2 * rows_local * cols_local * plane_devices)
    factor = jnp.minimum(1.0, 0.5 / jnp.sqrt(mean_square + 1e-06))
    total = plane_devices * lax.axis_size("beam") * count
    return (gradient * factor, probe_total / total, misfit_total / (total * length * length))


def solution(mesh):
    split = Mesh(
        mesh.devices.reshape(mesh.shape["beam"], mesh.shape["row"], 8, 2),
        ("beam", "row", "col_0", "col_1"),
    )
    in_specs = (
        P("beam", "row", COL),
        P("beam", "row", COL),
        P(),
        P("row", COL, "beam", None, None),
        P("row", COL, "beam"),
        P("row", COL, "beam"),
    )
    out_specs = (P(None, "row", COL), P(), P())
    return jax.shard_map(local, mesh=split, in_specs=in_specs, out_specs=out_specs, check_vma=False)
```

time: 410 us -> 195 us (0.48)
  local copies, waits for them, and re-layouts: 130 us -> 12.7 us
  waiting for transfers between devices: 109 us -> 72.3 us
  other arithmetic: 45 us -> 10.5 us
  loops' own time: 27 us -> 0 us
  Pallas kernels: 0 us -> 16.1 us
  matrix products: 11.8 us -> 0 us
  starting transfers between devices: 68 us -> 59.8 us
  blocking collectives: 13 us -> 19 us
    dynamic_update_slice x8 -> x0, local copies, waits for them, and re-layouts: 67.6 us -> none  [add_window(): return lax.dynamic_update_slice(canvas_now, piece + cells[index], where)]
    all_to_all x4, waiting for transfers between devices: 93.4 us -> 44.4 us  [sent_to_all(): return lax.all_to_all(copies, axis, split_axis=0, concat_axis=0, tiled=True)]
    another operation x2 -> x0, loops' own time: 27 us -> none  [the longest x1 26.9 us: local(): canvas = lax.fori_loop(0, count, add_window, canvas)]
    gather x40 -> x0, local copies, waits for them, and re-layouts: 24.3 us -> none
    dynamic_slice x32 -> x0, local copies, waits for them, and re-layouts: 19.2 us -> none  [the longest x16 10.3 us: add_window(): return lax.dynamic_update_slice(canvas_now, piece + cells[index], where)]
    pallas_call x0 -> x1, Pallas kernels: none -> 16.1 us  [window_terms(): pl.pallas_call(window_kernel, grid_spec=grid_spec, out_shape=[jax.ShapeDt...]
    another operation x7 -> x4, other arithmetic: 15.7 us -> 1.46 us  [the longest x1 1.27 us: local(): t = jnp.stack([damping * jnp.cos(wide[0]), damping * jnp.sin(wide[0])])]
    ppermute x4 -> x8, starting transfers between devices: 10.8 us -> 24.6 us  [from_behind(): lax.ppermute(value, axis, [(source, source + steps) for source in range(f...]
  transfers between devices with their start and end apart: 13 -> 14, of which waited for: 7 -> 10; matrix products, arithmetic and copies ran while one was open for 5% -> 4% of each run, Pallas kernels for 0% -> 0%
where the time goes in v1:
time: 195 us; the launch traced here: 194 us
  waiting for transfers between devices  72.3 us (37%)
  starting transfers between devices  59.8 us (31%)
  blocking collectives  19 us (10%)
  Pallas kernels  16.1 us (8%)
  local copies, waits for them, and re-layouts  12.7 us (7%)
  other arithmetic  10.5 us (5%)
  between operations  3.4 us (2%)
    all_to_all x4, waiting for transfers between devices, sent_to_all(): return lax.all_to_all(copies, axis, split_axis=0, concat_axis=0, tiled=True)  44.4 us
    ppermute x8, starting transfers between devices, from_behind(): lax.ppermute(value, axis, [(source, source + steps) for source in range(f...  24.6 us
    all_to_all x4, starting transfers between devices, sent_to_all(): return lax.all_to_all(copies, axis, split_axis=0, concat_axis=0, tiled=True)  20.5 us
    all_to_all x1, blocking collectives, sent_to_all(): return lax.all_to_all(copies, axis, split_axis=0, concat_axis=0, tiled=True)  19 us
    pallas_call x1, Pallas kernels, window_terms(): pl.pallas_call(window_kernel, grid_spec=grid_spec, out_shape=[jax.ShapeDt...  16.1 us
    all_to_all x1, waiting for transfers between devices, summed_on_arrival(): parts = lax.all_to_all(cut_along(x, dim, length), axis, 0, 0, tiled=True)  13.3 us
    all_to_all x1, starting transfers between devices, summed_on_arrival(): parts = lax.all_to_all(cut_along(x, dim, length), axis, 0, 0, tiled=True)  11.4 us
    ppermute x8, waiting for transfers between devices, from_behind(): lax.ppermute(value, axis, [(source, source + steps) for source in range(f...  10.5 us
  transfers between devices with their start and end apart: 14, of which 10 were waited for; matrix products, arithmetic and copies ran while one was open for 4% of the time, Pallas kernels for 0%

profile of v1, /device:TPU:1, one launch (start us, length us, event | category | flops | bytes accessed | tf_op | source)
XLA Modules:
  0.0 193.7 jit_solution(12569332223150509541)
XLA Ops:
  0.6 1.5 convert_reduce_fusion.1
  2.4 19.0 %all_to_all.44 = f32[4,2,256,128]{3,2,1,0:T(8,128)S(1)} all-to-all(f32[4,2,256,128]{3,2,1,0:T(8,128)S(1)} %broadcast_in_dim.18), channel_id=1, replica_groups=mesh['beam'=4,'row'=4,'col_0'=8,'col_1'=2] {'beam'}, dimensions={0} | all-to-all | bytes 2097152 | tf_op jit(solution)/shard_map/all_to_all | solution.py:166
  21.6 3.1 %collective-permute-start = (f32[2,128,128]{2,1,0:T(8,128)S(1)}, f32[2,128,128]{2,1,0:T(8,128)S(1)}, u32[]{:S(2)}, u32[]{:S(2)}) collective-permute-start(f32[2,128,128]{2,1,0:T(8,128)S(1)} %get-tuple-element.17), channel_id=1, source_target_pairs={{0,16},{16,32},{32,48},{1,17},{17,33},{33,49},{2,18},{18,34},{34,5... | collective-permute-start | bytes 393224 | tf_op jit(solution)/shard_map/ppermute | solution.py:161
  24.7 1.3 collective-permute-start.1
  26.0 0.6 collective-permute-done
  26.6 3.8 %collective-permute-done.1 = f32[2,128,128]{2,1,0:T(8,128)S(1)} collective-permute-done((f32[2,128,128]{2,1,0:T(8,128)S(1)}, f32[2,128,128]{2,1,0:T(8,128)S(1)}, u32[]{:S(2)}, u32[]{:S(2)}) %collective-permute-start.1) | collective-permute-done | bytes 131104 | tf_op jit(solution)/shard_map/ppermute | solution.py:161
  30.5 5.1 %collective-permute-start.3 = (f32[2,512,128]{2,1,0:T(8,128)S(1)}, f32[2,512,128]{2,1,0:T(8,128)S(1)}, u32[]{:S(2)}, u32[]{:S(2)}) collective-permute-start(f32[2,512,128]{2,1,0:T(8,128)S(1)} %get-tuple-element.16), channel_id=1, source_target_pairs={{1,0},{2,1},{3,2},{4,3},{5,4},{6,5},{7,6},{8,7},{9,8},{10,9},{11,1... | collective-permute-start | bytes 1572872 | tf_op jit(solution)/shard_map/ppermute | solution.py:161
  35.6 3.4 %collective-permute-start.2 = (f32[2,512,128]{2,1,0:T(8,128)S(1)}, f32[2,512,128]{2,1,0:T(8,128)S(1)}, u32[]{:S(2)}, u32[]{:S(2)}) collective-permute-start(f32[2,512,128]{2,1,0:T(8,128)S(1)} %get-tuple-element.16), channel_id=1, source_target_pairs={{0,1},{1,2},{2,3},{3,4},{4,5},{5,6},{6,7},{7,8},{8,9},{9,10},{10,1... | collective-permute-start | bytes 1572872 | tf_op jit(solution)/shard_map/ppermute | solution.py:161
  39.1 4.9 %collective-permute-done.3 = f32[2,512,128]{2,1,0:T(8,128)S(1)} collective-permute-done((f32[2,512,128]{2,1,0:T(8,128)S(1)}, f32[2,512,128]{2,1,0:T(8,128)S(1)}, u32[]{:S(2)}, u32[]{:S(2)}) %collective-permute-start.3) | collective-permute-done | bytes 524320 | tf_op jit(solution)/shard_map/ppermute | solution.py:161
  44.0 1.2 collective-permute-done.2
  45.3 2.9 %sine_multiply_fusion = (f32[1,3,512,128]{3,2,1,0:T(8,128)S(1)}, f32[1,3,512,128]{3,2,1,0:T(8,128)S(1)}) fusion(f32[2,3,512,128]{3,2,1,0:T(8,128)S(1)} %pad_maximum_fusion), kind=kLoop, calls=%fused_computation.6 | loop fusion | flops 589824 | bytes 3145728 | tf_op jit(solution)/shard_map/mul | solution.py:249
  48.2 1.3 pad_maximum_fusion.1.t_ref
  49.5 16.1 %windows.1 = (f32[2,3,512,128]{3,2,1,0:T(8,128)}, f32[2,256,256]{2,1,0:T(8,128)}, f32[8,128]{1,0:T(8,128)}) custom-call(s32[8]{0:T(128)} %bitcast.54, s32[8]{0:T(128)} %bitcast.55, f32[2,3,512,128]{3,2,1,0:T(8,128)} %pad_maximum_fusion.1.t_ref, f32[2,256,256]{2,1,0:T(8,128)} %probe_ref.1, bf16[8,256,256]{2,1,0:T(8,128)(2,1)} %bitcast.47, ...), custom_call_target="tpu_custom_call" | custom-call | tf_op jit(solution)/shard_map/windows/pallas_call | solution.py:145
  65.6 1.1 slice_bitcast_fusion.2
  66.7 1.9 slice_bitcast_fusion
  68.6 1.9 collective-permute-start.4
  70.5 4.4 %collective-permute-start.5 = (f32[2,512,128]{2,1,0:T(8,128)S(1)}, f32[2,512,128]{2,1,0:T(8,128)}, u32[]{:S(2)}, u32[]{:S(2)}) collective-permute-start(f32[2,512,128]{2,1,0:T(8,128)S(1)} %slice_bitcast_fusion.2), channel_id=1, source_target_pairs={{0,1},{1,2},{2,3},{3,4},{4,5},{5,6},{6,7},{7,8},{8,9},{9,10},{10,1... | collective-permute-start | bytes 1572872 | tf_op jit(solution)/shard_map/ppermute | solution.py:161
  75.0 0.6 reduce_sum.87
  75.6 0.3 copy.45
  75.9 1.0 concatenate.7
  76.8 0.5 reshape_reshape.6
  77.3 1.3 copy.41
  78.6 11.4 %all-to-all-start.3 = ((f32[64,4,513]{2,1,0:T(4,128)}), f32[64,4,513]{2,1,0:T(4,128)S(1)}, u32[]{:S(2)}, u32[]{:S(2)}) async-start(f32[64,4,513]{2,1,0:T(4,128)} %copy.41), calls=%async_computation.3 | async-start | bytes 1310720 | tf_op jit(solution)/shard_map/all_to_all | solution.py:209
  90.0 1.4 fusion.2
  91.5 1.3 collective-permute-start.6
  92.8 4.0 %collective-permute-start.7 = (f32[2,128,128]{2,1,0:T(8,128)S(1)}, f32[2,128,128]{2,1,0:T(8,128)S(1)}, u32[]{:S(2)}, u32[]{:S(2)}) collective-permute-start(f32[2,128,128]{2,1,0:T(8,128)S(1)} %get-tuple-element.14), channel_id=1, source_target_pairs={{0,16},{16,32},{32,48},{1,17},{17,33},{33,49},{2,18},{18,34},{34,5... | collective-permute-start | bytes 393224 | tf_op jit(solution)/shard_map/ppermute | solution.py:161
  96.8 13.3 %all-to-all-done.3 = f32[64,4,513]{2,1,0:T(4,128)S(1)} async-done(((f32[64,4,513]{2,1,0:T(4,128)}), f32[64,4,513]{2,1,0:T(4,128)S(1)}, u32[]{:S(2)}, u32[]{:S(2)}) %all-to-all-start.3) | async-done | bytes 525344 | tf_op jit(solution)/shard_map/all_to_all | solution.py:209
  110.2 0.6 all_to_all.32
  110.8 3.3 %all-to-all-start.4 = ((f32[4,1,513]{2,1,0:T(1,128)}), f32[4,1,513]{2,1,0:T(1,128)S(1)}, u32[]{:S(2)}, u32[]{:S(2)}) async-start(f32[4,1,513]{2,1,0:T(1,128)} %all_to_all.32), calls=%async_computation.4 | async-start | bytes 20480 | tf_op jit(solution)/shard_map/all_to_all | solution.py:216
  114.2 4.1 %all-to-all-done.4 = f32[4,1,513]{2,1,0:T(1,128)S(1)} async-done(((f32[4,1,513]{2,1,0:T(1,128)}), f32[4,1,513]{2,1,0:T(1,128)S(1)}, u32[]{:S(2)}, u32[]{:S(2)}) %all-to-all-start.4) | async-done | bytes 8240 | tf_op jit(solution)/shard_map/all_to_all | solution.py:216
  118.2 1.0 broadcast_in_dim.19
  119.3 3.5 %all-to-all-start.1 = ((f32[4,2,256,128]{3,2,1,0:T(8,128)}), f32[4,2,256,128]{3,2,1,0:T(8,128)S(1)}, u32[]{:S(2)}, u32[]{:S(2)}) async-start(f32[4,2,256,128]{3,2,1,0:T(8,128)} %broadcast_in_dim.19), calls=%async_computation.1 | async-start | bytes 2097152 | tf_op jit(solution)/shard_map/all_to_all | solution.py:166
  122.8 13.7 %all-to-all-done.1 = f32[4,2,256,128]{3,2,1,0:T(8,128)S(1)} async-done(((f32[4,2,256,128]{3,2,1,0:T(8,128)}), f32[4,2,256,128]{3,2,1,0:T(8,128)S(1)}, u32[]{:S(2)}, u32[]{:S(2)}) %all-to-all-start.1) | async-done | bytes 1048608 | tf_op jit(solution)/shard_map/all_to_all | solution.py:166
  136.6 0.6 broadcast_in_dim.22
  137.2 3.3 %all-to-all-start.5 = ((f32[4,1,513]{2,1,0:T(1,128)}), f32[4,1,513]{2,1,0:T(1,128)S(1)}, u32[]{:S(2)}, u32[]{:S(2)}) async-start(f32[4,1,513]{2,1,0:T(1,128)} %broadcast_in_dim.22), calls=%async_computation.5 | async-start | bytes 20480 | tf_op jit(solution)/shard_map/all_to_all | solution.py:166
  140.6 0.7 multiply_reduce_fusion
  141.2 3.4 %all-to-all-done.5 = f32[4,1,513]{2,1,0:T(1,128)S(1)} async-done(((f32[4,1,513]{2,1,0:T(1,128)}), f32[4,1,513]{2,1,0:T(1,128)S(1)}, u32[]{:S(2)}, u32[]{:S(2)}) %all-to-all-start.5) | async-done | bytes 8240 | tf_op jit(solution)/shard_map/all_to_all | solution.py:166
  144.6 1.3 broadcast_in_dim.20
  145.9 9.0 %all-to-all-start.2 = ((f32[64,1,1]{2,1,0:T(1,128)}), f32[64,1,1]{2,1,0:T(1,128)S(1)}, u32[]{:S(2)}, u32[]{:S(2)}) async-start(f32[64,1,1]{2,1,0:T(1,128)} %broadcast_in_dim.20), calls=%async_computation.2 | async-start | bytes 65536 | tf_op jit(solution)/shard_map/all_to_all | solution.py:166
  154.9 9.2 %all-to-all-done.2 = f32[64,1,1]{2,1,0:T(1,128)S(1)} async-done(((f32[64,1,1]{2,1,0:T(1,128)}), f32[64,1,1]{2,1,0:T(1,128)S(1)}, u32[]{:S(2)}, u32[]{:S(2)}) %all-to-all-start.2) | async-done | bytes 288 | tf_op jit(solution)/shard_map/all_to_all | solution.py:166
  164.1 0.9 broadcast_in_dim.23
  165.1 4.7 %all-to-all-start.6 = ((f32[64,4,513]{2,1,0:T(4,128)}), f32[64,4,513]{2,1,0:T(4,128)S(1)}, u32[]{:S(2)}, u32[]{:S(2)}) async-start(f32[64,4,513]{2,1,0:T(4,128)} %broadcast_in_dim.23), calls=%async_computation.6 | async-start | bytes 1310720 | tf_op jit(solution)/shard_map/all_to_all | solution.py:166
  169.8 0.7 reduce_sum.86
  171.2 0.7 fusion.4
  171.9 18.0 %all-to-all-done.6 = f32[64,4,513]{2,1,0:T(4,128)S(1)} async-done(((f32[64,4,513]{2,1,0:T(4,128)}), f32[64,4,513]{2,1,0:T(4,128)S(1)}, u32[]{:S(2)}, u32[]{:S(2)}) %all-to-all-start.6) | async-done | bytes 525344 | tf_op jit(solution)/shard_map/all_to_all | solution.py:166
  190.0 0.5 reshape_reshape.7
  190.5 0.5 slice.84
  191.0 0.9 div.23
  (27 shorter events, 1.0 us)
Async XLA Ops:
  0.6 1.5 copy-start
  21.6 5.1 %collective-permute-start = (f32[2,128,128]{2,1,0:T(8,128)S(1)}, f32[2,128,128]{2,1,0:T(8,128)S(1)}, u32[]{:S(2)}, u32[]{:S(2)}) collective-permute-start(f32[2,128,128]{2,1,0:T(8,128)S(1)} %get-tuple-element.17), channel_id=1, source_target_pairs={{0,16},{16,32},{32,48},{1,17},{17,33},{33,49},{2,18},{18,34},{34,5... | collective-permute-start | bytes 393224 | tf_op jit(solution)/shard_map/ppermute | solution.py:161
  24.7 5.7 %collective-permute-start.1 = (f32[2,128,128]{2,1,0:T(8,128)S(1)}, f32[2,128,128]{2,1,0:T(8,128)S(1)}, u32[]{:S(2)}, u32[]{:S(2)}) collective-permute-start(f32[2,128,128]{2,1,0:T(8,128)S(1)} %get-tuple-element.18), channel_id=1, source_target_pairs={{16,0},{32,16},{48,32},{17,1},{33,17},{49,33},{18,2},{34,18},{50,3... | collective-permute-start | bytes 393224 | tf_op jit(solution)/shard_map/ppermute | solution.py:161
  30.5 13.5 %collective-permute-start.3 = (f32[2,512,128]{2,1,0:T(8,128)S(1)}, f32[2,512,128]{2,1,0:T(8,128)S(1)}, u32[]{:S(2)}, u32[]{:S(2)}) collective-permute-start(f32[2,512,128]{2,1,0:T(8,128)S(1)} %get-tuple-element.16), channel_id=1, source_target_pairs={{1,0},{2,1},{3,2},{4,3},{5,4},{6,5},{7,6},{8,7},{9,8},{10,9},{11,1... | collective-permute-start | bytes 1572872 | tf_op jit(solution)/shard_map/ppermute | solution.py:161
  35.6 9.6 %collective-permute-start.2 = (f32[2,512,128]{2,1,0:T(8,128)S(1)}, f32[2,512,128]{2,1,0:T(8,128)S(1)}, u32[]{:S(2)}, u32[]{:S(2)}) collective-permute-start(f32[2,512,128]{2,1,0:T(8,128)S(1)} %get-tuple-element.16), channel_id=1, source_target_pairs={{0,1},{1,2},{2,3},{3,4},{4,5},{5,6},{6,7},{7,8},{8,9},{9,10},{10,1... | collective-permute-start | bytes 1572872 | tf_op jit(solution)/shard_map/ppermute | solution.py:161
  65.6 9.4 %copy-start.2 = (f32[8,128]{1,0:T(8,128)S(1)}, f32[8,128]{1,0:T(8,128)}, u32[]{:S(2)}) copy-start(f32[8,128]{1,0:T(8,128)} %get-tuple-element.8) | copy-start | bytes 12292
  65.6 10.0 %copy-start.1 = (f32[2,256,256]{2,1,0:T(8,128)S(1)}, f32[2,256,256]{2,1,0:T(8,128)}, u32[]{:S(2)}) copy-start(f32[2,256,256]{2,1,0:T(8,128)} %get-tuple-element.7) | copy-start | bytes 1572868
  68.6 21.4 %collective-permute-start.4 = (f32[2,512,128]{2,1,0:T(8,128)}, f32[2,512,128]{2,1,0:T(8,128)}, u32[]{:S(2)}, u32[]{:S(2)}) collective-permute-start(f32[2,512,128]{2,1,0:T(8,128)} %slice_bitcast_fusion), channel_id=1, source_target_pairs={{1,0},{2,1},{3,2},{4,3},{5,4},{6,5},{7,6},{8,7},{9,8},{10,9},{11,1... | collective-permute-start | bytes 1572872 | tf_op jit(solution)/shard_map/ppermute | solution.py:161
  70.5 19.5 %collective-permute-start.5 = (f32[2,512,128]{2,1,0:T(8,128)S(1)}, f32[2,512,128]{2,1,0:T(8,128)}, u32[]{:S(2)}, u32[]{:S(2)}) collective-permute-start(f32[2,512,128]{2,1,0:T(8,128)S(1)} %slice_bitcast_fusion.2), channel_id=1, source_target_pairs={{0,1},{1,2},{2,3},{3,4},{4,5},{5,6},{6,7},{7,8},{8,9},{9,10},{10,1... | collective-permute-start | bytes 1572872 | tf_op jit(solution)/shard_map/ppermute | solution.py:161
  78.6 31.5 %all-to-all-start.3 = ((f32[64,4,513]{2,1,0:T(4,128)}), f32[64,4,513]{2,1,0:T(4,128)S(1)}, u32[]{:S(2)}, u32[]{:S(2)}) async-start(f32[64,4,513]{2,1,0:T(4,128)} %copy.41), calls=%async_computation.3 | async-start | bytes 1310720 | tf_op jit(solution)/shard_map/all_to_all | solution.py:209
  91.5 22.6 %collective-permute-start.6 = (f32[2,128,128]{2,1,0:T(8,128)S(1)}, f32[2,128,128]{2,1,0:T(8,128)S(1)}, u32[]{:S(2)}, u32[]{:S(2)}) collective-permute-start(f32[2,128,128]{2,1,0:T(8,128)S(1)} %get-tuple-element.13), channel_id=1, source_target_pairs={{16,0},{32,16},{48,32},{17,1},{33,17},{49,33},{18,2},{34,18},{50,3... | collective-permute-start | bytes 393224 | tf_op jit(solution)/shard_map/ppermute | solution.py:161
  92.8 21.3 %collective-permute-start.7 = (f32[2,128,128]{2,1,0:T(8,128)S(1)}, f32[2,128,128]{2,1,0:T(8,128)S(1)}, u32[]{:S(2)}, u32[]{:S(2)}) collective-permute-start(f32[2,128,128]{2,1,0:T(8,128)S(1)} %get-tuple-element.14), channel_id=1, source_target_pairs={{0,16},{16,32},{32,48},{1,17},{17,33},{33,49},{2,18},{18,34},{34,5... | collective-permute-start | bytes 393224 | tf_op jit(solution)/shard_map/ppermute | solution.py:161
  110.8 7.4 %all-to-all-start.4 = ((f32[4,1,513]{2,1,0:T(1,128)}), f32[4,1,513]{2,1,0:T(1,128)S(1)}, u32[]{:S(2)}, u32[]{:S(2)}) async-start(f32[4,1,513]{2,1,0:T(1,128)} %all_to_all.32), calls=%async_computation.4 | async-start | bytes 20480 | tf_op jit(solution)/shard_map/all_to_all | solution.py:216
  119.3 17.3 %all-to-all-start.1 = ((f32[4,2,256,128]{3,2,1,0:T(8,128)}), f32[4,2,256,128]{3,2,1,0:T(8,128)S(1)}, u32[]{:S(2)}, u32[]{:S(2)}) async-start(f32[4,2,256,128]{3,2,1,0:T(8,128)} %broadcast_in_dim.19), calls=%async_computation.1 | async-start | bytes 2097152 | tf_op jit(solution)/shard_map/all_to_all | solution.py:166
  137.2 7.4 %all-to-all-start.5 = ((f32[4,1,513]{2,1,0:T(1,128)}), f32[4,1,513]{2,1,0:T(1,128)S(1)}, u32[]{:S(2)}, u32[]{:S(2)}) async-start(f32[4,1,513]{2,1,0:T(1,128)} %broadcast_in_dim.22), calls=%async_computation.5 | async-start | bytes 20480 | tf_op jit(solution)/shard_map/all_to_all | solution.py:166
  145.9 18.3 %all-to-all-start.2 = ((f32[64,1,1]{2,1,0:T(1,128)}), f32[64,1,1]{2,1,0:T(1,128)S(1)}, u32[]{:S(2)}, u32[]{:S(2)}) async-start(f32[64,1,1]{2,1,0:T(1,128)} %broadcast_in_dim.20), calls=%async_computation.2 | async-start | bytes 65536 | tf_op jit(solution)/shard_map/all_to_all | solution.py:166
  165.1 24.9 %all-to-all-start.6 = ((f32[64,4,513]{2,1,0:T(4,128)}), f32[64,4,513]{2,1,0:T(4,128)S(1)}, u32[]{:S(2)}, u32[]{:S(2)}) async-start(f32[64,4,513]{2,1,0:T(4,128)} %broadcast_in_dim.23), calls=%async_computation.6 | async-start | bytes 1310720 | tf_op jit(solution)/shard_map/all_to_all | solution.py:166

commit v2 on v1

--- a/solution.py
+++ b/solution.py
@@ -1,3 +1,4 @@
+import functools
 import math
 
 import jax
@@ -10,7 +11,7 @@
 from jax.sharding import PartitionSpec as P
 
 COL = ("col_0", "col_1")
-ROW_COL = ("row", "col_0", "col_1")
+MESH = pl.DeviceIdType.MESH
 LANES = 128
 CHUNK = 128
 
@@ -155,98 +156,498 @@
     )(rows, cols, t, probe, amplitudes, jnp.stack(dft_tables(n)))
 
 
-def from_behind(value, axis, steps):
-    count = lax.axis_size(axis)
-    first, last = (max(0, -steps), min(count, count - steps))
-    return lax.ppermute(value, axis, [(source, source + steps) for source in range(first, last)])
-
-
-def sent_to_all(x, axis):
-    copies = jnp.broadcast_to(x, (lax.axis_size(axis), *x.shape))
-    return lax.all_to_all(copies, axis, split_axis=0, concat_axis=0, tiled=True)
-
-
-def over_copies(x, axis):
-    return sent_to_all(x, axis).sum(axis=0)
-
-
-def extended(cells, sides, width):
-    for axis, dim in sides:
-        head = lax.slice_in_dim(cells, 0, width, axis=dim)
-        tail = lax.slice_in_dim(cells, cells.shape[dim] - width, cells.shape[dim], axis=dim)
-        cells = jnp.concatenate(
-            [from_behind(tail, axis, 1), cells, from_behind(head, axis, -1)], axis=dim
-        )
-    return cells
-
-
-def rows_for(lines, length):
-    spare = -lines.shape[0] % length
-    if not spare:
-        return lines
-    return jnp.concatenate([lines, jnp.zeros((spare, *lines.shape[1:]), lines.dtype)])
-
-
-def joined_along(parts, dim):
-    parts = jnp.moveaxis(parts, 0, dim)
-    dims = parts.shape
-    return parts.reshape(*dims[:dim], dims[dim] * dims[dim + 1], *dims[dim + 2 :])
-
-
-def gather_axes(x, axes, dim):
-    far, near = axes
-    parts = sent_to_all(sent_to_all(x, far), near)
-    return joined_along(parts.swapaxes(0, 1).reshape(-1, *x.shape), dim)
-
-
-def cut_along(x, dim, length):
-    before, after = (x.shape[:dim], x.shape[dim + 1 :])
-    return jnp.moveaxis(x.reshape(*before, length, -1, *after), dim, 0)
-
-
-def summed_on_arrival(x, axis, dim):
-    length = lax.axis_size(axis)
-    parts = lax.all_to_all(cut_along(x, dim, length), axis, 0, 0, tiled=True)
-    return jnp.sum(parts, axis=0)
-
-
-def summed_rows(x, axes, dim):
-    far, near = axes
-    own = summed_on_arrival(cut_along(x, dim, lax.axis_size(far)), near, dim + 1)
-    return jnp.sum(lax.all_to_all(own, far, 0, 0, tiled=True), axis=0)
-
-
-def sum_by_parts(x, axes):
-    padded = rows_for(x, lax.axis_size(axes[0]) * lax.axis_size(axes[1]))
-    whole = gather_axes(summed_rows(padded, axes, 0), axes, 0)
-    return lax.slice_in_dim(whole, 0, len(x)).reshape(x.shape)
-
-
-def packed_total(arrays, axis):
-    ends = [0]
-    for a in arrays:
-        ends.append(ends[-1] + a.size)
-    so_far = sum_by_parts(jnp.concatenate([a.ravel() for a in arrays]), axis)
-    return tuple((so_far[b:e].reshape(a.shape) for a, b, e in zip(arrays, ends, ends[1:])))
+def places():
+    return tuple(lax.axis_index(axis) for axis in ("beam", "row", "col_0", "col_1"))
+
+
+def sizes():
+    return tuple(lax.axis_size(axis) for axis in ("beam", "row", "col_0", "col_1"))
+
+
+def remote(src, dst, send_sem, recv_sem, **where):
+    return pltpu.make_async_remote_copy(
+        src_ref=src,
+        dst_ref=dst,
+        send_sem=send_sem,
+        recv_sem=recv_sem,
+        device_id=where,
+        device_id_type=MESH,
+    )
+
+
+def greet(barrier, **where):
+    pl.semaphore_signal(barrier, inc=1, device_id=where, device_id_type=MESH)
+
+
+def spread_kernel(
+    phase_ref, absorb_ref, t_ref, own_ref,
+    vol, part, inbox,
+    vol_sem, sum_send, sum_recv, beam_send, near_send, out_send, row_send, t_recv,
+):
+    beams, rows_n, deep_n, _ = sizes()
+    b, i, z, c = places()
+    h = phase_ref.shape[1] // beams
+    top = beams // 2
+    blocks = 2 * beams
+    half = top * h
+    out_z = z - 1 + 2 * c
+    has_out = (out_z >= 0) & (out_z < deep_n)
+    above, below = i > 0, i < rows_n - 1
+    order = [*range(1, beams), 0]
+    loads = {}
+    for o in order:
+        q = lax.rem(b + o, beams)
+        for p, ref in enumerate((phase_ref, absorb_ref)):
+            loads[o, p] = pltpu.make_async_copy(
+                ref.at[:, pl.ds(pl.multiple_of(q * h, h), h), :], vol.at[o, p], vol_sem.at[o, p]
+            )
+            loads[o, p].start()
+
+    barrier = pltpu.get_barrier_semaphore()
+    for o in range(1, beams):
+        greet(barrier, beam=lax.rem(b + o, beams))
+    greet(barrier, col_1=1 - c)
+
+    @pl.when(has_out)
+    def _():
+        greet(barrier, col_0=out_z, col_1=1 - c)
+
+    @pl.when(above)
+    def _():
+        greet(barrier, row=i - 1)
+
+    @pl.when(below)
+    def _():
+        greet(barrier, row=i + 1)
+
+    pl.semaphore_wait(
+        barrier,
+        beams + has_out.astype(jnp.int32) + above.astype(jnp.int32) + below.astype(jnp.int32),
+    )
+
+    sums = []
+    for o in order:
+        for p in range(2):
+            loads[o, p].wait()
+            total = vol[o, p, 0].astype(jnp.float32)
+            for d in range(1, phase_ref.shape[0]):
+                total = total + vol[o, p, d].astype(jnp.float32)
+            part[o, p] = total
+        if o:
+            copy = remote(
+                part.at[o], inbox.at[o], sum_send.at[o], sum_recv.at[o],
+                beam=lax.rem(b + o, beams),
+            )
+            copy.start()
+            sums.append(copy)
+    for copy in sums:
+        copy.wait_recv()
+    phase, absorb = part[0, 0], part[0, 1]
+    for o in range(1, beams):
+        phase = phase + inbox[o, 0]
+        absorb = absorb + inbox[o, 1]
+    damping = jnp.exp(-absorb)
+    tr, ti = damping * jnp.cos(phase), damping * jnp.sin(phase)
+    own_ref[0] = tr
+    own_ref[1] = ti
+
+    def cell(k, m):
+        return t_ref.at[:, k, pl.ds(pl.multiple_of(m * h, h), h), :]
+
+    mine = pl.ds(pl.multiple_of(half + b * h, h), h)
+    t_ref[0, 1, mine, :] = tr
+    t_ref[1, 1, mine, :] = ti
+    m0 = top + b
+    waits = []
+    ring = []
+    for o in [1, *range(3, beams), *range(2, min(3, beams))]:
+        copy = remote(
+            cell(1, m0), cell(1, m0), beam_send.at[o], t_recv.at[1, m0],
+            beam=lax.rem(b + o, beams),
+        )
+        copy.start()
+        waits.append((None, copy))
+        ring.append(o)
+
+    def sideways(m, slot, alive):
+        near = remote(
+            cell(1, m), cell(2 * c, m), near_send.at[slot], t_recv.at[2 * c, m], col_1=1 - c
+        )
+        far = remote(
+            cell(1, m), cell(2 - 2 * c, m), out_send.at[slot], t_recv.at[2 - 2 * c, m],
+            col_0=out_z, col_1=1 - c,
+        )
+        for copy, check in ((near, alive), (far, has_out if alive is None else has_out & alive)):
+            if check is None:
+                copy.start()
+            else:
+                pl.when(check)(copy.start)
+            waits.append((check, copy))
+
+    def arrived(k, m):
+        remote(cell(1, m), cell(k, m), near_send.at[0], t_recv.at[k, m], col_1=1 - c).wait_recv()
+
+    for slot, o in enumerate([0, *ring]):
+        q = lax.rem(b + o, beams)
+        m = top + q
+        if o:
+            arrived(1, m)
+        upper = q // top
+        goal = i - 1 + 2 * upper
+        copy = remote(
+            cell(1, m),
+            cell(1, q - top + (1 - upper) * blocks),
+            row_send.at[slot],
+            t_recv.at[1, q - top + (1 - upper) * blocks],
+            row=goal,
+        )
+        alive = (goal >= 0) & (goal < rows_n)
+        pl.when(alive)(copy.start)
+        waits.append((alive, copy))
+        sideways(m, slot, None)
+    for at in range(top):
+        for m, alive in ((at, above), (top + beams + at, below)):
+            pl.when(alive)(functools.partial(arrived, 1, m))
+            sideways(m, beams + (m if m < top else m - beams), alive)
+    for m in range(blocks):
+        alive = above if m < top else below if m >= top + beams else None
+        if alive is None:
+            arrived(2 - 2 * c, m)
+            pl.when(has_out)(functools.partial(arrived, 2 * c, m))
+        else:
+            pl.when(alive)(functools.partial(arrived, 2 - 2 * c, m))
+            pl.when(alive & has_out)(functools.partial(arrived, 2 * c, m))
+    for copy in sums:
+        copy.wait_send()
+    for alive, copy in waits:
+        if alive is None:
+            copy.wait_send()
+        else:
+            pl.when(alive)(copy.wait_send)
+    tall = blocks * h
+
+    def blank(tiles, start, size):
+        for k in tiles:
+            t_ref[0, k, pl.ds(start, size), :] = jnp.ones((size, LANES), jnp.float32)
+            t_ref[1, k, pl.ds(start, size), :] = jnp.zeros((size, LANES), jnp.float32)
+
+    pl.when(i == 0)(lambda: blank(range(3), 0, half))
+    pl.when(i == rows_n - 1)(lambda: blank(range(3), tall - half, half))
+    pl.when((z == 0) & (c == 0))(lambda: blank((0,), 0, tall))
+    pl.when((z == deep_n - 1) & (c == 1))(lambda: blank((2,), 0, tall))
+
+
+def transmission(phase_volume, absorb_volume):
+    deep, rows, lanes = phase_volume.shape
+    beams = lax.axis_size("beam")
+    h = rows // beams
+    return pl.pallas_call(
+        spread_kernel,
+        out_shape=[
+            jax.ShapeDtypeStruct((2, 3, 2 * rows, lanes), jnp.float32),
+            jax.ShapeDtypeStruct((2, h, lanes), jnp.float32),
+        ],
+        in_specs=[pl.BlockSpec(memory_space=pl.ANY)] * 2,
+        out_specs=[pl.BlockSpec(memory_space=pltpu.VMEM)] * 2,
+        scratch_shapes=[
+            pltpu.VMEM((beams, 2, deep, h, lanes), jnp.bfloat16),
+            pltpu.VMEM((beams, 2, h, lanes), jnp.float32),
+            pltpu.VMEM((beams, 2, h, lanes), jnp.float32),
+            pltpu.SemaphoreType.DMA((beams, 2)),
+            pltpu.SemaphoreType.DMA((beams,)),
+            pltpu.SemaphoreType.DMA((beams,)),
+            pltpu.SemaphoreType.DMA((beams,)),
+            pltpu.SemaphoreType.DMA((2 * beams,)),
+            pltpu.SemaphoreType.DMA((2 * beams,)),
+            pltpu.SemaphoreType.DMA((beams,)),
+            pltpu.SemaphoreType.DMA((3, 2 * beams)),
+        ],
+        compiler_params=pltpu.CompilerParams(collective_id=0, has_side_effects=True),
+        name="spread",
+    )(phase_volume, absorb_volume)
+
+
+def fold_kernel(
+    scale, pixels, canvas_ref, own_ref, probe_ref, misfit_ref,
+    step_ref, probe_out, loss_ref,
+    sib_in, out_in, acc, row_in, q_in, grad, p_in, p_sum, x_in, z_in, n_xy, n_zc,
+    sib_send, sib_recv, out_send, out_recv, row_send, row_recv, q_send, q_recv,
+    g_send, g_recv, p_send, p_recv, x_send, x_recv, z_send, z_recv, y_send, y_recv,
+    n_send, n_recv, m_send, m_recv,
+):
+    beams, rows_n, deep_n, cores = sizes()
+    b, i, z, c = places()
+    rows = grad.shape[1]
+    h = rows // beams
+    half = rows // 2
+    tall = 2 * rows
+    plane = beams * rows_n
+    across = deep_n * cores
+    share = p_sum.shape[0] // plane
+    me_xy = b * rows_n + i
+    me_zc = z * cores + c
+    out_z = z - 1 + 2 * c
+    has_out = (out_z >= 0) & (out_z < deep_n)
+    above, below = i > 0, i < rows_n - 1
+    finish = []
+
+    def go(copy, check=None):
+        if check is None:
+            copy.start()
+        else:
+            pl.when(check)(copy.start)
+        finish.append((check, copy))
+        return copy
+
+    def peer_xy(o):
+        return dict(beam=lax.rem(b + o // rows_n, beams), row=lax.rem(i + o % rows_n, rows_n))
+
+    def peer_zc(o):
+        return dict(col_0=lax.rem(z + o // cores, deep_n), col_1=lax.rem(c + o % cores, cores))
+
+    barrier = pltpu.get_barrier_semaphore()
+    for o in range(1, plane):
+        greet(barrier, **peer_xy(o))
+    for o in range(1, across):
+        greet(barrier, **peer_zc(o))
+    pl.semaphore_wait(barrier, plane + across - 2)
+
+    half_copy = go(remote(probe_ref.at[1 - c], p_in, p_send.at[0], p_recv.at[0], col_1=1 - c))
+    spans = [(0, half, above), (tall - half, half, below), (half, rows, None)]
+    near, far = [], []
+    for e, (start, size, alive) in enumerate(spans):
+        where = pl.ds(start, size)
+        far.append(
+            go(
+                remote(
+                    canvas_ref.at[:, 2 * c, where, :], out_in.at[:, where, :],
+                    out_send.at[e], out_recv.at[e], col_0=out_z, col_1=1 - c,
+                ),
+                has_out if alive is None else has_out & alive,
+            )
+        )
+        near.append(
+            go(
+                remote(
+                    canvas_ref.at[:, 2 - 2 * c, where, :], sib_in.at[:, where, :],
+                    sib_send.at[e], sib_recv.at[e], col_1=1 - c,
+                ),
+                alive,
+            )
+        )
+    half_copy.wait_recv()
+    p_sum[...] = probe_ref[c] + p_in[...]
+    parts = []
+    for o in range(1, plane):
+        peer = peer_xy(o)
+        there = pl.multiple_of((peer["beam"] * rows_n + peer["row"]) * share, share)
+        parts.append(
+            go(
+                remote(
+                    p_sum.at[pl.ds(there, share), :], x_in.at[o], x_send.at[o], x_recv.at[o], **peer
+                )
+            )
+        )
+
+    def merge(e):
+        start, size, _ = spans[e]
+        where = pl.ds(start, size)
+        near[e].wait_recv()
+        acc[:, where, :] = canvas_ref[:, 1, where, :] + sib_in[:, where, :]
+
+        @pl.when(has_out)
+        def _():
+            far[e].wait_recv()
+            acc[:, where, :] += out_in[:, where, :]
+
+    rims = []
+    for e, goal in ((0, i - 1), (1, i + 1)):
+        start, size, alive = spans[e]
+        pl.when(alive)(functools.partial(merge, e))
+        rims.append(
+            go(
+                remote(
+                    acc.at[:, pl.ds(start, size), :], row_in.at[e],
+                    row_send.at[e], row_recv.at[e], row=goal,
+                ),
+                alive,
+            )
+        )
+    merge(2)
+
+    @pl.when(below)
+    def _():
+        rims[0].wait_recv()
+        acc[:, pl.ds(rows, half), :] += row_in[0]
+
+    @pl.when(above)
+    def _():
+        rims[1].wait_recv()
+        acc[:, pl.ds(half, half), :] += row_in[1]
+
+    quarters = []
+    for o in range(1, beams):
+        q = lax.rem(b + o, beams)
+        there = pl.multiple_of(half + q * h, h)
+        quarters.append(
+            go(
+                remote(
+                    acc.at[:, pl.ds(there, h), :], q_in.at[o], q_send.at[o], q_recv.at[o], beam=q
+                )
+            )
+        )
+    total = p_sum[pl.ds(pl.multiple_of(me_xy * share, share), share), :]
+    for o in range(1, plane):
+        parts[o - 1].wait_recv()
+        total = total + x_in[o]
+    z_in[z] = total
+    levels = []
+    for o in range(1, deep_n):
+        levels.append(
+            go(
+                remote(
+                    z_in.at[z], z_in.at[z], z_send.at[o], z_recv.at[o],
+                    col_0=lax.rem(z + o, deep_n),
+                )
+            )
+        )
+
+    mine = pl.ds(pl.multiple_of(half + b * h, h), h)
+    cr, ci = acc[0, mine, :], acc[1, mine, :]
+    for o in range(1, beams):
+        quarters[o - 1].wait_recv()
+        cr = cr + q_in[o, 0]
+        ci = ci + q_in[o, 1]
+    tr, ti = own_ref[0], own_ref[1]
+    phase = tr * ci - ti * cr
+    absorb = -(tr * cr + ti * ci)
+    home = pl.ds(pl.multiple_of(b * h, h), h)
+    grad[0, home, :] = phase
+    grad[1, home, :] = absorb
+    squares = phase * phase + absorb * absorb
+    n_xy[me_xy, 0] = jnp.sum(squares.reshape(h // 8, 8, LANES), axis=0)
+    n_xy[me_xy, 1] = misfit_ref[...]
+    norms = []
+    for o in range(1, plane):
+        norms.append(
+            go(
+                remote(
+                    n_xy.at[me_xy], n_xy.at[me_xy], n_send.at[o], n_recv.at[o], **peer_xy(o)
+                )
+            )
+        )
+    grads = []
+    for o in range(1, beams):
+        grads.append(
+            go(
+                remote(
+                    grad.at[:, home, :], grad.at[:, home, :], g_send.at[o], g_recv.at[o],
+                    beam=lax.rem(b + o, beams),
+                )
+            )
+        )
+
+    for copy in levels:
+        copy.wait_recv()
+    total = z_in[0]
+    for k in range(1, deep_n):
+        total = total + z_in[k]
+    piece = pl.ds(pl.multiple_of(me_xy * share, share), share)
+    probe_out[c, piece, :] = total * scale
+    spreads = []
+    for o in range(1, plane):
+        spreads.append(
+            go(
+                remote(
+                    probe_out.at[c, piece, :], probe_out.at[c, piece, :],
+                    y_send.at[o], y_recv.at[o], **peer_xy(o),
+                )
+            )
+        )
+
+    for copy in norms:
+        copy.wait_recv()
+    pair = n_xy[0]
+    for k in range(1, plane):
+        pair = pair + n_xy[k]
+    n_zc[me_zc] = pair
+    norms = []
+    for o in range(1, across):
+        norms.append(
+            go(
+                remote(
+                    n_zc.at[me_zc], n_zc.at[me_zc], m_send.at[o], m_recv.at[o], **peer_zc(o)
+                )
+            )
+        )
+    for copy in spreads:
+        copy.wait_recv()
+    last = go(remote(probe_out.at[c], probe_out.at[c], p_send.at[1], p_recv.at[1], col_1=1 - c))
+    for copy in norms:
+        copy.wait_recv()
+    pair = n_zc[0]
+    for k in range(1, across):
+        pair = pair + n_zc[k]
+    sums = jnp.sum(jnp.sum(pair, axis=1, keepdims=True), axis=2, keepdims=True)
+    mean_square = sums[0] / (2 * rows * LANES * rows_n * across)
+    factor = jnp.minimum(1.0, 0.5 / jnp.sqrt(mean_square + 1e-06))
+    loss_ref[...] = jnp.broadcast_to(sums[1] * (scale / pixels), loss_ref.shape)
+    for copy in grads:
+        copy.wait_recv()
+    for p in range(2):
+        step_ref[p] = grad[p] * factor
+    last.wait_recv()
+    for check, copy in finish:
+        if check is None:
+            copy.wait_send()
+        else:
+            pl.when(check)(copy.wait_send)
+
+
+def folded(canvas, own, probe_sum, misfit, positions):
+    beams, rows_n, deep_n, cores = sizes()
+    _, _, tall, lanes = canvas.shape
+    rows = tall // 2
+    h = rows // beams
+    n = probe_sum.shape[1]
+    plane, across = beams * rows_n, deep_n * cores
+    f32 = functools.partial(pltpu.VMEM, dtype=jnp.float32)
+    sems = [3, 3, 3, 3, 2, 2, beams, beams, beams, beams, 2, 2, plane, plane, deep_n, deep_n]
+    sems += [plane, plane, plane, plane, across, across]
+    return pl.pallas_call(
+        functools.partial(fold_kernel, 1.0 / positions, n * n),
+        out_shape=[
+            jax.ShapeDtypeStruct((2, rows, lanes), jnp.float32),
+            jax.ShapeDtypeStruct(probe_sum.shape, jnp.float32),
+            jax.ShapeDtypeStruct((8, LANES), jnp.float32),
+        ],
+        in_specs=[pl.BlockSpec(memory_space=pltpu.VMEM)] * 4,
+        out_specs=[pl.BlockSpec(memory_space=pltpu.VMEM)] * 3,
+        scratch_shapes=[
+            f32((2, tall, lanes)),
+            f32((2, tall, lanes)),
+            f32((2, tall, lanes)),
+            f32((2, 2, rows // 2, lanes)),
+            f32((beams, 2, h, lanes)),
+            f32((2, rows, lanes)),
+            f32((n, n)),
+            f32((n, n)),
+            f32((plane, n // plane, n)),
+            f32((deep_n, n // plane, n)),
+            f32((plane, 2, 8, LANES)),
+            f32((across, 2, 8, LANES)),
+            *[pltpu.SemaphoreType.DMA((count,)) for count in sems],
+        ],
+        compiler_params=pltpu.CompilerParams(collective_id=1, has_side_effects=True),
+        name="fold",
+    )(canvas, own, probe_sum, misfit)
 
 
 def local(phase_volume, absorb_volume, probe, amplitudes, scan_rows, scan_cols):
     length = probe.shape[1]
-    half = length // 2
     count = scan_rows.shape[2]
-    rows_local = phase_volume.shape[1]
-    cols_local = phase_volume.shape[2]
-    part = jnp.stack(
-        [
-            jnp.sum(phase_volume, axis=0, dtype=jnp.float32),
-            jnp.sum(absorb_volume, axis=0, dtype=jnp.float32),
-        ]
-    )
-    summed = over_copies(part, "beam")
-    tall = extended(summed, (("row", 1),), half)
-    wide = jnp.stack([from_behind(tall, COL, 1), tall, from_behind(tall, COL, -1)], axis=1)
-    damping = jnp.exp(-wide[1])
-    t = jnp.stack([damping * jnp.cos(wide[0]), damping * jnp.sin(wide[0])])
+    beams, rows_n, deep_n, cores = sizes()
+    t, own = transmission(phase_volume, absorb_volume)
     canvas, probe_term, misfit = window_terms(
         t,
         probe,
@@ -254,32 +655,15 @@
         scan_rows.reshape(count),
         scan_cols.reshape(count),
     )
-    middle = canvas[:, 1] + from_behind(canvas[:, 0], COL, -1) + from_behind(canvas[:, 2], COL, 1)
-    center = middle[:, half : half + rows_local]
-    below = from_behind(middle[:, :half], "row", -1)
-    above = from_behind(middle[:, half + rows_local :], "row", 1)
-    center = center + jnp.pad(below, ((0, 0), (rows_local - half, 0), (0, 0)))
-    center = center + jnp.pad(above, ((0, 0), (0, rows_local - half), (0, 0)))
-    center = over_copies(center, "beam")
-    tr = t[0, 1, half : half + rows_local]
-    ti = t[1, 1, half : half + rows_local]
-    gradient = jnp.stack(
-        [tr * center[1] - ti * center[0], -(tr * center[0] + ti * center[1])]
-    )
-    probe_total, misfit_total = packed_total(
-        (probe_term, jnp.sum(misfit)), ("beam", ("row", "col_0", "col_1"))
-    )
-    square_sum = over_copies(jnp.sum(gradient * gradient), ROW_COL)
-    plane_devices = lax.axis_size("row") * lax.axis_size(COL)
-    mean_square = square_sum / (2 * rows_local * cols_local * plane_devices)
-    factor = jnp.minimum(1.0, 0.5 / jnp.sqrt(mean_square + 1e-06))
-    total = plane_devices * lax.axis_size("beam") * count
-    return (gradient * factor, probe_total / total, misfit_total / (total * length * length))
+    step, probe_total, loss = folded(
+        canvas, own, probe_term, misfit, beams * rows_n * deep_n * cores * count
+    )
+    return (step, probe_total, loss[0, 0])
 
 
 def solution(mesh):
     split = Mesh(
-        mesh.devices.reshape(mesh.shape["beam"], mesh.shape["row"], 8, 2),
+        mesh.devices.reshape(mesh.shape["beam"], mesh.shape["row"], -1, 2),
         ("beam", "row", "col_0", "col_1"),
     )
     in_specs = (

time: 195 us -> 84.9 us (0.44)
  waiting for transfers between devices: 72.3 us -> 0 us
  Pallas kernels: 16.1 us -> 79.2 us
  starting transfers between devices: 59.8 us -> 0 us
  blocking collectives: 19 us -> 0 us
  other arithmetic: 10.5 us -> 0 us
  local copies, waits for them, and re-layouts: 12.7 us -> 4.71 us
  between operations: 3.4 us -> 0.65 us
    pallas_call x0 -> x2, Pallas kernels: none -> 63.1 us  [the longest x1 40.2 us: folded(): pl.pallas_call(functools.partial(fold_kernel, 1.0 / positions, n * n), ou...]
    all_to_all x6 -> x0, waiting for transfers between devices: 61.8 us -> none  [the longest x4 44.4 us: sent_to_all(): return lax.all_to_all(copies, axis, split_axis=0, concat_axis=0, tiled=True)]
    all_to_all x6 -> x0, starting transfers between devices: 35.2 us -> none  [the longest x4 20.5 us: sent_to_all(): return lax.all_to_all(copies, axis, split_axis=0, concat_axis=0, tiled=True)]
    ppermute x8 -> x0, starting transfers between devices: 24.6 us -> none  [from_behind(): lax.ppermute(value, axis, [(source, source + steps) for source in range(f...]
    all_to_all x1 -> x0, blocking collectives: 19 us -> none  [sent_to_all(): return lax.all_to_all(copies, axis, split_axis=0, concat_axis=0, tiled=True)]
    ppermute x8 -> x0, waiting for transfers between devices: 10.5 us -> none  [from_behind(): lax.ppermute(value, axis, [(source, source + steps) for source in range(f...]
    broadcast_in_dim x6 -> x0, local copies, waits for them, and re-layouts: 3.92 us -> none  [the longest x5 3.92 us: sent_to_all(): copies = jnp.broadcast_to(x, (lax.axis_size(axis), *x.shape))]
    reduce_sum x9 -> x0, other arithmetic: 3.84 us -> none  [the longest x1 1.46 us: local(): jnp.sum(phase_volume, axis=0, dtype=jnp.float32)]
  transfers between devices with their start and end apart: 14 -> 0, of which waited for: 10 -> 0; matrix products, arithmetic and copies ran while one was open for 4% -> 0% of each run, Pallas kernels for 0% -> 0%
where the time goes in v2:
time: 84.9 us; the launch traced here: 84.5 us
  Pallas kernels  79.2 us (93%)
  local copies, waits for them, and re-layouts  4.71 us (6%)
    pallas_call x1, Pallas kernels, folded(): pl.pallas_call(functools.partial(fold_kernel, 1.0 / positions, n * n), ou...  40.2 us
    pallas_call x1, Pallas kernels, transmission(): pl.pallas_call(spread_kernel, out_shape=[jax.ShapeDtypeStruct((2, 3, 2 *...  22.9 us
    pallas_call x1, Pallas kernels, window_terms(): pl.pallas_call(window_kernel, grid_spec=grid_spec, out_shape=[jax.ShapeDt...  16.1 us
    unnamed x2, local copies, waits for them, and re-layouts  3.54 us

profile of v2, /device:TPU:1, one launch (start us, length us, event | category | flops | bytes accessed | tf_op | source)
XLA Modules:
  0.0 84.5 jit_solution(2026335007547722446)
XLA Ops:
  0.6 22.9 %spread.1 = (f32[2,3,512,128]{3,2,1,0:T(8,128)}, f32[2,64,128]{2,1,0:T(8,128)}) custom-call(bf16[16,256,128]{2,1,0:T(8,128)(2,1)} %phase_ref.1, bf16[16,256,128]{2,1,0:T(8,128)(2,1)} %absorb_ref.1), custom_call_target="tpu_custom_call" | custom-call | tf_op jit(solution)/shard_map/spread/pallas_call | solution.py:344
  23.5 16.1 %windows.1 = (f32[2,3,512,128]{3,2,1,0:T(8,128)}, f32[2,256,256]{2,1,0:T(8,128)}, f32[8,128]{1,0:T(8,128)}) custom-call(s32[8]{0:T(128)} %bitcast.5, s32[8]{0:T(128)} %bitcast.6, f32[2,3,512,128]{3,2,1,0:T(8,128)} %get-tuple-element.11.t_ref, f32[2,256,256]{2,1,0:T(8,128)} %probe_ref.1, bf16[8,256,256]{2,1,0:T(8,128)(2,1)} %bitcast.4, ...), custom_call_target="tpu_custom_call" | custom-call | tf_op jit(solution)/shard_map/windows/pallas_call | solution.py:146
  39.6 40.2 %fold.1 = (f32[2,256,128]{2,1,0:T(8,128)}, f32[2,256,256]{2,1,0:T(8,128)}, f32[8,128]{1,0:T(8,128)}) custom-call(f32[2,3,512,128]{3,2,1,0:T(8,128)} %get-tuple-element.12.canvas_ref, f32[2,64,128]{2,1,0:T(8,128)} %get-tuple-element.13.own_ref, f32[2,256,256]{2,1,0:T(8,128)} %get-tuple-element.14.probe_ref, f32[8,128]{1,0:T(8,128)} %get-tuple-element.15.misfit_ref), custom_call_target="tpu_custom_call" | custom-call | tf_op jit(solution)/shard_map/fold/pallas_call | solution.py:617
  79.8 1.2 %slice.3 = f32[1,1]{1,0:T(1,128)} slice(f32[8,128]{1,0:T(8,128)} %get-tuple-element.18), slice={[0:1], [0:1]} | slice | bytes 8 | tf_op jit(solution)/shard_map/slice | solution.py:661
  81.0 1.7 %copy.13 = f32[2,256,128]{2,1,0:T(8,128)} copy(f32[2,256,128]{2,1,0:T(8,128)} %get-tuple-element.22) | data formatting | bytes 524288
  82.7 1.9 %copy.14 = f32[2,256,256]{2,1,0:T(8,128)} copy(f32[2,256,256]{2,1,0:T(8,128)} %get-tuple-element.23) | data formatting | bytes 1048576

commit v3 on v2

--- a/solution.py
+++ b/solution.py
@@ -14,6 +14,7 @@
 MESH = pl.DeviceIdType.MESH
 LANES = 128
 CHUNK = 128
+VMEM_LIMIT = 20 << 20
 
 
 def dft_tables(length):
@@ -151,7 +152,7 @@
             jax.ShapeDtypeStruct(probe.shape, jnp.float32),
             jax.ShapeDtypeStruct((8, LANES), jnp.float32),
         ],
-        compiler_params=pltpu.CompilerParams(dimension_semantics=("arbitrary",)),
+        compiler_params=pltpu.CompilerParams(dimension_semantics=("arbitrary",), vmem_limit_bytes=VMEM_LIMIT),
         name="windows",
     )(rows, cols, t, probe, amplitudes, jnp.stack(dft_tables(n)))
 
@@ -347,7 +348,7 @@
             jax.ShapeDtypeStruct((2, 3, 2 * rows, lanes), jnp.float32),
             jax.ShapeDtypeStruct((2, h, lanes), jnp.float32),
         ],
-        in_specs=[pl.BlockSpec(memory_space=pl.ANY)] * 2,
+        in_specs=[pl.BlockSpec(memory_space=pltpu.HBM)] * 2,
         out_specs=[pl.BlockSpec(memory_space=pltpu.VMEM)] * 2,
         scratch_shapes=[
             pltpu.VMEM((beams, 2, deep, h, lanes), jnp.bfloat16),
@@ -362,15 +363,17 @@
             pltpu.SemaphoreType.DMA((beams,)),
             pltpu.SemaphoreType.DMA((3, 2 * beams)),
         ],
-        compiler_params=pltpu.CompilerParams(collective_id=0, has_side_effects=True),
+        compiler_params=pltpu.CompilerParams(
+            collective_id=0, has_side_effects=True, vmem_limit_bytes=VMEM_LIMIT
+        ),
         name="spread",
     )(phase_volume, absorb_volume)
 
 
 def fold_kernel(
-    scale, pixels, canvas_ref, own_ref, probe_ref, misfit_ref,
-    step_ref, probe_out, loss_ref,
-    sib_in, out_in, acc, row_in, q_in, grad, p_in, p_sum, x_in, z_in, n_xy, n_zc,
+    scale, canvas_ref, own_ref, probe_ref, misfit_ref,
+    grad, probe_out, sums_ref,
+    sib_in, out_in, acc, row_in, q_in, p_in, p_sum, x_in, z_in, n_xy, n_zc,
     sib_send, sib_recv, out_send, out_recv, row_send, row_recv, q_send, q_recv,
     g_send, g_recv, p_send, p_recv, x_send, x_recv, z_send, z_recv, y_send, y_recv,
     n_send, n_recv, m_send, m_recv,
@@ -524,9 +527,14 @@
     home = pl.ds(pl.multiple_of(b * h, h), h)
     grad[0, home, :] = phase
     grad[1, home, :] = absorb
-    squares = phase * phase + absorb * absorb
-    n_xy[me_xy, 0] = jnp.sum(squares.reshape(h // 8, 8, LANES), axis=0)
-    n_xy[me_xy, 1] = misfit_ref[...]
+    squares = jnp.sum(phase * phase + absorb * absorb, axis=0, keepdims=True)
+    misfits = jnp.sum(misfit_ref[...], axis=0, keepdims=True)
+    left = lax.broadcasted_iota(jnp.int32, (1, LANES), 1) < LANES // 2
+    n_xy[me_xy] = jnp.where(
+        left,
+        squares + pltpu.roll(squares, LANES // 2, 1),
+        misfits + pltpu.roll(misfits, LANES // 2, 1),
+    )
     norms = []
     for o in range(1, plane):
         norms.append(
@@ -588,14 +596,9 @@
     pair = n_zc[0]
     for k in range(1, across):
         pair = pair + n_zc[k]
-    sums = jnp.sum(jnp.sum(pair, axis=1, keepdims=True), axis=2, keepdims=True)
-    mean_square = sums[0] / (2 * rows * LANES * rows_n * across)
-    factor = jnp.minimum(1.0, 0.5 / jnp.sqrt(mean_square + 1e-06))
-    loss_ref[...] = jnp.broadcast_to(sums[1] * (scale / pixels), loss_ref.shape)
+    sums_ref[...] = pair
     for copy in grads:
         copy.wait_recv()
-    for p in range(2):
-        step_ref[p] = grad[p] * factor
     last.wait_recv()
     for check, copy in finish:
         if check is None:
@@ -615,11 +618,11 @@
     sems = [3, 3, 3, 3, 2, 2, beams, beams, beams, beams, 2, 2, plane, plane, deep_n, deep_n]
     sems += [plane, plane, plane, plane, across, across]
     return pl.pallas_call(
-        functools.partial(fold_kernel, 1.0 / positions, n * n),
+        functools.partial(fold_kernel, 1.0 / positions),
         out_shape=[
             jax.ShapeDtypeStruct((2, rows, lanes), jnp.float32),
             jax.ShapeDtypeStruct(probe_sum.shape, jnp.float32),
-            jax.ShapeDtypeStruct((8, LANES), jnp.float32),
+            jax.ShapeDtypeStruct((1, LANES), jnp.float32),
         ],
         in_specs=[pl.BlockSpec(memory_space=pltpu.VMEM)] * 4,
         out_specs=[pl.BlockSpec(memory_space=pltpu.VMEM)] * 3,
@@ -629,18 +632,46 @@
             f32((2, tall, lanes)),
             f32((2, 2, rows // 2, lanes)),
             f32((beams, 2, h, lanes)),
-            f32((2, rows, lanes)),
             f32((n, n)),
             f32((n, n)),
             f32((plane, n // plane, n)),
             f32((deep_n, n // plane, n)),
-            f32((plane, 2, 8, LANES)),
-            f32((across, 2, 8, LANES)),
+            f32((plane, 1, LANES)),
+            f32((across, 1, LANES)),
             *[pltpu.SemaphoreType.DMA((count,)) for count in sems],
         ],
-        compiler_params=pltpu.CompilerParams(collective_id=1, has_side_effects=True),
+        compiler_params=pltpu.CompilerParams(
+            collective_id=1, has_side_effects=True, vmem_limit_bytes=VMEM_LIMIT
+        ),
         name="fold",
     )(canvas, own, probe_sum, misfit)
+
+
+def finish_kernel(entries, terms, grad_ref, probe_ref, sums_ref, step_ref, probe_out, loss_ref):
+    sums = sums_ref[...]
+    left = lax.broadcasted_iota(jnp.int32, sums.shape, 1) < LANES // 2
+    square = jnp.sum(jnp.where(left, sums, 0.0), axis=1, keepdims=True)
+    factor = jnp.minimum(1.0, 0.5 / jnp.sqrt(square / entries + 1e-06))
+    for p in range(2):
+        step_ref[p] = grad_ref[p] * factor
+    probe_out[...] = probe_ref[...]
+    loss_ref[...] = jnp.sum(jnp.where(left, 0.0, sums), axis=1, keepdims=True) / terms
+
+
+def finished(grad, probe_total, sums, entries, terms):
+    vmem = pl.BlockSpec(memory_space=pltpu.VMEM)
+    return pl.pallas_call(
+        functools.partial(finish_kernel, entries, terms),
+        out_shape=[
+            jax.ShapeDtypeStruct(grad.shape, jnp.float32),
+            jax.ShapeDtypeStruct(probe_total.shape, jnp.float32),
+            jax.ShapeDtypeStruct((1, 1), jnp.float32),
+        ],
+        in_specs=[vmem] * 3,
+        out_specs=[vmem] * 3,
+        compiler_params=pltpu.CompilerParams(vmem_limit_bytes=VMEM_LIMIT),
+        name="finish",
+    )(grad, probe_total, sums)
 
 
 def local(phase_volume, absorb_volume, probe, amplitudes, scan_rows, scan_cols):
@@ -655,8 +686,11 @@
         scan_rows.reshape(count),
         scan_cols.reshape(count),
     )
-    step, probe_total, loss = folded(
-        canvas, own, probe_term, misfit, beams * rows_n * deep_n * cores * count
+    positions = beams * rows_n * deep_n * cores * count
+    grad, probe_total, sums = folded(canvas, own, probe_term, misfit, positions)
+    entries = grad.size * rows_n * deep_n * cores
+    step, probe_total, loss = finished(
+        grad, probe_total, sums, entries, positions * length * length
     )
     return (step, probe_total, loss[0, 0])
 

time: 84.9 us -> 75.1 us (0.88)
  Pallas kernels: 79.2 us -> 71.6 us
  local copies, waits for them, and re-layouts: 4.71 us -> 2.47 us
    pallas_call x1 -> x2, Pallas kernels: 40.2 us -> 36.9 us  [the longest x1 36 us: folded(): pl.pallas_call(functools.partial(fold_kernel, 1.0 / positions), out_shape...]
    pallas_call x1, Pallas kernels: 16.1 us -> 13 us  [window_terms(): pl.pallas_call(window_kernel, grid_spec=grid_spec, out_shape=[jax.ShapeDt...]
    pallas_call x1, Pallas kernels: 22.9 us -> 21.7 us  [transmission(): pl.pallas_call(spread_kernel, out_shape=[jax.ShapeDtypeStruct((2, 3, 2 *...]
    slice x1 -> x0, local copies, waits for them, and re-layouts: 1.17 us -> none  [local(): return (step, probe_total, loss[0, 0])]
    unnamed x2 -> x14, local copies, waits for them, and re-layouts: 3.54 us -> 2.47 us
where the time goes in v3:
time: 75.1 us; the launch traced here: 74.8 us
  Pallas kernels  71.6 us (95%)
  local copies, waits for them, and re-layouts  2.47 us (3%)
    pallas_call x1, Pallas kernels, folded(): pl.pallas_call(functools.partial(fold_kernel, 1.0 / positions), out_shape...  36 us
    pallas_call x1, Pallas kernels, transmission(): pl.pallas_call(spread_kernel, out_shape=[jax.ShapeDtypeStruct((2, 3, 2 *...  21.7 us
    pallas_call x1, Pallas kernels, window_terms(): pl.pallas_call(window_kernel, grid_spec=grid_spec, out_shape=[jax.ShapeDt...  13 us
    unnamed x14, local copies, waits for them, and re-layouts  2.47 us

profile of v3, /device:TPU:1, one launch (start us, length us, event | category | flops | bytes accessed | tf_op | source)
XLA Modules:
  0.0 74.8 jit_solution(9870688944876728206)
XLA Ops:
  0.6 0.0 copy-start.6
  0.6 0.0 copy-start.5
  0.7 0.0 copy-start
  0.7 1.2 %copy-done = bf16[16,256,128]{2,1,0:T(8,128)(2,1)S(1)} copy-done((bf16[16,256,128]{2,1,0:T(8,128)(2,1)S(1)}, bf16[16,256,128]{2,1,0:T(8,128)(2,1)}, u32[]{:S(2)}) %copy-start) | copy-done | bytes 1048600
  1.9 0.0 copy-start.1
  1.9 1.2 %copy-done.1 = bf16[16,256,128]{2,1,0:T(8,128)(2,1)S(1)} copy-done((bf16[16,256,128]{2,1,0:T(8,128)(2,1)S(1)}, bf16[16,256,128]{2,1,0:T(8,128)(2,1)}, u32[]{:S(2)}) %copy-start.1) | copy-done | bytes 1048600
  3.1 0.0 copy-start.2
  3.1 0.0 copy-start.3
  3.1 0.0 copy-start.4
  3.1 21.7 %spread.1 = (f32[2,3,512,128]{3,2,1,0:T(8,128)S(1)}, f32[2,64,128]{2,1,0:T(8,128)S(1)}) custom-call(bf16[16,256,128]{2,1,0:T(8,128)(2,1)S(1)} %copy-done, bf16[16,256,128]{2,1,0:T(8,128)(2,1)S(1)} %copy-done.1), custom_call_target="tpu_custom_call" | custom-call | tf_op jit(solution)/shard_map/spread/pallas_call | solution.py:345
  24.8 0.0 copy-done.6
  24.8 0.0 copy-done.5
  24.8 0.0 copy-done.2
  24.9 0.0 copy-done.3
  24.9 0.0 copy-done.4
  24.9 13.0 %windows.1 = (f32[2,3,512,128]{3,2,1,0:T(8,128)S(1)}, f32[2,256,256]{2,1,0:T(8,128)S(1)}, f32[8,128]{1,0:T(8,128)S(1)}) custom-call(s32[8]{0:T(128)S(1)} %bitcast.5, s32[8]{0:T(128)S(1)} %bitcast.6, f32[2,3,512,128]{3,2,1,0:T(8,128)S(1)} %get-tuple-element.14.t_ref, f32[2,256,256]{2,1,0:T(8,128)S(1)} %copy-done.3, bf16[8,256,256]{2,1,0:T(8,128)(2,1)S(1)} %bitcast.4, ...), custom_call_target="tpu_custom_call" | custom-call | tf_op jit(solution)/shard_map/windows/pallas_call | solution.py:147
  37.9 36.0 %fold.1 = (f32[2,256,128]{2,1,0:T(8,128)S(1)}, f32[2,256,256]{2,1,0:T(8,128)S(1)}, f32[1,128]{1,0:T(1,128)S(1)}) custom-call(f32[2,3,512,128]{3,2,1,0:T(8,128)S(1)} %get-tuple-element.15.canvas_ref, f32[2,64,128]{2,1,0:T(8,128)S(1)} %get-tuple-element.16.own_ref, f32[2,256,256]{2,1,0:T(8,128)S(1)} %get-tuple-element.17.probe_ref, ...), custom_call_target="tpu_custom_call" | custom-call | tf_op jit(solution)/shard_map/fold/pallas_call | solution.py:620
  73.9 0.9 %finish.1 = (f32[2,256,128]{2,1,0:T(8,128)}, f32[2,256,256]{2,1,0:T(8,128)}, f32[1,1]{1,0:T(1,128)}) custom-call(f32[2,256,128]{2,1,0:T(8,128)S(1)} %get-tuple-element.19.grad_ref, f32[2,256,256]{2,1,0:T(8,128)S(1)} %get-tuple-element.20.probe_ref, f32[1,128]{1,0:T(1,128)S(1)} %get-tuple-element.21.sums_ref), custom_call_target="tpu_custom_call" | custom-call | tf_op jit(solution)/shard_map/finish/pallas_call | solution.py:663
Async XLA Ops:
  0.6 24.2 %copy-start.6 = (s32[1,1,8]{2,1,0:T(1,128)S(1)}, s32[1,1,8]{2,1,0:T(1,128)}, u32[]{:S(2)}) copy-start(s32[1,1,8]{2,1,0:T(1,128)} %param.13) | copy-start | bytes 100
  0.6 24.2 %copy-start.5 = (s32[1,1,8]{2,1,0:T(1,128)S(1)}, s32[1,1,8]{2,1,0:T(1,128)}, u32[]{:S(2)}) copy-start(s32[1,1,8]{2,1,0:T(1,128)} %param.12) | copy-start | bytes 100
  0.7 1.2 %copy-start = (bf16[16,256,128]{2,1,0:T(8,128)(2,1)S(1)}, bf16[16,256,128]{2,1,0:T(8,128)(2,1)}, u32[]{:S(2)}) copy-start(bf16[16,256,128]{2,1,0:T(8,128)(2,1)} %phase_ref.1) | copy-start | bytes 3145732
  1.9 1.2 %copy-start.1 = (bf16[16,256,128]{2,1,0:T(8,128)(2,1)S(1)}, bf16[16,256,128]{2,1,0:T(8,128)(2,1)}, u32[]{:S(2)}) copy-start(bf16[16,256,128]{2,1,0:T(8,128)(2,1)} %absorb_ref.1) | copy-start | bytes 3145732
  3.1 21.7 %copy-start.2 = (bf16[1,1,8,256,256]{4,3,2,1,0:T(8,128)(2,1)S(1)}, bf16[1,1,8,256,256]{4,3,2,1,0:T(8,128)(2,1)}, u32[]{:S(2)}) copy-start(bf16[1,1,8,256,256]{4,3,2,1,0:T(8,128)(2,1)} %param.11) | copy-start | bytes 3145732
  3.1 21.7 %copy-start.3 = (f32[2,256,256]{2,1,0:T(8,128)S(1)}, f32[2,256,256]{2,1,0:T(8,128)}, u32[]{:S(2)}) copy-start(f32[2,256,256]{2,1,0:T(8,128)} %probe_ref.1) | copy-start | bytes 1572868
  3.1 21.7 %copy-start.4 = (bf16[2,256,256]{2,1,0:T(8,128)(2,1)S(1)}, bf16[2,256,256]{2,1,0:T(8,128)(2,1)}, u32[]{:S(2)}) copy-start(bf16[2,256,256]{2,1,0:T(8,128)(2,1)} %constant.13.table_ref) | copy-start | bytes 786436

commit v4 on v3

--- a/solution.py
+++ b/solution.py
@@ -221,12 +221,6 @@
     def _():
         greet(barrier, row=i + 1)
 
-    pl.semaphore_wait(
-        barrier,
-        beams + has_out.astype(jnp.int32) + above.astype(jnp.int32) + below.astype(jnp.int32),
-    )
-
-    sums = []
     for o in order:
         for p in range(2):
             loads[o, p].wait()
@@ -234,13 +228,17 @@
             for d in range(1, phase_ref.shape[0]):
                 total = total + vol[o, p, d].astype(jnp.float32)
             part[o, p] = total
-        if o:
-            copy = remote(
-                part.at[o], inbox.at[o], sum_send.at[o], sum_recv.at[o],
-                beam=lax.rem(b + o, beams),
-            )
-            copy.start()
-            sums.append(copy)
+    pl.semaphore_wait(
+        barrier,
+        beams + has_out.astype(jnp.int32) + above.astype(jnp.int32) + below.astype(jnp.int32),
+    )
+    sums = []
+    for o in order[:-1]:
+        copy = remote(
+            part.at[o], inbox.at[o], sum_send.at[o], sum_recv.at[o], beam=lax.rem(b + o, beams)
+        )
+        copy.start()
+        sums.append(copy)
     for copy in sums:
         copy.wait_recv()
     phase, absorb = part[0, 0], part[0, 1]
@@ -260,64 +258,99 @@
     t_ref[1, 1, mine, :] = ti
     m0 = top + b
     waits = []
-    ring = []
-    for o in [1, *range(3, beams), *range(2, min(3, beams))]:
-        copy = remote(
-            cell(1, m0), cell(1, m0), beam_send.at[o], t_recv.at[1, m0],
-            beam=lax.rem(b + o, beams),
-        )
-        copy.start()
-        waits.append((None, copy))
-        ring.append(o)
-
-    def sideways(m, slot, alive):
-        near = remote(
-            cell(1, m), cell(2 * c, m), near_send.at[slot], t_recv.at[2 * c, m], col_1=1 - c
-        )
-        far = remote(
-            cell(1, m), cell(2 - 2 * c, m), out_send.at[slot], t_recv.at[2 - 2 * c, m],
-            col_0=out_z, col_1=1 - c,
-        )
-        for copy, check in ((near, alive), (far, has_out if alive is None else has_out & alive)):
-            if check is None:
-                copy.start()
-            else:
-                pl.when(check)(copy.start)
-            waits.append((check, copy))
-
-    def arrived(k, m):
-        remote(cell(1, m), cell(k, m), near_send.at[0], t_recv.at[k, m], col_1=1 - c).wait_recv()
-
-    for slot, o in enumerate([0, *ring]):
+
+    def send(copy, check=None):
+        if check is None:
+            copy.start()
+        else:
+            pl.when(check)(copy.start)
+        waits.append((check, copy))
+
+    def arrived(k, m, check=None):
+        wait = remote(cell(1, m), cell(k, m), near_send.at[0], t_recv.at[k, m], col_1=1 - c).wait_recv
+        if check is None:
+            wait()
+        else:
+            pl.when(check)(wait)
+
+    def both(first, second):
+        return second if first is None else first & second
+
+    def to_sibling(m, slot, check=None):
+        send(
+            remote(
+                cell(1, m), cell(2 * c, m), near_send.at[slot], t_recv.at[2 * c, m], col_1=1 - c
+            ),
+            check,
+        )
+
+    def to_outer(m, slot, check=None):
+        send(
+            remote(
+                cell(1, m), cell(2 - 2 * c, m), out_send.at[slot], t_recv.at[2 - 2 * c, m],
+                col_0=out_z, col_1=1 - c,
+            ),
+            both(check, has_out),
+        )
+
+    def quarter(o):
         q = lax.rem(b + o, beams)
-        m = top + q
+        upper = q // top
+        rim = q - top + (1 - upper) * blocks
+        goal, source = i - 1 + 2 * upper, i + 1 - 2 * upper
+        return top + q, rim, goal, (goal >= 0) & (goal < rows_n), (source >= 0) & (source < rows_n)
+
+    def to_row(o, k, slot, check=None):
+        m, rim, goal, alive, _ = quarter(o)
+        send(
+            remote(cell(k, m), cell(k, rim), row_send.at[slot], t_recv.at[k, rim], row=goal),
+            both(check, alive),
+        )
+
+    ring = [1, *range(3, beams), *range(2, min(3, beams))]
+    by_row = {0, 2}
+    for o in ring:
+        send(
+            remote(
+                cell(1, m0), cell(1, m0), beam_send.at[o], t_recv.at[1, m0],
+                beam=lax.rem(b + o, beams),
+            )
+        )
+
+    def spread_tile(o):
+        m = quarter(o)[0]
         if o:
             arrived(1, m)
-        upper = q // top
-        goal = i - 1 + 2 * upper
-        copy = remote(
-            cell(1, m),
-            cell(1, q - top + (1 - upper) * blocks),
-            row_send.at[slot],
-            t_recv.at[1, q - top + (1 - upper) * blocks],
-            row=goal,
-        )
-        alive = (goal >= 0) & (goal < rows_n)
-        pl.when(alive)(copy.start)
-        waits.append((alive, copy))
-        sideways(m, slot, None)
-    for at in range(top):
-        for m, alive in ((at, above), (top + beams + at, below)):
-            pl.when(alive)(functools.partial(arrived, 1, m))
-            sideways(m, beams + (m if m < top else m - beams), alive)
-    for m in range(blocks):
-        alive = above if m < top else below if m >= top + beams else None
-        if alive is None:
-            arrived(2 - 2 * c, m)
-            pl.when(has_out)(functools.partial(arrived, 2 * c, m))
-        else:
-            pl.when(alive)(functools.partial(arrived, 2 - 2 * c, m))
-            pl.when(alive & has_out)(functools.partial(arrived, 2 * c, m))
+        to_outer(m, o)
+        to_row(o, 1, o)
+        to_sibling(m, o)
+
+    def spread_rim(o):
+        _, rim, _, _, alive = quarter(o)
+        arrived(1, rim, alive)
+        if o not in by_row:
+            to_outer(rim, beams + o, alive)
+        to_sibling(rim, beams + o, alive)
+
+    def spread_corner(o):
+        m = quarter(o)[0]
+        arrived(2 * c, m, has_out)
+        if o in by_row:
+            to_row(o, 2 * c, beams + o, has_out)
+
+    events = [(spread_tile, 0), (spread_tile, ring[0]), (spread_corner, 0), (spread_rim, 0)]
+    for now, later in zip(ring, ring[1:] + [None]):
+        if later is not None:
+            events.append((spread_tile, later))
+        events.append((spread_corner, now))
+        events.append((spread_rim, now))
+    for event, o in events:
+        event(o)
+    for o in range(beams):
+        m, rim, _, _, alive = quarter(o)
+        arrived(2 - 2 * c, m)
+        arrived(2 - 2 * c, rim, alive)
+        arrived(2 * c, rim, alive & has_out)
     for copy in sums:
         copy.wait_send()
     for alive, copy in waits:
@@ -360,23 +393,25 @@
             pltpu.SemaphoreType.DMA((beams,)),
             pltpu.SemaphoreType.DMA((2 * beams,)),
             pltpu.SemaphoreType.DMA((2 * beams,)),
-            pltpu.SemaphoreType.DMA((beams,)),
+            pltpu.SemaphoreType.DMA((2 * beams,)),
             pltpu.SemaphoreType.DMA((3, 2 * beams)),
         ],
         compiler_params=pltpu.CompilerParams(
             collective_id=0, has_side_effects=True, vmem_limit_bytes=VMEM_LIMIT
         ),
         name="spread",
-    )(phase_volume, absorb_volume)
+    )(
+        pltpu.with_memory_space_constraint(phase_volume, pltpu.HBM),
+        pltpu.with_memory_space_constraint(absorb_volume, pltpu.HBM),
+    )
 
 
 def fold_kernel(
     scale, canvas_ref, own_ref, probe_ref, misfit_ref,
     grad, probe_out, sums_ref,
-    sib_in, out_in, acc, row_in, q_in, p_in, p_sum, x_in, z_in, n_xy, n_zc,
-    sib_send, sib_recv, out_send, out_recv, row_send, row_recv, q_send, q_recv,
-    g_send, g_recv, p_send, p_recv, x_send, x_recv, z_send, z_recv, y_send, y_recv,
-    n_send, n_recv, m_send, m_recv,
+    sib_in, out_in, acc, corner_in, corner, row_in, q_in, p_in, p_sum, y_in, x_in, z_in, n_xy, n_zc,
+    sib_send, sib_recv, out_send, out_recv, corner_send, corner_recv, row_send, row_recv,
+    pair_send, pair_recv, group_send, group_recv,
 ):
     beams, rows_n, deep_n, cores = sizes()
     b, i, z, c = places()
@@ -386,10 +421,9 @@
     tall = 2 * rows
     plane = beams * rows_n
     across = deep_n * cores
-    share = p_sum.shape[0] // plane
+    out_z = z - 1 + 2 * c
     me_xy = b * rows_n + i
     me_zc = z * cores + c
-    out_z = z - 1 + 2 * c
     has_out = (out_z >= 0) & (out_z < deep_n)
     above, below = i > 0, i < rows_n - 1
     finish = []
@@ -408,6 +442,13 @@
     def peer_zc(o):
         return dict(col_0=lax.rem(z + o // cores, deep_n), col_1=lax.rem(c + o % cores, cores))
 
+    def group(g, copies, like):
+        for src, dst, where in copies:
+            remote(src, dst, group_send.at[g], group_recv.at[g], **where).start()
+        everything = remote(like, like, group_send.at[g], group_recv.at[g], col_1=1 - c)
+        finish.append((None, everything))
+        return everything
+
     barrier = pltpu.get_barrier_semaphore()
     for o in range(1, plane):
         greet(barrier, **peer_xy(o))
@@ -415,21 +456,13 @@
         greet(barrier, **peer_zc(o))
     pl.semaphore_wait(barrier, plane + across - 2)
 
-    half_copy = go(remote(probe_ref.at[1 - c], p_in, p_send.at[0], p_recv.at[0], col_1=1 - c))
-    spans = [(0, half, above), (tall - half, half, below), (half, rows, None)]
-    near, far = [], []
-    for e, (start, size, alive) in enumerate(spans):
-        where = pl.ds(start, size)
-        far.append(
-            go(
-                remote(
-                    canvas_ref.at[:, 2 * c, where, :], out_in.at[:, where, :],
-                    out_send.at[e], out_recv.at[e], col_0=out_z, col_1=1 - c,
-                ),
-                has_out if alive is None else has_out & alive,
-            )
-        )
-        near.append(
+    middle = pl.ds(half, rows)
+    rims = [(pl.ds(0, half), above, i - 1), (pl.ds(tall - half, half), below, i + 1)]
+    outer = dict(col_0=out_z, col_1=1 - c)
+    half_copy = go(remote(probe_ref.at[1 - c], p_in, pair_send.at[0], pair_recv.at[0], col_1=1 - c))
+    far_rims, near_rims, corners = [], [], []
+    for e, (where, alive, goal) in enumerate(rims):
+        near_rims.append(
             go(
                 remote(
                     canvas_ref.at[:, 2 - 2 * c, where, :], sib_in.at[:, where, :],
@@ -438,87 +471,158 @@
                 alive,
             )
         )
-    half_copy.wait_recv()
-    p_sum[...] = probe_ref[c] + p_in[...]
-    parts = []
-    for o in range(1, plane):
-        peer = peer_xy(o)
-        there = pl.multiple_of((peer["beam"] * rows_n + peer["row"]) * share, share)
-        parts.append(
+        far_rims.append(
             go(
                 remote(
-                    p_sum.at[pl.ds(there, share), :], x_in.at[o], x_send.at[o], x_recv.at[o], **peer
-                )
+                    canvas_ref.at[0, 2 * c, where, :], out_in.at[0, where, :],
+                    out_send.at[e], out_recv.at[e], **outer,
+                ),
+                has_out & alive,
             )
         )
-
-    def merge(e):
-        start, size, _ = spans[e]
-        where = pl.ds(start, size)
-        near[e].wait_recv()
-        acc[:, where, :] = canvas_ref[:, 1, where, :] + sib_in[:, where, :]
-
-        @pl.when(has_out)
-        def _():
-            far[e].wait_recv()
-            acc[:, where, :] += out_in[:, where, :]
-
-    rims = []
-    for e, goal in ((0, i - 1), (1, i + 1)):
-        start, size, alive = spans[e]
-        pl.when(alive)(functools.partial(merge, e))
-        rims.append(
+        corners.append(
             go(
                 remote(
-                    acc.at[:, pl.ds(start, size), :], row_in.at[e],
-                    row_send.at[e], row_recv.at[e], row=goal,
+                    canvas_ref.at[1, 2 * c, where, :], corner_in.at[e],
+                    corner_send.at[e], corner_recv.at[e], row=goal,
+                ),
+                has_out & alive,
+            )
+        )
+    far_first = go(
+        remote(
+            canvas_ref.at[0, 2 * c, middle, :], out_in.at[0, middle, :],
+            out_send.at[2], out_recv.at[2], **outer,
+        ),
+        has_out,
+    )
+    near_middle = go(
+        remote(
+            canvas_ref.at[:, 2 - 2 * c, middle, :], sib_in.at[:, middle, :],
+            sib_send.at[2], sib_recv.at[2], col_1=1 - c,
+        )
+    )
+    half_copy.wait_recv()
+    p_sum[...] = (probe_ref[c] + p_in[...]).reshape(p_sum.shape)
+    parts = group(
+        0,
+        [
+            (p_sum.at[:, lax.rem(b + o, beams)], y_in.at[o], dict(beam=lax.rem(b + o, beams)))
+            for o in range(1, beams)
+        ],
+        y_in.at[pl.ds(1, beams - 1)],
+    )
+
+    edges = {}
+    for p in (1, 0):
+        for e, (where, alive, goal) in enumerate(rims):
+
+            def rim(p=p, e=e, where=where):
+                if p == 1:
+                    near_rims[e].wait_recv()
+                acc[p, where, :] = canvas_ref[p, 1, where, :] + sib_in[p, where, :]
+                if p == 0:
+
+                    @pl.when(has_out)
+                    def _():
+                        far_rims[e].wait_recv()
+                        acc[0, where, :] += out_in[0, where, :]
+
+            pl.when(alive)(rim)
+            edges[p, e] = go(
+                remote(
+                    acc.at[p, where, :], row_in.at[p, e],
+                    row_send.at[p, e], row_recv.at[p, e], row=goal,
                 ),
                 alive,
             )
-        )
-    merge(2)
-
-    @pl.when(below)
+    low, high = pl.ds(half, half), pl.ds(rows, half)
+
+    @pl.when(has_out)
     def _():
-        rims[0].wait_recv()
-        acc[:, pl.ds(rows, half), :] += row_in[0]
-
-    @pl.when(above)
+        corner[...] = canvas_ref[1, 2 * c, middle, :]
+
+        @pl.when(below)
+        def _():
+            corners[0].wait_recv()
+            corner[pl.ds(half, half), :] += corner_in[0]
+
+        @pl.when(above)
+        def _():
+            corners[1].wait_recv()
+            corner[pl.ds(0, half), :] += corner_in[1]
+
+    far_second = go(
+        remote(
+            corner, out_in.at[1, middle, :], out_send.at[3], out_recv.at[3], **outer
+        ),
+        has_out,
+    )
+    near_middle.wait_recv()
+    acc[:, middle, :] = canvas_ref[:, 1, middle, :] + sib_in[:, middle, :]
+    parts.wait_recv()
+    block = p_sum[:, b]
+    for o in range(1, beams):
+        block = block + y_in[o]
+    y_in[0] = block
+    parts = group(
+        1,
+        [
+            (y_in.at[0, lax.rem(i + o, rows_n)], x_in.at[o], dict(row=lax.rem(i + o, rows_n)))
+            for o in range(1, rows_n)
+        ],
+        x_in.at[pl.ds(1, rows_n - 1)],
+    )
+
+    @pl.when(has_out)
     def _():
-        rims[1].wait_recv()
-        acc[:, pl.ds(half, half), :] += row_in[1]
-
-    quarters = []
-    for o in range(1, beams):
-        q = lax.rem(b + o, beams)
-        there = pl.multiple_of(half + q * h, h)
-        quarters.append(
-            go(
-                remote(
-                    acc.at[:, pl.ds(there, h), :], q_in.at[o], q_send.at[o], q_recv.at[o], beam=q
-                )
+        far_first.wait_recv()
+        acc[0, middle, :] += out_in[0, middle, :]
+
+    for p in (1, 0):
+        for e, (alive, where) in enumerate(((below, high), (above, low))):
+
+            def settle(p=p, e=e, where=where):
+                edges[p, e].wait_recv()
+                acc[p, where, :] += row_in[p, e]
+
+            pl.when(alive)(settle)
+
+    @pl.when(has_out)
+    def _():
+        far_second.wait_recv()
+        acc[1, middle, :] += out_in[1, middle, :]
+
+    quarters = group(
+        2,
+        [
+            (
+                acc.at[:, pl.ds(pl.multiple_of(half + lax.rem(b + o, beams) * h, h), h), :],
+                q_in.at[o],
+                dict(beam=lax.rem(b + o, beams)),
             )
-        )
-    total = p_sum[pl.ds(pl.multiple_of(me_xy * share, share), share), :]
-    for o in range(1, plane):
-        parts[o - 1].wait_recv()
+            for o in [*range(2, beams), 1]
+        ],
+        q_in.at[pl.ds(1, beams - 1)],
+    )
+    parts.wait_recv()
+    total = y_in[0, i]
+    for o in range(1, rows_n):
         total = total + x_in[o]
     z_in[z] = total
-    levels = []
-    for o in range(1, deep_n):
-        levels.append(
-            go(
-                remote(
-                    z_in.at[z], z_in.at[z], z_send.at[o], z_recv.at[o],
-                    col_0=lax.rem(z + o, deep_n),
-                )
-            )
-        )
+    levels = group(
+        3,
+        [
+            (z_in.at[z], z_in.at[z], dict(col_0=lax.rem(z + o, deep_n)))
+            for o in sorted(range(1, deep_n), key=lambda o: -min(o, deep_n - o))
+        ],
+        z_in.at[pl.ds(0, deep_n - 1)],
+    )
 
     mine = pl.ds(pl.multiple_of(half + b * h, h), h)
+    quarters.wait_recv()
     cr, ci = acc[0, mine, :], acc[1, mine, :]
     for o in range(1, beams):
-        quarters[o - 1].wait_recv()
         cr = cr + q_in[o, 0]
         ci = ci + q_in[o, 1]
     tr, ti = own_ref[0], own_ref[1]
@@ -535,70 +639,66 @@
         squares + pltpu.roll(squares, LANES // 2, 1),
         misfits + pltpu.roll(misfits, LANES // 2, 1),
     )
-    norms = []
-    for o in range(1, plane):
-        norms.append(
-            go(
-                remote(
-                    n_xy.at[me_xy], n_xy.at[me_xy], n_send.at[o], n_recv.at[o], **peer_xy(o)
-                )
-            )
-        )
-    grads = []
-    for o in range(1, beams):
-        grads.append(
-            go(
-                remote(
-                    grad.at[:, home, :], grad.at[:, home, :], g_send.at[o], g_recv.at[o],
-                    beam=lax.rem(b + o, beams),
-                )
-            )
-        )
-
-    for copy in levels:
-        copy.wait_recv()
+    norms = group(
+        4,
+        [(n_xy.at[me_xy], n_xy.at[me_xy], peer_xy(o)) for o in range(1, plane)],
+        n_xy.at[pl.ds(0, plane - 1)],
+    )
+
+    levels.wait_recv()
     total = z_in[0]
     for k in range(1, deep_n):
         total = total + z_in[k]
-    piece = pl.ds(pl.multiple_of(me_xy * share, share), share)
-    probe_out[c, piece, :] = total * scale
-    spreads = []
-    for o in range(1, plane):
-        spreads.append(
-            go(
-                remote(
-                    probe_out.at[c, piece, :], probe_out.at[c, piece, :],
-                    y_send.at[o], y_recv.at[o], **peer_xy(o),
-                )
-            )
-        )
-
-    for copy in norms:
-        copy.wait_recv()
+    probe_out[c, i, b] = total * scale
+    spreads = group(
+        5,
+        [
+            (probe_out.at[c, i, b], probe_out.at[c, i, b], dict(beam=lax.rem(b + o, beams)))
+            for o in range(1, beams)
+        ],
+        z_in.at[pl.ds(0, beams - 1)] if beams <= deep_n else y_in.at[0, pl.ds(0, beams - 1)],
+    )
+    grads = group(
+        6,
+        [
+            (grad.at[:, home, :], grad.at[:, home, :], dict(beam=lax.rem(b + o, beams)))
+            for o in range(1, beams)
+        ],
+        q_in.at[pl.ds(1, beams - 1)],
+    )
+
+    norms.wait_recv()
     pair = n_xy[0]
     for k in range(1, plane):
         pair = pair + n_xy[k]
     n_zc[me_zc] = pair
-    norms = []
-    for o in range(1, across):
-        norms.append(
-            go(
-                remote(
-                    n_zc.at[me_zc], n_zc.at[me_zc], m_send.at[o], m_recv.at[o], **peer_zc(o)
-                )
-            )
-        )
-    for copy in spreads:
-        copy.wait_recv()
-    last = go(remote(probe_out.at[c], probe_out.at[c], p_send.at[1], p_recv.at[1], col_1=1 - c))
-    for copy in norms:
-        copy.wait_recv()
+    norms = group(
+        7,
+        [
+            (n_zc.at[me_zc], n_zc.at[me_zc], peer_zc(o))
+            for o in sorted(range(1, across), key=lambda o: -min(o // cores, deep_n - o // cores))
+        ],
+        n_zc.at[pl.ds(0, across - 1)],
+    )
+    spreads.wait_recv()
+    spreads = group(
+        8,
+        [
+            (probe_out.at[c, i], probe_out.at[c, i], dict(row=lax.rem(i + o, rows_n)))
+            for o in range(1, rows_n)
+        ],
+        y_in.at[pl.ds(0, rows_n - 1)] if rows_n == beams else probe_out.at[0, pl.ds(0, rows_n - 1)],
+    )
+    spreads.wait_recv()
+    last = go(
+        remote(probe_out.at[c], probe_out.at[c], pair_send.at[1], pair_recv.at[1], col_1=1 - c)
+    )
+    norms.wait_recv()
     pair = n_zc[0]
     for k in range(1, across):
         pair = pair + n_zc[k]
     sums_ref[...] = pair
-    for copy in grads:
-        copy.wait_recv()
+    grads.wait_recv()
     last.wait_recv()
     for check, copy in finish:
         if check is None:
@@ -614,14 +714,14 @@
     h = rows // beams
     n = probe_sum.shape[1]
     plane, across = beams * rows_n, deep_n * cores
+    share = n // plane
     f32 = functools.partial(pltpu.VMEM, dtype=jnp.float32)
-    sems = [3, 3, 3, 3, 2, 2, beams, beams, beams, beams, 2, 2, plane, plane, deep_n, deep_n]
-    sems += [plane, plane, plane, plane, across, across]
-    return pl.pallas_call(
+    sems = [(3,), (3,), (4,), (4,), (2,), (2,), (2, 2), (2, 2), (2,), (2,), (9,), (9,)]
+    grad, probe_total, sums = pl.pallas_call(
         functools.partial(fold_kernel, 1.0 / positions),
         out_shape=[
             jax.ShapeDtypeStruct((2, rows, lanes), jnp.float32),
-            jax.ShapeDtypeStruct(probe_sum.shape, jnp.float32),
+            jax.ShapeDtypeStruct((2, rows_n, beams, share, n), jnp.float32),
             jax.ShapeDtypeStruct((1, LANES), jnp.float32),
         ],
         in_specs=[pl.BlockSpec(memory_space=pltpu.VMEM)] * 4,
@@ -630,21 +730,25 @@
             f32((2, tall, lanes)),
             f32((2, tall, lanes)),
             f32((2, tall, lanes)),
+            f32((2, rows // 2, lanes)),
+            f32((rows, lanes)),
             f32((2, 2, rows // 2, lanes)),
             f32((beams, 2, h, lanes)),
             f32((n, n)),
-            f32((n, n)),
-            f32((plane, n // plane, n)),
-            f32((deep_n, n // plane, n)),
+            f32((rows_n, beams, share, n)),
+            f32((beams, rows_n, share, n)),
+            f32((rows_n, share, n)),
+            f32((deep_n, share, n)),
             f32((plane, 1, LANES)),
             f32((across, 1, LANES)),
-            *[pltpu.SemaphoreType.DMA((count,)) for count in sems],
+            *[pltpu.SemaphoreType.DMA(count) for count in sems],
         ],
         compiler_params=pltpu.CompilerParams(
             collective_id=1, has_side_effects=True, vmem_limit_bytes=VMEM_LIMIT
         ),
         name="fold",
     )(canvas, own, probe_sum, misfit)
+    return grad, probe_total.reshape(probe_sum.shape), sums
 
 
 def finish_kernel(entries, terms, grad_ref, probe_ref, sums_ref, step_ref, probe_out, loss_ref):

time: 75.1 us -> 74.2 us (0.988)
  local copies, waits for them, and re-layouts: 2.47 us -> 0.02 us
  Pallas kernels: 71.6 us -> 73.4 us
    unnamed x14 -> x10, local copies, waits for them, and re-layouts: 2.47 us -> 0.02 us
    pallas_call x1, Pallas kernels: 21.7 us -> 23.3 us  [transmission(): pl.pallas_call(spread_kernel, out_shape=[jax.ShapeDtypeStruct((2, 3, 2 *...]
where the time goes in v4:
time: 74.2 us; the launch traced here: 74.1 us
  Pallas kernels  73.4 us (99%)
    pallas_call x1, Pallas kernels, folded(): pl.pallas_call(functools.partial(fold_kernel, 1.0 / positions), out_shape...  36.1 us
    pallas_call x1, Pallas kernels, transmission(): pl.pallas_call(spread_kernel, out_shape=[jax.ShapeDtypeStruct((2, 3, 2 *...  23.3 us
    pallas_call x1, Pallas kernels, window_terms(): pl.pallas_call(window_kernel, grid_spec=grid_spec, out_shape=[jax.ShapeDt...  13 us

profile of v4, /device:TPU:1, one launch (start us, length us, event | category | flops | bytes accessed | tf_op | source)
XLA Modules:
  0.0 74.1 jit_solution(10271204029160371896)
XLA Ops:
  0.6 0.0 copy-start.2
  0.6 0.0 copy-start.4
  0.7 0.0 copy-start.3
  0.7 0.0 copy-start
  0.7 0.0 copy-start.1
  0.7 23.3 %spread.1 = (f32[2,3,512,128]{3,2,1,0:T(8,128)S(1)}, f32[2,64,128]{2,1,0:T(8,128)S(1)}) custom-call(bf16[16,256,128]{2,1,0:T(8,128)(2,1)} %phase_ref.1, bf16[16,256,128]{2,1,0:T(8,128)(2,1)} %absorb_ref.1), custom_call_target="tpu_custom_call" | custom-call | tf_op jit(solution)/shard_map/spread/pallas_call | solution.py:378
  24.0 0.0 copy-done.2
  24.0 0.0 copy-done.4
  24.1 0.0 copy-done.3
  24.1 0.0 copy-done
  24.1 0.0 copy-done.1
  24.1 13.0 %windows.1 = (f32[2,3,512,128]{3,2,1,0:T(8,128)S(1)}, f32[2,256,256]{2,1,0:T(8,128)S(1)}, f32[8,128]{1,0:T(8,128)S(1)}) custom-call(s32[8]{0:T(128)S(1)} %bitcast.7, s32[8]{0:T(128)S(1)} %bitcast.8, f32[2,3,512,128]{3,2,1,0:T(8,128)S(1)} %get-tuple-element.14.t_ref, f32[2,256,256]{2,1,0:T(8,128)S(1)} %copy-done.1, bf16[8,256,256]{2,1,0:T(8,128)(2,1)S(1)} %bitcast.5, ...), custom_call_target="tpu_custom_call" | custom-call | tf_op jit(solution)/shard_map/windows/pallas_call | solution.py:147
  37.1 36.1 %fold.1 = (f32[2,256,128]{2,1,0:T(8,128)S(1)}, f32[2,4,4,16,256]{4,3,2,1,0:T(8,128)S(1)}, f32[1,128]{1,0:T(1,128)S(1)}) custom-call(f32[2,3,512,128]{3,2,1,0:T(8,128)S(1)} %get-tuple-element.15.canvas_ref, f32[2,64,128]{2,1,0:T(8,128)S(1)} %get-tuple-element.16.own_ref, f32[2,256,256]{2,1,0:T(8,128)S(1)} %get-tuple-element.17.probe_ref, ...), custom_call_target="tpu_custom_call" | custom-call | tf_op jit(solution)/shard_map/fold/pallas_call | solution.py:720
  73.2 0.9 %finish.1 = (f32[2,256,128]{2,1,0:T(8,128)}, f32[2,256,256]{2,1,0:T(8,128)}, f32[1,1]{1,0:T(1,128)}) custom-call(f32[2,256,128]{2,1,0:T(8,128)S(1)} %get-tuple-element.19.grad_ref, f32[2,256,256]{2,1,0:T(8,128)S(1)} %bitcast.6, f32[1,128]{1,0:T(1,128)S(1)} %get-tuple-element.21.sums_ref), custom_call_target="tpu_custom_call" | custom-call | tf_op jit(solution)/shard_map/finish/pallas_call | solution.py:767
Async XLA Ops:
  0.6 23.4 %copy-start.2 = (bf16[2,256,256]{2,1,0:T(8,128)(2,1)S(1)}, bf16[2,256,256]{2,1,0:T(8,128)(2,1)}, u32[]{:S(2)}) copy-start(bf16[2,256,256]{2,1,0:T(8,128)(2,1)} %constant.13.table_ref) | copy-start | bytes 786436
  0.6 23.4 %copy-start.4 = (s32[1,1,8]{2,1,0:T(1,128)S(1)}, s32[1,1,8]{2,1,0:T(1,128)}, u32[]{:S(2)}) copy-start(s32[1,1,8]{2,1,0:T(1,128)} %param.13) | copy-start | bytes 100
  0.7 23.4 %copy-start.3 = (s32[1,1,8]{2,1,0:T(1,128)S(1)}, s32[1,1,8]{2,1,0:T(1,128)}, u32[]{:S(2)}) copy-start(s32[1,1,8]{2,1,0:T(1,128)} %param.12) | copy-start | bytes 100
  0.7 23.4 %copy-start = (bf16[1,1,8,256,256]{4,3,2,1,0:T(8,128)(2,1)S(1)}, bf16[1,1,8,256,256]{4,3,2,1,0:T(8,128)(2,1)}, u32[]{:S(2)}) copy-start(bf16[1,1,8,256,256]{4,3,2,1,0:T(8,128)(2,1)} %param.11) | copy-start | bytes 3145732
  0.7 23.4 %copy-start.1 = (f32[2,256,256]{2,1,0:T(8,128)S(1)}, f32[2,256,256]{2,1,0:T(8,128)}, u32[]{:S(2)}) copy-start(f32[2,256,256]{2,1,0:T(8,128)} %probe_ref.1) | copy-start | bytes 1572868

commit v5 on v4

--- a/solution.py
+++ b/solution.py
@@ -14,6 +14,7 @@
 MESH = pl.DeviceIdType.MESH
 LANES = 128
 CHUNK = 128
+BATCH = 4
 VMEM_LIMIT = 20 << 20
 
 
@@ -35,6 +36,7 @@
 ):
     step = pl.program_id(0)
     n = probe_ref.shape[1]
+    batch = amp_ref.shape[0]
 
     @pl.when(step == 0)
     def _():
@@ -52,81 +54,99 @@
         probe_sum_ref[...] = jnp.zeros_like(probe_sum_ref)
         misfit_ref[...] = jnp.zeros_like(misfit_ref)
 
-    row = rows_ref[step]
-    col = cols_ref[step]
-    turn = lax.rem(LANES - col, LANES)
     lane = lax.broadcasted_iota(jnp.int32, (32, LANES), 1)
-    near = lane < LANES - col
-    for at in range(0, n, 32):
-        here = pl.ds(at, 32)
-        pieces = []
+
+    def cut_windows(j):
+        row, col = rows_ref[step * batch + j], cols_ref[step * batch + j]
+        turn = lax.rem(LANES - col, LANES)
+        near = lane < LANES - col
+        for at in range(0, n, 32):
+            here = pl.ds(at, 32)
+            pieces = []
+            for part in range(2):
+                turned = [
+                    pltpu.roll(t_ref[part, k, pl.ds(row + at, 32), :], turn, 1)
+                    for k in range(3)
+                ]
+                pieces.append([jnp.where(near, turned[k], turned[k + 1]) for k in range(2)])
+            for k in range(2):
+                lanes = pl.ds(k * LANES, LANES)
+                tr, ti = pieces[0][k], pieces[1][k]
+                cut[j, 0, here, lanes] = tr
+                cut[j, 1, here, lanes] = ti
+                pr = probe_ref[0, here, lanes]
+                pi = probe_ref[1, here, lanes]
+                psi[j, here, lanes] = (pr * tr - pi * ti).astype(jnp.bfloat16)
+                psi[j, pl.ds(n + at, 32), lanes] = (pr * ti + pi * tr).astype(jnp.bfloat16)
+
+    def to_half(j):
         for part in range(2):
-            turned = [
-                pltpu.roll(t_ref[part, k, pl.ds(row + at, 32), :], turn, 1) for k in range(3)
-            ]
-            pieces.append([jnp.where(near, turned[k], turned[k + 1]) for k in range(2)])
-        for k in range(2):
-            lanes = pl.ds(k * LANES, LANES)
-            tr, ti = pieces[0][k], pieces[1][k]
-            cut[0, here, lanes] = tr
-            cut[1, here, lanes] = ti
-            pr = probe_ref[0, here, lanes]
-            pi = probe_ref[1, here, lanes]
-            psi[here, lanes] = (pr * tr - pi * ti).astype(jnp.bfloat16)
-            psi[pl.ds(n + at, 32), lanes] = (pr * ti + pi * tr).astype(jnp.bfloat16)
-    for part in range(2):
-        half[:, part * n : (part + 1) * n] = jnp.dot(
-            fwd[part * n : (part + 1) * n, :], psi[...], preferred_element_type=jnp.float32
-        ).astype(jnp.bfloat16)
-    total = jnp.zeros((8, LANES), jnp.float32)
-    for at in range(0, n, CHUNK):
-        here = pl.ds(at, CHUNK)
-        far = jnp.dot(half[here, :], bwd[...], preferred_element_type=jnp.float32)
-        fr, fi = far[:, :n], far[:, n:]
-        amp = amp_ref[0, here, :].astype(jnp.float32)
-        power = fr * fr + fi * fi
-        inverse = lax.rsqrt(power)
-        modulus = jnp.where(power > 0.0, power * inverse, 0.0)
-        off = modulus - amp
-        square = off * off
-        total = total + jnp.sum(
-            (square[:, :LANES] + square[:, LANES:]).reshape(CHUNK // 8, 8, LANES), axis=0
-        )
-        ratio = 1.0 - amp * jnp.minimum(inverse, 2.0)
-        chi[here, :] = (fr * ratio).astype(jnp.bfloat16)
-        chi[pl.ds(n + at, CHUNK), :] = (fi * ratio).astype(jnp.bfloat16)
-    misfit_ref[...] += total
-    for part in range(2):
-        back[:, part * n : (part + 1) * n] = jnp.dot(
-            bwd[part * n : (part + 1) * n, :], chi[...], preferred_element_type=jnp.float32
-        ).astype(jnp.bfloat16)
-    far_side = lax.broadcasted_iota(jnp.int32, (CHUNK, LANES), 1) >= col
-    for at in range(0, n, CHUNK):
-        here = pl.ds(at, CHUNK)
-        grad = jnp.dot(back[here, :], fwd[...], preferred_element_type=jnp.float32)
-        gr, gi = grad[:, :n], grad[:, n:]
-        tr, ti = cut[0, here, :], cut[1, here, :]
-        probe_sum_ref[0, here, :] += tr * gr + ti * gi
-        probe_sum_ref[1, here, :] += tr * gi - ti * gr
-        pr, pi = probe_ref[0, here, :], probe_ref[1, here, :]
-        for part, value in enumerate((pr * gr + pi * gi, pr * gi - pi * gr)):
-            first = pltpu.roll(value[:, :LANES], col, 1)
-            second = pltpu.roll(value[:, LANES:], col, 1)
-            there = pl.ds(row + at, CHUNK)
-            canvas_ref[part, 0, there, :] += jnp.where(far_side, first, 0.0)
-            canvas_ref[part, 1, there, :] += jnp.where(far_side, second, first)
-            canvas_ref[part, 2, there, :] += jnp.where(far_side, 0.0, second)
+            half[j, :, part * n : (part + 1) * n] = jnp.dot(
+                fwd[part * n : (part + 1) * n, :], psi[j], preferred_element_type=jnp.float32
+            ).astype(jnp.bfloat16)
+
+    def to_far(j):
+        total = jnp.zeros((8, LANES), jnp.float32)
+        for at in range(0, n, CHUNK):
+            here = pl.ds(at, CHUNK)
+            far = jnp.dot(half[j, here, :], bwd[...], preferred_element_type=jnp.float32)
+            fr, fi = far[:, :n], far[:, n:]
+            amp = amp_ref[j, here, :].astype(jnp.float32)
+            power = fr * fr + fi * fi
+            inverse = lax.rsqrt(power)
+            modulus = jnp.where(power > 0.0, power * inverse, 0.0)
+            off = modulus - amp
+            square = off * off
+            total = total + jnp.sum(
+                (square[:, :LANES] + square[:, LANES:]).reshape(CHUNK // 8, 8, LANES), axis=0
+            )
+            ratio = 1.0 - amp * jnp.minimum(inverse, 2.0)
+            chi[j, here, :] = (fr * ratio).astype(jnp.bfloat16)
+            chi[j, pl.ds(n + at, CHUNK), :] = (fi * ratio).astype(jnp.bfloat16)
+        misfit_ref[...] += total
+
+    def to_back(j):
+        for part in range(2):
+            back[j, :, part * n : (part + 1) * n] = jnp.dot(
+                bwd[part * n : (part + 1) * n, :], chi[j], preferred_element_type=jnp.float32
+            ).astype(jnp.bfloat16)
+
+    def add_terms(j):
+        row, col = rows_ref[step * batch + j], cols_ref[step * batch + j]
+        far_side = lax.broadcasted_iota(jnp.int32, (CHUNK, LANES), 1) >= col
+        for at in range(0, n, CHUNK):
+            here = pl.ds(at, CHUNK)
+            grad = jnp.dot(back[j, here, :], fwd[...], preferred_element_type=jnp.float32)
+            gr, gi = grad[:, :n], grad[:, n:]
+            tr, ti = cut[j, 0, here, :], cut[j, 1, here, :]
+            probe_sum_ref[0, here, :] += tr * gr + ti * gi
+            probe_sum_ref[1, here, :] += tr * gi - ti * gr
+            pr, pi = probe_ref[0, here, :], probe_ref[1, here, :]
+            for part, value in enumerate((pr * gr + pi * gi, pr * gi - pi * gr)):
+                first = pltpu.roll(value[:, :LANES], col, 1)
+                second = pltpu.roll(value[:, LANES:], col, 1)
+                there = pl.ds(row + at, CHUNK)
+                canvas_ref[part, 0, there, :] += jnp.where(far_side, first, 0.0)
+                canvas_ref[part, 1, there, :] += jnp.where(far_side, second, first)
+                canvas_ref[part, 2, there, :] += jnp.where(far_side, 0.0, second)
+
+    steps = (cut_windows, to_half, to_far, to_back, add_terms)
+    for tick in range(batch + len(steps) - 1):
+        for at, stage in reversed(list(enumerate(steps))):
+            if 0 <= tick - at < batch:
+                stage(tick - at)
 
 
 def window_terms(t, probe, amplitudes, rows, cols):
     count, n, _ = amplitudes.shape
+    batch = max(size for size in (1, 2, BATCH) if count % size == 0)
     grid_spec = pltpu.PrefetchScalarGridSpec(
         num_scalar_prefetch=2,
-        grid=(count,),
+        grid=(count // batch,),
         in_specs=[
             pl.BlockSpec(t.shape, lambda s, *_: (0, 0, 0, 0)),
             pl.BlockSpec(probe.shape, lambda s, *_: (0, 0, 0)),
-            pl.BlockSpec((1, n, n), lambda s, *_: (s, 0, 0)),
+            pl.BlockSpec((batch, n, n), lambda s, *_: (s, 0, 0)),
             pl.BlockSpec((2, n, n), lambda s, *_: (0, 0, 0)),
         ],
         out_specs=[
@@ -137,11 +157,11 @@
         scratch_shapes=[
             pltpu.VMEM((2 * n, 2 * n), jnp.bfloat16),
             pltpu.VMEM((2 * n, 2 * n), jnp.bfloat16),
-            pltpu.VMEM((2, n, n), jnp.float32),
-            pltpu.VMEM((2 * n, n), jnp.bfloat16),
-            pltpu.VMEM((n, 2 * n), jnp.bfloat16),
-            pltpu.VMEM((2 * n, n), jnp.bfloat16),
-            pltpu.VMEM((n, 2 * n), jnp.bfloat16),
+            pltpu.VMEM((batch, 2, n, n), jnp.float32),
+            pltpu.VMEM((batch, 2 * n, n), jnp.bfloat16),
+            pltpu.VMEM((batch, n, 2 * n), jnp.bfloat16),
+            pltpu.VMEM((batch, 2 * n, n), jnp.bfloat16),
+            pltpu.VMEM((batch, n, 2 * n), jnp.bfloat16),
         ],
     )
     return pl.pallas_call(
@@ -152,7 +172,9 @@
             jax.ShapeDtypeStruct(probe.shape, jnp.float32),
             jax.ShapeDtypeStruct((8, LANES), jnp.float32),
         ],
-        compiler_params=pltpu.CompilerParams(dimension_semantics=("arbitrary",), vmem_limit_bytes=VMEM_LIMIT),
+        compiler_params=pltpu.CompilerParams(
+            dimension_semantics=("arbitrary",), vmem_limit_bytes=VMEM_LIMIT
+        ),
         name="windows",
     )(rows, cols, t, probe, amplitudes, jnp.stack(dft_tables(n)))
 
@@ -213,13 +235,15 @@
     def _():
         greet(barrier, col_0=out_z, col_1=1 - c)
 
-    @pl.when(above)
-    def _():
-        greet(barrier, row=i - 1)
-
-    @pl.when(below)
-    def _():
-        greet(barrier, row=i + 1)
+    for alive, row in ((above, i - 1), (below, i + 1)):
+
+        @pl.when(alive)
+        def _(row=row):
+            greet(barrier, row=row)
+
+        @pl.when(alive & has_out)
+        def _(row=row):
+            greet(barrier, row=row, col_0=out_z, col_1=1 - c)
 
     for o in order:
         for p in range(2):
@@ -228,10 +252,8 @@
             for d in range(1, phase_ref.shape[0]):
                 total = total + vol[o, p, d].astype(jnp.float32)
             part[o, p] = total
-    pl.semaphore_wait(
-        barrier,
-        beams + has_out.astype(jnp.int32) + above.astype(jnp.int32) + below.astype(jnp.int32),
-    )
+    ups, downs, outs = (flag.astype(jnp.int32) for flag in (above, below, has_out))
+    pl.semaphore_wait(barrier, beams + outs + (1 + outs) * (ups + downs))
     sums = []
     for o in order[:-1]:
         copy = remote(
@@ -308,7 +330,7 @@
         )
 
     ring = [1, *range(3, beams), *range(2, min(3, beams))]
-    by_row = {0, 2}
+    by_row, direct = {0}, {2}
     for o in ring:
         send(
             remote(
@@ -317,18 +339,30 @@
             )
         )
 
+    def to_diagonal(o, slot):
+        m, rim, goal, alive, _ = quarter(o)
+        send(
+            remote(
+                cell(1, m), cell(2 - 2 * c, rim), out_send.at[slot], t_recv.at[2 - 2 * c, rim],
+                row=goal, col_0=out_z, col_1=1 - c,
+            ),
+            alive & has_out,
+        )
+
     def spread_tile(o):
         m = quarter(o)[0]
         if o:
             arrived(1, m)
         to_outer(m, o)
         to_row(o, 1, o)
+        if o in direct:
+            to_diagonal(o, beams + o)
         to_sibling(m, o)
 
     def spread_rim(o):
         _, rim, _, _, alive = quarter(o)
         arrived(1, rim, alive)
-        if o not in by_row:
+        if o not in by_row and o not in direct:
             to_outer(rim, beams + o, alive)
         to_sibling(rim, beams + o, alive)
 
@@ -339,11 +373,9 @@
             to_row(o, 2 * c, beams + o, has_out)
 
     events = [(spread_tile, 0), (spread_tile, ring[0]), (spread_corner, 0), (spread_rim, 0)]
-    for now, later in zip(ring, ring[1:] + [None]):
-        if later is not None:
-            events.append((spread_tile, later))
-        events.append((spread_corner, now))
-        events.append((spread_rim, now))
+    events += [(spread_tile, o) for o in ring[1:]]
+    for o in ring:
+        events += [(spread_corner, o), (spread_rim, o)]
     for event, o in events:
         event(o)
     for o in range(beams):
@@ -409,7 +441,7 @@
 def fold_kernel(
     scale, canvas_ref, own_ref, probe_ref, misfit_ref,
     grad, probe_out, sums_ref,
-    sib_in, out_in, acc, corner_in, corner, row_in, q_in, p_in, p_sum, y_in, x_in, z_in, n_xy, n_zc,
+    sib_in, out_in, acc, corner_in, corner, row_in, q_in, p_in, p_sum, x_in, z_in, n_xy, n_zc,
     sib_send, sib_recv, out_send, out_recv, corner_send, corner_recv, row_send, row_recv,
     pair_send, pair_recv, group_send, group_recv,
 ):
@@ -504,14 +536,6 @@
     )
     half_copy.wait_recv()
     p_sum[...] = (probe_ref[c] + p_in[...]).reshape(p_sum.shape)
-    parts = group(
-        0,
-        [
-            (p_sum.at[:, lax.rem(b + o, beams)], y_in.at[o], dict(beam=lax.rem(b + o, beams)))
-            for o in range(1, beams)
-        ],
-        y_in.at[pl.ds(1, beams - 1)],
-    )
 
     edges = {}
     for p in (1, 0):
@@ -538,6 +562,16 @@
             )
     low, high = pl.ds(half, half), pl.ds(rows, half)
 
+    def at_xy(o):
+        peer = peer_xy(o)
+        return peer["beam"] * rows_n + peer["row"]
+
+    parts = group(
+        0,
+        [(p_sum.at[at_xy(o)], x_in.at[o], peer_xy(o)) for o in range(1, plane)],
+        x_in.at[pl.ds(1, plane - 1)],
+    )
+
     @pl.when(has_out)
     def _():
         corner[...] = canvas_ref[1, 2 * c, middle, :]
@@ -560,20 +594,6 @@
     )
     near_middle.wait_recv()
     acc[:, middle, :] = canvas_ref[:, 1, middle, :] + sib_in[:, middle, :]
-    parts.wait_recv()
-    block = p_sum[:, b]
-    for o in range(1, beams):
-        block = block + y_in[o]
-    y_in[0] = block
-    parts = group(
-        1,
-        [
-            (y_in.at[0, lax.rem(i + o, rows_n)], x_in.at[o], dict(row=lax.rem(i + o, rows_n)))
-            for o in range(1, rows_n)
-        ],
-        x_in.at[pl.ds(1, rows_n - 1)],
-    )
-
     @pl.when(has_out)
     def _():
         far_first.wait_recv()
@@ -606,8 +626,8 @@
         q_in.at[pl.ds(1, beams - 1)],
     )
     parts.wait_recv()
-    total = y_in[0, i]
-    for o in range(1, rows_n):
+    total = p_sum[me_xy]
+    for o in range(1, plane):
         total = total + x_in[o]
     z_in[z] = total
     levels = group(
@@ -649,14 +669,11 @@
     total = z_in[0]
     for k in range(1, deep_n):
         total = total + z_in[k]
-    probe_out[c, i, b] = total * scale
+    probe_out[c, me_xy] = total * scale
     spreads = group(
         5,
-        [
-            (probe_out.at[c, i, b], probe_out.at[c, i, b], dict(beam=lax.rem(b + o, beams)))
-            for o in range(1, beams)
-        ],
-        z_in.at[pl.ds(0, beams - 1)] if beams <= deep_n else y_in.at[0, pl.ds(0, beams - 1)],
+        [(probe_out.at[c, me_xy], probe_out.at[c, me_xy], peer_xy(o)) for o in range(1, plane)],
+        x_in.at[pl.ds(1, plane - 1)],
     )
     grads = group(
         6,
@@ -679,15 +696,6 @@
             for o in sorted(range(1, across), key=lambda o: -min(o // cores, deep_n - o // cores))
         ],
         n_zc.at[pl.ds(0, across - 1)],
-    )
-    spreads.wait_recv()
-    spreads = group(
-        8,
-        [
-            (probe_out.at[c, i], probe_out.at[c, i], dict(row=lax.rem(i + o, rows_n)))
-            for o in range(1, rows_n)
-        ],
-        y_in.at[pl.ds(0, rows_n - 1)] if rows_n == beams else probe_out.at[0, pl.ds(0, rows_n - 1)],
     )
     spreads.wait_recv()
     last = go(
@@ -721,7 +729,7 @@
         functools.partial(fold_kernel, 1.0 / positions),
         out_shape=[
             jax.ShapeDtypeStruct((2, rows, lanes), jnp.float32),
-            jax.ShapeDtypeStruct((2, rows_n, beams, share, n), jnp.float32),
+            jax.ShapeDtypeStruct((2, plane, share, n), jnp.float32),
             jax.ShapeDtypeStruct((1, LANES), jnp.float32),
         ],
         in_specs=[pl.BlockSpec(memory_space=pltpu.VMEM)] * 4,
@@ -735,9 +743,8 @@
             f32((2, 2, rows // 2, lanes)),
             f32((beams, 2, h, lanes)),
             f32((n, n)),
-            f32((rows_n, beams, share, n)),
-            f32((beams, rows_n, share, n)),
-            f32((rows_n, share, n)),
+            f32((plane, share, n)),
+            f32((plane, share, n)),
             f32((deep_n, share, n)),
             f32((plane, 1, LANES)),
             f32((across, 1, LANES)),

time: 74.2 us -> 66.5 us (0.90)
  Pallas kernels: 73.4 us -> 65.8 us
    pallas_call x1, Pallas kernels: 13 us -> 8.27 us  [window_terms(): pl.pallas_call(window_kernel, grid_spec=grid_spec, out_shape=[jax.ShapeDt...]
    pallas_call x1, Pallas kernels: 23.3 us -> 21.4 us  [transmission(): pl.pallas_call(spread_kernel, out_shape=[jax.ShapeDtypeStruct((2, 3, 2 *...]
    pallas_call x1, Pallas kernels: 36.1 us -> 35.2 us  [folded(): pl.pallas_call(functools.partial(fold_kernel, 1.0 / positions), out_shape...]
where the time goes in v5:
time: 66.5 us
  Pallas kernels  65.8 us (99%)
  between operations  0.73 us (1%)
    pallas_call x1, Pallas kernels, folded(): pl.pallas_call(functools.partial(fold_kernel, 1.0 / positions), out_shape...  35.2 us
    pallas_call x1, Pallas kernels, transmission(): pl.pallas_call(spread_kernel, out_shape=[jax.ShapeDtypeStruct((2, 3, 2 *...  21.4 us
    pallas_call x1, Pallas kernels, window_terms(): pl.pallas_call(window_kernel, grid_spec=grid_spec, out_shape=[jax.ShapeDt...  8.27 us

profile of v5, /device:TPU:1, one launch (start us, length us, event | category | flops | bytes accessed | tf_op | source)
XLA Modules:
  0.0 66.5 jit_solution(15394265363366412160)
XLA Ops:
  0.6 0.0 copy-start.2
  0.6 0.0 copy-start.4
  0.7 0.0 copy-start.3
  0.7 0.0 copy-start
  0.7 0.0 copy-start.1
  0.7 21.4 %spread.1 = (f32[2,3,512,128]{3,2,1,0:T(8,128)S(1)}, f32[2,64,128]{2,1,0:T(8,128)S(1)}) custom-call(bf16[16,256,128]{2,1,0:T(8,128)(2,1)} %phase_ref.1, bf16[16,256,128]{2,1,0:T(8,128)(2,1)} %absorb_ref.1), custom_call_target="tpu_custom_call" | custom-call | tf_op jit(solution)/shard_map/spread/pallas_call | solution.py:410
  22.1 0.0 copy-done.2
  22.1 0.0 copy-done.4
  22.1 0.0 copy-done.3
  22.1 0.0 copy-done
  22.2 0.0 copy-done.1
  22.2 8.3 %windows.1 = (f32[2,3,512,128]{3,2,1,0:T(8,128)S(1)}, f32[2,256,256]{2,1,0:T(8,128)S(1)}, f32[8,128]{1,0:T(8,128)S(1)}) custom-call(s32[8]{0:T(128)S(1)} %bitcast.7, s32[8]{0:T(128)S(1)} %bitcast.8, f32[2,3,512,128]{3,2,1,0:T(8,128)S(1)} %get-tuple-element.14.t_ref, f32[2,256,256]{2,1,0:T(8,128)S(1)} %copy-done.1, bf16[8,256,256]{2,1,0:T(8,128)(2,1)S(1)} %bitcast.5, ...), custom_call_target="tpu_custom_call" | custom-call | tf_op jit(solution)/shard_map/windows/pallas_call | solution.py:167
  30.5 35.2 %fold.1 = (f32[2,256,128]{2,1,0:T(8,128)S(1)}, f32[2,16,16,256]{3,2,1,0:T(8,128)S(1)}, f32[1,128]{1,0:T(1,128)S(1)}) custom-call(f32[2,3,512,128]{3,2,1,0:T(8,128)S(1)} %get-tuple-element.15.canvas_ref, f32[2,64,128]{2,1,0:T(8,128)S(1)} %get-tuple-element.16.own_ref, f32[2,256,256]{2,1,0:T(8,128)S(1)} %get-tuple-element.17.probe_ref, ...), custom_call_target="tpu_custom_call" | custom-call | tf_op jit(solution)/shard_map/fold/pallas_call | solution.py:728
  65.6 0.9 %finish.1 = (f32[2,256,128]{2,1,0:T(8,128)}, f32[2,256,256]{2,1,0:T(8,128)}, f32[1,1]{1,0:T(1,128)}) custom-call(f32[2,256,128]{2,1,0:T(8,128)S(1)} %get-tuple-element.19.grad_ref, f32[2,256,256]{2,1,0:T(8,128)S(1)} %bitcast.6, f32[1,128]{1,0:T(1,128)S(1)} %get-tuple-element.21.sums_ref), custom_call_target="tpu_custom_call" | custom-call | tf_op jit(solution)/shard_map/finish/pallas_call | solution.py:774
Async XLA Ops:
  0.6 21.5 %copy-start.2 = (bf16[2,256,256]{2,1,0:T(8,128)(2,1)S(1)}, bf16[2,256,256]{2,1,0:T(8,128)(2,1)}, u32[]{:S(2)}) copy-start(bf16[2,256,256]{2,1,0:T(8,128)(2,1)} %constant.13.table_ref) | copy-start | bytes 786436
  0.6 21.5 %copy-start.4 = (s32[1,1,8]{2,1,0:T(1,128)S(1)}, s32[1,1,8]{2,1,0:T(1,128)}, u32[]{:S(2)}) copy-start(s32[1,1,8]{2,1,0:T(1,128)} %param.13) | copy-start | bytes 100
  0.7 21.5 %copy-start.3 = (s32[1,1,8]{2,1,0:T(1,128)S(1)}, s32[1,1,8]{2,1,0:T(1,128)}, u32[]{:S(2)}) copy-start(s32[1,1,8]{2,1,0:T(1,128)} %param.12) | copy-start | bytes 100
  0.7 21.5 %copy-start = (bf16[1,1,8,256,256]{4,3,2,1,0:T(8,128)(2,1)S(1)}, bf16[1,1,8,256,256]{4,3,2,1,0:T(8,128)(2,1)}, u32[]{:S(2)}) copy-start(bf16[1,1,8,256,256]{4,3,2,1,0:T(8,128)(2,1)} %param.11) | copy-start | bytes 3145732
  0.7 21.5 %copy-start.1 = (f32[2,256,256]{2,1,0:T(8,128)S(1)}, f32[2,256,256]{2,1,0:T(8,128)}, u32[]{:S(2)}) copy-start(f32[2,256,256]{2,1,0:T(8,128)} %probe_ref.1) | copy-start | bytes 1572868

commit v6 on v5

--- a/solution.py
+++ b/solution.py
@@ -15,6 +15,7 @@
 LANES = 128
 CHUNK = 128
 BATCH = 4
+SUBS = 2
 VMEM_LIMIT = 20 << 20
 
 
@@ -132,7 +133,7 @@
 
     steps = (cut_windows, to_half, to_far, to_back, add_terms)
     for tick in range(batch + len(steps) - 1):
-        for at, stage in reversed(list(enumerate(steps))):
+        for at, stage in enumerate(steps):
             if 0 <= tick - at < batch:
                 stage(tick - at)
 
@@ -205,24 +206,28 @@
 def spread_kernel(
     phase_ref, absorb_ref, t_ref, own_ref,
     vol, part, inbox,
-    vol_sem, sum_send, sum_recv, beam_send, near_send, out_send, row_send, t_recv,
+    vol_sem, sum_send, sum_recv, beam_send, near_send, rim_send, out_send, row_send, corner_send,
+    t_recv,
 ):
     beams, rows_n, deep_n, _ = sizes()
     b, i, z, c = places()
-    h = phase_ref.shape[1] // beams
+    subs, h = part.shape[1], part.shape[3]
+    quarter_rows = subs * h
     top = beams // 2
-    blocks = 2 * beams
-    half = top * h
+    half = top * quarter_rows
+    blocks = 2 * beams * subs
     out_z = z - 1 + 2 * c
     has_out = (out_z >= 0) & (out_z < deep_n)
     above, below = i > 0, i < rows_n - 1
+    outer = dict(col_0=out_z, col_1=1 - c)
     order = [*range(1, beams), 0]
     loads = {}
     for o in order:
         q = lax.rem(b + o, beams)
+        rows_here = pl.ds(pl.multiple_of(q * quarter_rows, quarter_rows), quarter_rows)
         for p, ref in enumerate((phase_ref, absorb_ref)):
             loads[o, p] = pltpu.make_async_copy(
-                ref.at[:, pl.ds(pl.multiple_of(q * h, h), h), :], vol.at[o, p], vol_sem.at[o, p]
+                ref.at[:, rows_here, :], vol.at[o, p], vol_sem.at[o, p]
             )
             loads[o, p].start()
 
@@ -233,7 +238,7 @@
 
     @pl.when(has_out)
     def _():
-        greet(barrier, col_0=out_z, col_1=1 - c)
+        greet(barrier, **outer)
 
     for alive, row in ((above, i - 1), (below, i + 1)):
 
@@ -243,7 +248,7 @@
 
         @pl.when(alive & has_out)
         def _(row=row):
-            greet(barrier, row=row, col_0=out_z, col_1=1 - c)
+            greet(barrier, row=row, **outer)
 
     for o in order:
         for p in range(2):
@@ -251,145 +256,125 @@
             total = vol[o, p, 0].astype(jnp.float32)
             for d in range(1, phase_ref.shape[0]):
                 total = total + vol[o, p, d].astype(jnp.float32)
-            part[o, p] = total
+            for s in range(subs):
+                part[o, s, p] = total[s * h : (s + 1) * h]
     ups, downs, outs = (flag.astype(jnp.int32) for flag in (above, below, has_out))
     pl.semaphore_wait(barrier, beams + outs + (1 + outs) * (ups + downs))
-    sums = []
-    for o in order[:-1]:
-        copy = remote(
-            part.at[o], inbox.at[o], sum_send.at[o], sum_recv.at[o], beam=lax.rem(b + o, beams)
-        )
-        copy.start()
-        sums.append(copy)
-    for copy in sums:
-        copy.wait_recv()
-    phase, absorb = part[0, 0], part[0, 1]
-    for o in range(1, beams):
-        phase = phase + inbox[o, 0]
-        absorb = absorb + inbox[o, 1]
-    damping = jnp.exp(-absorb)
-    tr, ti = damping * jnp.cos(phase), damping * jnp.sin(phase)
-    own_ref[0] = tr
-    own_ref[1] = ti
+    for s in range(subs):
+        for o in order[:-1]:
+            remote(
+                part.at[o, s], inbox.at[s, o], sum_send.at[s], sum_recv.at[s],
+                beam=lax.rem(b + o, beams),
+            ).start()
 
     def cell(k, m):
         return t_ref.at[:, k, pl.ds(pl.multiple_of(m * h, h), h), :]
 
-    mine = pl.ds(pl.multiple_of(half + b * h, h), h)
-    t_ref[0, 1, mine, :] = tr
-    t_ref[1, 1, mine, :] = ti
-    m0 = top + b
-    waits = []
-
-    def send(copy, check=None):
-        if check is None:
-            copy.start()
-        else:
-            pl.when(check)(copy.start)
-        waits.append((check, copy))
-
     def arrived(k, m, check=None):
-        wait = remote(cell(1, m), cell(k, m), near_send.at[0], t_recv.at[k, m], col_1=1 - c).wait_recv
+        wait = remote(cell(1, m), cell(k, m), near_send, t_recv.at[k, m], col_1=1 - c).wait_recv
         if check is None:
             wait()
         else:
             pl.when(check)(wait)
 
-    def both(first, second):
-        return second if first is None else first & second
-
-    def to_sibling(m, slot, check=None):
-        send(
-            remote(
-                cell(1, m), cell(2 * c, m), near_send.at[slot], t_recv.at[2 * c, m], col_1=1 - c
-            ),
-            check,
-        )
-
-    def to_outer(m, slot, check=None):
-        send(
-            remote(
-                cell(1, m), cell(2 - 2 * c, m), out_send.at[slot], t_recv.at[2 - 2 * c, m],
-                col_0=out_z, col_1=1 - c,
-            ),
-            both(check, has_out),
-        )
-
-    def quarter(o):
+    def spot(o, s):
         q = lax.rem(b + o, beams)
         upper = q // top
-        rim = q - top + (1 - upper) * blocks
+        rim = q * subs + s - top * subs + (1 - upper) * blocks
         goal, source = i - 1 + 2 * upper, i + 1 - 2 * upper
-        return top + q, rim, goal, (goal >= 0) & (goal < rows_n), (source >= 0) & (source < rows_n)
-
-    def to_row(o, k, slot, check=None):
-        m, rim, goal, alive, _ = quarter(o)
-        send(
-            remote(cell(k, m), cell(k, rim), row_send.at[slot], t_recv.at[k, rim], row=goal),
-            both(check, alive),
+        return (
+            top * subs + q * subs + s, rim, upper, goal,
+            (goal >= 0) & (goal < rows_n), (source >= 0) & (source < rows_n),
         )
 
     ring = [1, *range(3, beams), *range(2, min(3, beams))]
     by_row, direct = {0}, {2}
-    for o in ring:
-        send(
-            remote(
-                cell(1, m0), cell(1, m0), beam_send.at[o], t_recv.at[1, m0],
-                beam=lax.rem(b + o, beams),
-            )
-        )
-
-    def to_diagonal(o, slot):
-        m, rim, goal, alive, _ = quarter(o)
-        send(
-            remote(
-                cell(1, m), cell(2 - 2 * c, rim), out_send.at[slot], t_recv.at[2 - 2 * c, rim],
-                row=goal, col_0=out_z, col_1=1 - c,
-            ),
-            alive & has_out,
-        )
-
-    def spread_tile(o):
-        m = quarter(o)[0]
+    singles = []
+
+    def single(check, slot, src, k, m, **where):
+        copy = remote(src, cell(k, m), corner_send.at[slot], t_recv.at[k, m], **where)
+        pl.when(check)(copy.start)
+        singles.append((check, copy))
+
+    def tile(o, s):
+        m, rim, upper, goal, alive, _ = spot(o, s)
         if o:
             arrived(1, m)
-        to_outer(m, o)
-        to_row(o, 1, o)
+        far = remote(
+            cell(1, m), cell(2 - 2 * c, m), out_send, t_recv.at[2 - 2 * c, m], **outer
+        )
+        pl.when(has_out)(far.start)
+        side = remote(cell(1, m), cell(1, rim), row_send.at[upper], t_recv.at[1, rim], row=goal)
+        pl.when(alive)(side.start)
         if o in direct:
-            to_diagonal(o, beams + o)
-        to_sibling(m, o)
-
-    def spread_rim(o):
-        _, rim, _, _, alive = quarter(o)
+            single(
+                alive & has_out, o * subs + s, cell(1, m), 2 - 2 * c, rim, row=goal, **outer
+            )
+        remote(cell(1, m), cell(2 * c, m), near_send, t_recv.at[2 * c, m], col_1=1 - c).start()
+
+    def corner(o, s):
+        m, rim, _, goal, alive, _ = spot(o, s)
+        arrived(2 * c, m, has_out)
+        if o in by_row:
+            single(alive & has_out, o * subs + s, cell(2 * c, m), 2 * c, rim, row=goal)
+
+    def edge(o, s):
+        _, rim, upper, _, _, alive = spot(o, s)
         arrived(1, rim, alive)
         if o not in by_row and o not in direct:
-            to_outer(rim, beams + o, alive)
-        to_sibling(rim, beams + o, alive)
-
-    def spread_corner(o):
-        m = quarter(o)[0]
-        arrived(2 * c, m, has_out)
-        if o in by_row:
-            to_row(o, 2 * c, beams + o, has_out)
-
-    events = [(spread_tile, 0), (spread_tile, ring[0]), (spread_corner, 0), (spread_rim, 0)]
-    events += [(spread_tile, o) for o in ring[1:]]
-    for o in ring:
-        events += [(spread_corner, o), (spread_rim, o)]
-    for event, o in events:
-        event(o)
-    for o in range(beams):
-        m, rim, _, _, alive = quarter(o)
-        arrived(2 - 2 * c, m)
-        arrived(2 - 2 * c, rim, alive)
-        arrived(2 * c, rim, alive & has_out)
-    for copy in sums:
-        copy.wait_send()
-    for alive, copy in waits:
-        if alive is None:
-            copy.wait_send()
-        else:
-            pl.when(alive)(copy.wait_send)
+            single(alive & has_out, o * subs + s, cell(1, rim), 2 - 2 * c, rim, **outer)
+        copy = remote(
+            cell(1, rim), cell(2 * c, rim), rim_send.at[upper], t_recv.at[2 * c, rim], col_1=1 - c
+        )
+        pl.when(alive)(copy.start)
+
+    def total_of(like, send, recv):
+        return remote(like, like, send, recv, col_1=1 - c)
+
+    for s in range(subs):
+        sums = total_of(inbox.at[s, pl.ds(1, beams - 1)], sum_send.at[s], sum_recv.at[s])
+        sums.wait_recv()
+        phase, absorb = part[0, s, 0], part[0, s, 1]
+        for o in range(1, beams):
+            phase = phase + inbox[s, o, 0]
+            absorb = absorb + inbox[s, o, 1]
+        damping = jnp.exp(-absorb)
+        mine = pl.ds(pl.multiple_of(half + (b * subs + s) * h, h), h)
+        for p, value in enumerate((damping * jnp.cos(phase), damping * jnp.sin(phase))):
+            t_ref[p, 1, mine, :] = value
+            own_ref[p, pl.ds(s * h, h), :] = value
+        m = top * subs + b * subs + s
+        for o in ring:
+            remote(
+                cell(1, m), cell(1, m), beam_send, t_recv.at[1, m], beam=lax.rem(b + o, beams)
+            ).start()
+        tile(0, s)
+    events = []
+    for s in range(subs):
+        events += [(corner, 0, s), *[(tile, o, s) for o in ring if o not in direct], (edge, 0, s)]
+        events += [(tile, o, s) for o in ring if o in direct]
+    events += [(edge, o, s) for s in range(subs) for o in ring]
+    for event, o, s in events:
+        event(o, s)
+    for s in range(subs):
+        for o in range(beams):
+            m, rim, _, _, _, alive = spot(o, s)
+            if o:
+                corner(o, s)
+            arrived(2 - 2 * c, m)
+            arrived(2 - 2 * c, rim, alive)
+            arrived(2 * c, rim, alive & has_out)
+    for s in range(subs):
+        total_of(part.at[pl.ds(1, beams - 1), s], sum_send.at[s], sum_recv.at[s]).wait_send()
+    total_of(part.at[pl.ds(1, beams - 1)], beam_send, beam_send).wait_send()
+    total_of(part, near_send, near_send).wait_send()
+    pl.when(has_out)(total_of(part, out_send, out_send).wait_send)
+    for upper, (goal_here, source_here) in enumerate(((above, below), (below, above))):
+        like = part.at[pl.ds(0, top)]
+        pl.when(goal_here)(total_of(like, row_send.at[upper], row_send.at[upper]).wait_send)
+        pl.when(source_here)(total_of(like, rim_send.at[upper], rim_send.at[upper]).wait_send)
+    for check, copy in singles:
+        pl.when(check)(copy.wait_send)
     tall = blocks * h
 
     def blank(tiles, start, size):
@@ -406,27 +391,30 @@
 def transmission(phase_volume, absorb_volume):
     deep, rows, lanes = phase_volume.shape
     beams = lax.axis_size("beam")
-    h = rows // beams
+    h = rows // (beams * SUBS)
+    dma = pltpu.SemaphoreType.DMA
     return pl.pallas_call(
         spread_kernel,
         out_shape=[
             jax.ShapeDtypeStruct((2, 3, 2 * rows, lanes), jnp.float32),
-            jax.ShapeDtypeStruct((2, h, lanes), jnp.float32),
+            jax.ShapeDtypeStruct((2, SUBS * h, lanes), jnp.float32),
         ],
         in_specs=[pl.BlockSpec(memory_space=pltpu.HBM)] * 2,
         out_specs=[pl.BlockSpec(memory_space=pltpu.VMEM)] * 2,
         scratch_shapes=[
-            pltpu.VMEM((beams, 2, deep, h, lanes), jnp.bfloat16),
-            pltpu.VMEM((beams, 2, h, lanes), jnp.float32),
-            pltpu.VMEM((beams, 2, h, lanes), jnp.float32),
-            pltpu.SemaphoreType.DMA((beams, 2)),
-            pltpu.SemaphoreType.DMA((beams,)),
-            pltpu.SemaphoreType.DMA((beams,)),
-            pltpu.SemaphoreType.DMA((beams,)),
-            pltpu.SemaphoreType.DMA((2 * beams,)),
-            pltpu.SemaphoreType.DMA((2 * beams,)),
-            pltpu.SemaphoreType.DMA((2 * beams,)),
-            pltpu.SemaphoreType.DMA((3, 2 * beams)),
+            pltpu.VMEM((beams, 2, deep, SUBS * h, lanes), jnp.bfloat16),
+            pltpu.VMEM((beams, SUBS, 2, h, lanes), jnp.float32),
+            pltpu.VMEM((SUBS, beams, 2, h, lanes), jnp.float32),
+            dma((beams, 2)),
+            dma((SUBS,)),
+            dma((SUBS,)),
+            dma,
+            dma,
+            dma((2,)),
+            dma,
+            dma((2,)),
+            dma((beams * SUBS,)),
+            dma((3, 2 * beams * SUBS)),
         ],
         compiler_params=pltpu.CompilerParams(
             collective_id=0, has_side_effects=True, vmem_limit_bytes=VMEM_LIMIT

time: 66.5 us -> 64.1 us (0.964)
  Pallas kernels: 65.8 us -> 63.5 us
    pallas_call x1, Pallas kernels: 35.2 us -> 32.4 us  [folded(): pl.pallas_call(functools.partial(fold_kernel, 1.0 / positions), out_shape...]
where the time goes in v6:
time: 64.1 us; the launch traced here: 64.2 us
  Pallas kernels  63.5 us (99%)
  between operations  0.73 us (1%)
    pallas_call x1, Pallas kernels, folded(): pl.pallas_call(functools.partial(fold_kernel, 1.0 / positions), out_shape...  32.4 us
    pallas_call x1, Pallas kernels, transmission(): pl.pallas_call(spread_kernel, out_shape=[jax.ShapeDtypeStruct((2, 3, 2 *...  21.8 us
    pallas_call x1, Pallas kernels, window_terms(): pl.pallas_call(window_kernel, grid_spec=grid_spec, out_shape=[jax.ShapeDt...  8.28 us

profile of v6, /device:TPU:1, one launch (start us, length us, event | category | flops | bytes accessed | tf_op | source)
XLA Modules:
  0.0 64.2 jit_solution(13148245636785805265)
XLA Ops:
  0.6 0.0 copy-start.2
  0.6 0.0 copy-start.4
  0.7 0.0 copy-start.3
  0.7 0.0 copy-start
  0.7 0.0 copy-start.1
  0.7 21.8 %spread.1 = (f32[2,3,512,128]{3,2,1,0:T(8,128)S(1)}, f32[2,64,128]{2,1,0:T(8,128)S(1)}) custom-call(bf16[16,256,128]{2,1,0:T(8,128)(2,1)} %phase_ref.1, bf16[16,256,128]{2,1,0:T(8,128)(2,1)} %absorb_ref.1), custom_call_target="tpu_custom_call" | custom-call | tf_op jit(solution)/shard_map/spread/pallas_call | solution.py:396
  22.5 0.0 copy-done.2
  22.5 0.0 copy-done.4
  22.5 0.0 copy-done.3
  22.6 0.0 copy-done
  22.6 0.0 copy-done.1
  22.6 8.3 %windows.1 = (f32[2,3,512,128]{3,2,1,0:T(8,128)S(1)}, f32[2,256,256]{2,1,0:T(8,128)S(1)}, f32[8,128]{1,0:T(8,128)S(1)}) custom-call(s32[8]{0:T(128)S(1)} %bitcast.7, s32[8]{0:T(128)S(1)} %bitcast.8, f32[2,3,512,128]{3,2,1,0:T(8,128)S(1)} %get-tuple-element.14.t_ref, f32[2,256,256]{2,1,0:T(8,128)S(1)} %copy-done.1, bf16[8,256,256]{2,1,0:T(8,128)(2,1)S(1)} %bitcast.5, ...), custom_call_target="tpu_custom_call" | custom-call | tf_op jit(solution)/shard_map/windows/pallas_call | solution.py:168
  30.9 32.4 %fold.1 = (f32[2,256,128]{2,1,0:T(8,128)S(1)}, f32[2,16,16,256]{3,2,1,0:T(8,128)S(1)}, f32[1,128]{1,0:T(1,128)S(1)}) custom-call(f32[2,3,512,128]{3,2,1,0:T(8,128)S(1)} %get-tuple-element.15.canvas_ref, f32[2,64,128]{2,1,0:T(8,128)S(1)} %get-tuple-element.16.own_ref, f32[2,256,256]{2,1,0:T(8,128)S(1)} %get-tuple-element.17.probe_ref, ...), custom_call_target="tpu_custom_call" | custom-call | tf_op jit(solution)/shard_map/fold/pallas_call | solution.py:716
  63.3 0.9 %finish.1 = (f32[2,256,128]{2,1,0:T(8,128)}, f32[2,256,256]{2,1,0:T(8,128)}, f32[1,1]{1,0:T(1,128)}) custom-call(f32[2,256,128]{2,1,0:T(8,128)S(1)} %get-tuple-element.19.grad_ref, f32[2,256,256]{2,1,0:T(8,128)S(1)} %bitcast.6, f32[1,128]{1,0:T(1,128)S(1)} %get-tuple-element.21.sums_ref), custom_call_target="tpu_custom_call" | custom-call | tf_op jit(solution)/shard_map/finish/pallas_call | solution.py:762
Async XLA Ops:
  0.6 21.9 %copy-start.2 = (bf16[2,256,256]{2,1,0:T(8,128)(2,1)S(1)}, bf16[2,256,256]{2,1,0:T(8,128)(2,1)}, u32[]{:S(2)}) copy-start(bf16[2,256,256]{2,1,0:T(8,128)(2,1)} %constant.13.table_ref) | copy-start | bytes 786436
  0.6 21.9 %copy-start.4 = (s32[1,1,8]{2,1,0:T(1,128)S(1)}, s32[1,1,8]{2,1,0:T(1,128)}, u32[]{:S(2)}) copy-start(s32[1,1,8]{2,1,0:T(1,128)} %param.13) | copy-start | bytes 100
  0.7 21.9 %copy-start.3 = (s32[1,1,8]{2,1,0:T(1,128)S(1)}, s32[1,1,8]{2,1,0:T(1,128)}, u32[]{:S(2)}) copy-start(s32[1,1,8]{2,1,0:T(1,128)} %param.12) | copy-start | bytes 100
  0.7 21.9 %copy-start = (bf16[1,1,8,256,256]{4,3,2,1,0:T(8,128)(2,1)S(1)}, bf16[1,1,8,256,256]{4,3,2,1,0:T(8,128)(2,1)}, u32[]{:S(2)}) copy-start(bf16[1,1,8,256,256]{4,3,2,1,0:T(8,128)(2,1)} %param.11) | copy-start | bytes 3145732
  0.7 21.9 %copy-start.1 = (f32[2,256,256]{2,1,0:T(8,128)S(1)}, f32[2,256,256]{2,1,0:T(8,128)}, u32[]{:S(2)}) copy-start(f32[2,256,256]{2,1,0:T(8,128)} %probe_ref.1) | copy-start | bytes 1572868

commit v7 on v6

--- a/solution.py
+++ b/solution.py
@@ -429,7 +429,7 @@
 def fold_kernel(
     scale, canvas_ref, own_ref, probe_ref, misfit_ref,
     grad, probe_out, sums_ref,
-    sib_in, out_in, acc, corner_in, corner, row_in, q_in, p_in, p_sum, x_in, z_in, n_xy, n_zc,
+    sib_in, out_in, acc, corner_in, corner, row_in, q_in, p_in, p_sum, y_in, x_in, z_in, n_xy, n_zc,
     sib_send, sib_recv, out_send, out_recv, corner_send, corner_recv, row_send, row_recv,
     pair_send, pair_recv, group_send, group_recv,
 ):
@@ -477,11 +477,16 @@
     pl.semaphore_wait(barrier, plane + across - 2)
 
     middle = pl.ds(half, rows)
-    rims = [(pl.ds(0, half), above, i - 1), (pl.ds(tall - half, half), below, i + 1)]
+    subs = beams // 2
+    pieces = []
+    for s in range(subs):
+        pieces.append((s * h, above, i - 1, below, subs + s))
+        pieces.append((tall - half + s * h, below, i + 1, above, s))
     outer = dict(col_0=out_z, col_1=1 - c)
     half_copy = go(remote(probe_ref.at[1 - c], p_in, pair_send.at[0], pair_recv.at[0], col_1=1 - c))
     far_rims, near_rims, corners = [], [], []
-    for e, (where, alive, goal) in enumerate(rims):
+    for e, (start, alive, goal, _, _) in enumerate(pieces):
+        where = pl.ds(start, h)
         near_rims.append(
             go(
                 remote(
@@ -512,110 +517,135 @@
     far_first = go(
         remote(
             canvas_ref.at[0, 2 * c, middle, :], out_in.at[0, middle, :],
-            out_send.at[2], out_recv.at[2], **outer,
+            out_send.at[beams], out_recv.at[beams], **outer,
         ),
         has_out,
     )
     near_middle = go(
         remote(
             canvas_ref.at[:, 2 - 2 * c, middle, :], sib_in.at[:, middle, :],
-            sib_send.at[2], sib_recv.at[2], col_1=1 - c,
+            sib_send.at[beams], sib_recv.at[beams], col_1=1 - c,
         )
     )
     half_copy.wait_recv()
     p_sum[...] = (probe_ref[c] + p_in[...]).reshape(p_sum.shape)
-
-    edges = {}
-    for p in (1, 0):
-        for e, (where, alive, goal) in enumerate(rims):
-
-            def rim(p=p, e=e, where=where):
-                if p == 1:
-                    near_rims[e].wait_recv()
-                acc[p, where, :] = canvas_ref[p, 1, where, :] + sib_in[p, where, :]
-                if p == 0:
-
-                    @pl.when(has_out)
-                    def _():
-                        far_rims[e].wait_recv()
-                        acc[0, where, :] += out_in[0, where, :]
-
-            pl.when(alive)(rim)
-            edges[p, e] = go(
-                remote(
-                    acc.at[p, where, :], row_in.at[p, e],
-                    row_send.at[p, e], row_recv.at[p, e], row=goal,
-                ),
-                alive,
-            )
-    low, high = pl.ds(half, half), pl.ds(rows, half)
-
-    def at_xy(o):
-        peer = peer_xy(o)
-        return peer["beam"] * rows_n + peer["row"]
-
     parts = group(
         0,
-        [(p_sum.at[at_xy(o)], x_in.at[o], peer_xy(o)) for o in range(1, plane)],
-        x_in.at[pl.ds(1, plane - 1)],
-    )
-
-    @pl.when(has_out)
-    def _():
-        corner[...] = canvas_ref[1, 2 * c, middle, :]
-
-        @pl.when(below)
+        [
+            (p_sum.at[:, lax.rem(b + o, beams)], y_in.at[o], dict(beam=lax.rem(b + o, beams)))
+            for o in range(1, beams)
+        ],
+        y_in.at[pl.ds(1, beams - 1)],
+    )
+
+    edges, far_second = {}, {}
+
+    def rim(p, e):
+        start, alive, goal, _, _ = pieces[e]
+        where = pl.ds(start, h)
+
+        @pl.when(alive)
         def _():
-            corners[0].wait_recv()
-            corner[pl.ds(half, half), :] += corner_in[0]
-
-        @pl.when(above)
+            if p == 1:
+                near_rims[e].wait_recv()
+            acc[p, where, :] = canvas_ref[p, 1, where, :] + sib_in[p, where, :]
+            if p == 0:
+
+                @pl.when(has_out)
+                def _():
+                    far_rims[e].wait_recv()
+                    acc[0, where, :] += out_in[0, where, :]
+
+        edges[p, e] = go(
+            remote(
+                acc.at[p, where, :], row_in.at[p, e],
+                row_send.at[p, e], row_recv.at[p, e], row=goal,
+            ),
+            alive,
+        )
+
+    def corner_piece(e):
+        _, _, _, given, quarter = pieces[e]
+        inside, there = pl.ds(quarter * h, h), pl.ds(half + quarter * h, h)
+
+        @pl.when(has_out)
         def _():
-            corners[1].wait_recv()
-            corner[pl.ds(0, half), :] += corner_in[1]
-
-    far_second = go(
-        remote(
-            corner, out_in.at[1, middle, :], out_send.at[3], out_recv.at[3], **outer
-        ),
-        has_out,
-    )
+            corner[inside, :] = canvas_ref[1, 2 * c, there, :]
+
+            @pl.when(given)
+            def _():
+                corners[e].wait_recv()
+                corner[inside, :] += corner_in[e]
+
+        far_second[e] = go(
+            remote(
+                corner.at[inside, :], out_in.at[1, there, :],
+                out_send.at[beams + 1 + e], out_recv.at[beams + 1 + e], **outer,
+            ),
+            has_out,
+        )
+
+    for e in range(beams):
+        rim(1, e)
+    for e in range(beams):
+        rim(0, e)
+        corner_piece(e)
     near_middle.wait_recv()
     acc[:, middle, :] = canvas_ref[:, 1, middle, :] + sib_in[:, middle, :]
+
     @pl.when(has_out)
     def _():
         far_first.wait_recv()
         acc[0, middle, :] += out_in[0, middle, :]
 
-    for p in (1, 0):
-        for e, (alive, where) in enumerate(((below, high), (above, low))):
-
-            def settle(p=p, e=e, where=where):
+    quarters = remote(
+        q_in.at[pl.ds(1, beams - 1)], q_in.at[pl.ds(1, beams - 1)],
+        group_send.at[2], group_recv.at[2], col_1=1 - c,
+    )
+    finish.append((None, quarters))
+
+    def settle(e):
+        _, _, _, given, quarter = pieces[e]
+        there = pl.ds(half + quarter * h, h)
+
+        @pl.when(given)
+        def _():
+            for p in (1, 0):
                 edges[p, e].wait_recv()
-                acc[p, where, :] += row_in[p, e]
-
-            pl.when(alive)(settle)
-
-    @pl.when(has_out)
-    def _():
-        far_second.wait_recv()
-        acc[1, middle, :] += out_in[1, middle, :]
-
-    quarters = group(
-        2,
+                acc[p, there, :] += row_in[p, e]
+
+        @pl.when(has_out)
+        def _():
+            far_second[e].wait_recv()
+            acc[1, there, :] += out_in[1, there, :]
+
+        copy = remote(
+            acc.at[:, there, :], q_in.at[b], group_send.at[2], group_recv.at[2], beam=quarter
+        )
+        pl.when(b != quarter)(copy.start)
+
+    for e in range(2):
+        settle(e)
+    parts.wait_recv()
+    block = p_sum[:, b]
+    for o in range(1, beams):
+        block = block + y_in[o]
+    y_in[0] = block
+    parts = group(
+        1,
         [
-            (
-                acc.at[:, pl.ds(pl.multiple_of(half + lax.rem(b + o, beams) * h, h), h), :],
-                q_in.at[o],
-                dict(beam=lax.rem(b + o, beams)),
-            )
-            for o in [*range(2, beams), 1]
-        ],
-        q_in.at[pl.ds(1, beams - 1)],
-    )
+            (y_in.at[0, lax.rem(i + o, rows_n)], x_in.at[o], dict(row=lax.rem(i + o, rows_n)))
+            for o in range(1, rows_n)
+        ],
+        x_in.at[pl.ds(1, rows_n - 1)],
+    )
+    for e in range(2, beams):
+        settle(e)
+    mine = pl.ds(pl.multiple_of(half + b * h, h), h)
+    q_in[b] = acc[:, mine, :]
     parts.wait_recv()
-    total = p_sum[me_xy]
-    for o in range(1, plane):
+    total = y_in[0, i]
+    for o in range(1, rows_n):
         total = total + x_in[o]
     z_in[z] = total
     levels = group(
@@ -627,9 +657,8 @@
         z_in.at[pl.ds(0, deep_n - 1)],
     )
 
-    mine = pl.ds(pl.multiple_of(half + b * h, h), h)
     quarters.wait_recv()
-    cr, ci = acc[0, mine, :], acc[1, mine, :]
+    cr, ci = q_in[0, 0], q_in[0, 1]
     for o in range(1, beams):
         cr = cr + q_in[o, 0]
         ci = ci + q_in[o, 1]
@@ -653,16 +682,6 @@
         n_xy.at[pl.ds(0, plane - 1)],
     )
 
-    levels.wait_recv()
-    total = z_in[0]
-    for k in range(1, deep_n):
-        total = total + z_in[k]
-    probe_out[c, me_xy] = total * scale
-    spreads = group(
-        5,
-        [(probe_out.at[c, me_xy], probe_out.at[c, me_xy], peer_xy(o)) for o in range(1, plane)],
-        x_in.at[pl.ds(1, plane - 1)],
-    )
     grads = group(
         6,
         [
@@ -672,6 +691,16 @@
         q_in.at[pl.ds(1, beams - 1)],
     )
 
+    levels.wait_recv()
+    total = z_in[0]
+    for k in range(1, deep_n):
+        total = total + z_in[k]
+    probe_out[c, i, b] = total * scale
+    spreads = group(
+        5,
+        [(probe_out.at[c, i, b], probe_out.at[c, i, b], peer_xy(o)) for o in range(1, plane)],
+        p_in.at[pl.ds(0, (plane - 1) * p_sum.shape[2]), :],
+    )
     norms.wait_recv()
     pair = n_xy[0]
     for k in range(1, plane):
@@ -712,12 +741,14 @@
     plane, across = beams * rows_n, deep_n * cores
     share = n // plane
     f32 = functools.partial(pltpu.VMEM, dtype=jnp.float32)
-    sems = [(3,), (3,), (4,), (4,), (2,), (2,), (2, 2), (2, 2), (2,), (2,), (9,), (9,)]
+    outs, sides = 2 * beams + 1, beams + 1
+    sems = [(sides,), (sides,), (outs,), (outs,), (beams,), (beams,)]
+    sems += [(2, beams), (2, beams), (2,), (2,), (9,), (9,)]
     grad, probe_total, sums = pl.pallas_call(
         functools.partial(fold_kernel, 1.0 / positions),
         out_shape=[
             jax.ShapeDtypeStruct((2, rows, lanes), jnp.float32),
-            jax.ShapeDtypeStruct((2, plane, share, n), jnp.float32),
+            jax.ShapeDtypeStruct((2, rows_n, beams, share, n), jnp.float32),
             jax.ShapeDtypeStruct((1, LANES), jnp.float32),
         ],
         in_specs=[pl.BlockSpec(memory_space=pltpu.VMEM)] * 4,
@@ -726,13 +757,14 @@
             f32((2, tall, lanes)),
             f32((2, tall, lanes)),
             f32((2, tall, lanes)),
-            f32((2, rows // 2, lanes)),
+            f32((beams, h, lanes)),
             f32((rows, lanes)),
-            f32((2, 2, rows // 2, lanes)),
+            f32((2, beams, h, lanes)),
             f32((beams, 2, h, lanes)),
             f32((n, n)),
-            f32((plane, share, n)),
-            f32((plane, share, n)),
+            f32((rows_n, beams, share, n)),
+            f32((beams, rows_n, share, n)),
+            f32((rows_n, share, n)),
             f32((deep_n, share, n)),
             f32((plane, 1, LANES)),
             f32((across, 1, LANES)),

time: 64.1 us -> 63 us (0.983)
  Pallas kernels: 63.5 us -> 62.1 us
    pallas_call x1, Pallas kernels: 32.4 us -> 31.1 us  [folded(): pl.pallas_call(functools.partial(fold_kernel, 1.0 / positions), out_shape...]
where the time goes in v7:
time: 63 us; the launch traced here: 62.9 us
  Pallas kernels  62.1 us (99%)
  between operations  0.73 us (1%)
    pallas_call x1, Pallas kernels, folded(): pl.pallas_call(functools.partial(fold_kernel, 1.0 / positions), out_shape...  31.1 us
    pallas_call x1, Pallas kernels, transmission(): pl.pallas_call(spread_kernel, out_shape=[jax.ShapeDtypeStruct((2, 3, 2 *...  21.8 us
    pallas_call x1, Pallas kernels, window_terms(): pl.pallas_call(window_kernel, grid_spec=grid_spec, out_shape=[jax.ShapeDt...  8.24 us

profile of v7, /device:TPU:1, one launch (start us, length us, event | category | flops | bytes accessed | tf_op | source)
XLA Modules:
  0.0 62.9 jit_solution(6410169106851761343)
XLA Ops:
  0.6 0.0 copy-start.2
  0.6 0.0 copy-start.4
  0.7 0.0 copy-start.3
  0.7 0.0 copy-start
  0.7 0.0 copy-start.1
  0.7 21.8 %spread.1 = (f32[2,3,512,128]{3,2,1,0:T(8,128)S(1)}, f32[2,64,128]{2,1,0:T(8,128)S(1)}) custom-call(bf16[16,256,128]{2,1,0:T(8,128)(2,1)} %phase_ref.1, bf16[16,256,128]{2,1,0:T(8,128)(2,1)} %absorb_ref.1), custom_call_target="tpu_custom_call" | custom-call | tf_op jit(solution)/shard_map/spread/pallas_call | solution.py:396
  22.5 0.0 copy-done.2
  22.5 0.0 copy-done.4
  22.5 0.0 copy-done.3
  22.6 0.0 copy-done
  22.6 0.0 copy-done.1
  22.6 8.2 %windows.1 = (f32[2,3,512,128]{3,2,1,0:T(8,128)S(1)}, f32[2,256,256]{2,1,0:T(8,128)S(1)}, f32[8,128]{1,0:T(8,128)S(1)}) custom-call(s32[8]{0:T(128)S(1)} %bitcast.7, s32[8]{0:T(128)S(1)} %bitcast.8, f32[2,3,512,128]{3,2,1,0:T(8,128)S(1)} %get-tuple-element.14.t_ref, f32[2,256,256]{2,1,0:T(8,128)S(1)} %copy-done.1, bf16[8,256,256]{2,1,0:T(8,128)(2,1)S(1)} %bitcast.5, ...), custom_call_target="tpu_custom_call" | custom-call | tf_op jit(solution)/shard_map/windows/pallas_call | solution.py:168
  30.8 31.1 %fold.1 = (f32[2,256,128]{2,1,0:T(8,128)S(1)}, f32[2,4,4,16,256]{4,3,2,1,0:T(8,128)S(1)}, f32[1,128]{1,0:T(1,128)S(1)}) custom-call(f32[2,3,512,128]{3,2,1,0:T(8,128)S(1)} %get-tuple-element.15.canvas_ref, f32[2,64,128]{2,1,0:T(8,128)S(1)} %get-tuple-element.16.own_ref, f32[2,256,256]{2,1,0:T(8,128)S(1)} %get-tuple-element.17.probe_ref, ...), custom_call_target="tpu_custom_call" | custom-call | tf_op jit(solution)/shard_map/fold/pallas_call | solution.py:747
  61.9 0.9 %finish.1 = (f32[2,256,128]{2,1,0:T(8,128)}, f32[2,256,256]{2,1,0:T(8,128)}, f32[1,1]{1,0:T(1,128)}) custom-call(f32[2,256,128]{2,1,0:T(8,128)S(1)} %get-tuple-element.19.grad_ref, f32[2,256,256]{2,1,0:T(8,128)S(1)} %bitcast.6, f32[1,128]{1,0:T(1,128)S(1)} %get-tuple-element.21.sums_ref), custom_call_target="tpu_custom_call" | custom-call | tf_op jit(solution)/shard_map/finish/pallas_call | solution.py:794
Async XLA Ops:
  0.6 21.9 %copy-start.2 = (bf16[2,256,256]{2,1,0:T(8,128)(2,1)S(1)}, bf16[2,256,256]{2,1,0:T(8,128)(2,1)}, u32[]{:S(2)}) copy-start(bf16[2,256,256]{2,1,0:T(8,128)(2,1)} %constant.13.table_ref) | copy-start | bytes 786436
  0.6 21.9 %copy-start.4 = (s32[1,1,8]{2,1,0:T(1,128)S(1)}, s32[1,1,8]{2,1,0:T(1,128)}, u32[]{:S(2)}) copy-start(s32[1,1,8]{2,1,0:T(1,128)} %param.13) | copy-start | bytes 100
  0.7 21.9 %copy-start.3 = (s32[1,1,8]{2,1,0:T(1,128)S(1)}, s32[1,1,8]{2,1,0:T(1,128)}, u32[]{:S(2)}) copy-start(s32[1,1,8]{2,1,0:T(1,128)} %param.12) | copy-start | bytes 100
  0.7 21.9 %copy-start = (bf16[1,1,8,256,256]{4,3,2,1,0:T(8,128)(2,1)S(1)}, bf16[1,1,8,256,256]{4,3,2,1,0:T(8,128)(2,1)}, u32[]{:S(2)}) copy-start(bf16[1,1,8,256,256]{4,3,2,1,0:T(8,128)(2,1)} %param.11) | copy-start | bytes 3145732
  0.7 21.9 %copy-start.1 = (f32[2,256,256]{2,1,0:T(8,128)S(1)}, f32[2,256,256]{2,1,0:T(8,128)}, u32[]{:S(2)}) copy-start(f32[2,256,256]{2,1,0:T(8,128)} %probe_ref.1) | copy-start | bytes 1572868

commit v8 on v7

--- a/solution.py
+++ b/solution.py
@@ -431,7 +431,7 @@
     grad, probe_out, sums_ref,
     sib_in, out_in, acc, corner_in, corner, row_in, q_in, p_in, p_sum, y_in, x_in, z_in, n_xy, n_zc,
     sib_send, sib_recv, out_send, out_recv, corner_send, corner_recv, row_send, row_recv,
-    pair_send, pair_recv, group_send, group_recv,
+    pair_send, pair_recv, group_send, group_recv, word,
 ):
     beams, rows_n, deep_n, cores = sizes()
     b, i, z, c = places()
@@ -470,11 +470,23 @@
         return everything
 
     barrier = pltpu.get_barrier_semaphore()
-    for o in range(1, plane):
-        greet(barrier, **peer_xy(o))
-    for o in range(1, across):
-        greet(barrier, **peer_zc(o))
-    pl.semaphore_wait(barrier, plane + across - 2)
+    for o in range(1, beams):
+        greet(barrier, beam=lax.rem(b + o, beams))
+    for o in range(1, rows_n):
+        greet(barrier, row=lax.rem(i + o, rows_n))
+    greet(barrier, col_1=1 - c)
+    for o in (1, deep_n - 1):
+        greet(barrier, col_0=lax.rem(z + o, deep_n))
+
+    @pl.when(has_out)
+    def _():
+        greet(barrier, col_0=out_z, col_1=1 - c)
+
+    pl.semaphore_wait(barrier, beams + rows_n + 1 + has_out.astype(jnp.int32))
+    for o in range(1, rows_n):
+        greet(word.at[0], row=lax.rem(i + o, rows_n))
+    for o in (1, deep_n - 1):
+        greet(word.at[1], col_0=lax.rem(z + o, deep_n))
 
     middle = pl.ds(half, rows)
     subs = beams // 2
@@ -590,6 +602,9 @@
     for e in range(beams):
         rim(0, e)
         corner_piece(e)
+    pl.semaphore_wait(word.at[1], 2)
+    for o in (2, deep_n - 2):
+        greet(word.at[2], col_0=lax.rem(z + o, deep_n))
     near_middle.wait_recv()
     acc[:, middle, :] = canvas_ref[:, 1, middle, :] + sib_in[:, middle, :]
 
@@ -643,6 +658,8 @@
         settle(e)
     mine = pl.ds(pl.multiple_of(half + b * h, h), h)
     q_in[b] = acc[:, mine, :]
+    pl.semaphore_wait(word.at[0], rows_n - 1)
+    pl.semaphore_wait(word.at[2], 2)
     parts.wait_recv()
     total = y_in[0, i]
     for o in range(1, rows_n):
@@ -769,6 +786,7 @@
             f32((plane, 1, LANES)),
             f32((across, 1, LANES)),
             *[pltpu.SemaphoreType.DMA(count) for count in sems],
+            pltpu.SemaphoreType.REGULAR((3,)),
         ],
         compiler_params=pltpu.CompilerParams(
             collective_id=1, has_side_effects=True, vmem_limit_bytes=VMEM_LIMIT

time: 63 us -> 61.9 us (0.983)
  Pallas kernels: 62.1 us -> 61 us
    pallas_call x1, Pallas kernels: 31.1 us -> 30 us  [folded(): pl.pallas_call(functools.partial(fold_kernel, 1.0 / positions), out_shape...]
where the time goes in v8:
time: 61.9 us; the launch traced here: 61.8 us
  Pallas kernels  61 us (99%)
  between operations  0.73 us (1%)
    pallas_call x1, Pallas kernels, folded(): pl.pallas_call(functools.partial(fold_kernel, 1.0 / positions), out_shape...  30 us
    pallas_call x1, Pallas kernels, transmission(): pl.pallas_call(spread_kernel, out_shape=[jax.ShapeDtypeStruct((2, 3, 2 *...  21.8 us
    pallas_call x1, Pallas kernels, window_terms(): pl.pallas_call(window_kernel, grid_spec=grid_spec, out_shape=[jax.ShapeDt...  8.21 us

profile of v8, /device:TPU:1, one launch (start us, length us, event | category | flops | bytes accessed | tf_op | source)
XLA Modules:
  0.0 61.8 jit_solution(1265407078842706273)
XLA Ops:
  0.6 0.0 copy-start.2
  0.6 0.0 copy-start.4
  0.7 0.0 copy-start.3
  0.7 0.0 copy-start
  0.7 0.0 copy-start.1
  0.7 21.8 %spread.1 = (f32[2,3,512,128]{3,2,1,0:T(8,128)S(1)}, f32[2,64,128]{2,1,0:T(8,128)S(1)}) custom-call(bf16[16,256,128]{2,1,0:T(8,128)(2,1)} %phase_ref.1, bf16[16,256,128]{2,1,0:T(8,128)(2,1)} %absorb_ref.1), custom_call_target="tpu_custom_call" | custom-call | tf_op jit(solution)/shard_map/spread/pallas_call | solution.py:396
  22.5 0.0 copy-done.2
  22.5 0.0 copy-done.4
  22.5 0.0 copy-done.3
  22.6 0.0 copy-done
  22.6 0.0 copy-done.1
  22.6 8.2 %windows.1 = (f32[2,3,512,128]{3,2,1,0:T(8,128)S(1)}, f32[2,256,256]{2,1,0:T(8,128)S(1)}, f32[8,128]{1,0:T(8,128)S(1)}) custom-call(s32[8]{0:T(128)S(1)} %bitcast.7, s32[8]{0:T(128)S(1)} %bitcast.8, f32[2,3,512,128]{3,2,1,0:T(8,128)S(1)} %get-tuple-element.14.t_ref, f32[2,256,256]{2,1,0:T(8,128)S(1)} %copy-done.1, bf16[8,256,256]{2,1,0:T(8,128)(2,1)S(1)} %bitcast.5, ...), custom_call_target="tpu_custom_call" | custom-call | tf_op jit(solution)/shard_map/windows/pallas_call | solution.py:168
  30.8 30.0 %fold.1 = (f32[2,256,128]{2,1,0:T(8,128)S(1)}, f32[2,4,4,16,256]{4,3,2,1,0:T(8,128)S(1)}, f32[1,128]{1,0:T(1,128)S(1)}) custom-call(f32[2,3,512,128]{3,2,1,0:T(8,128)S(1)} %get-tuple-element.15.canvas_ref, f32[2,64,128]{2,1,0:T(8,128)S(1)} %get-tuple-element.16.own_ref, f32[2,256,256]{2,1,0:T(8,128)S(1)} %get-tuple-element.17.probe_ref, ...), custom_call_target="tpu_custom_call" | custom-call | tf_op jit(solution)/shard_map/fold/pallas_call | solution.py:764
  60.8 0.9 %finish.1 = (f32[2,256,128]{2,1,0:T(8,128)}, f32[2,256,256]{2,1,0:T(8,128)}, f32[1,1]{1,0:T(1,128)}) custom-call(f32[2,256,128]{2,1,0:T(8,128)S(1)} %get-tuple-element.19.grad_ref, f32[2,256,256]{2,1,0:T(8,128)S(1)} %bitcast.6, f32[1,128]{1,0:T(1,128)S(1)} %get-tuple-element.21.sums_ref), custom_call_target="tpu_custom_call" | custom-call | tf_op jit(solution)/shard_map/finish/pallas_call | solution.py:812
Async XLA Ops:
  0.6 21.9 %copy-start.2 = (bf16[2,256,256]{2,1,0:T(8,128)(2,1)S(1)}, bf16[2,256,256]{2,1,0:T(8,128)(2,1)}, u32[]{:S(2)}) copy-start(bf16[2,256,256]{2,1,0:T(8,128)(2,1)} %constant.13.table_ref) | copy-start | bytes 786436
  0.6 21.9 %copy-start.4 = (s32[1,1,8]{2,1,0:T(1,128)S(1)}, s32[1,1,8]{2,1,0:T(1,128)}, u32[]{:S(2)}) copy-start(s32[1,1,8]{2,1,0:T(1,128)} %param.13) | copy-start | bytes 100
  0.7 21.9 %copy-start.3 = (s32[1,1,8]{2,1,0:T(1,128)S(1)}, s32[1,1,8]{2,1,0:T(1,128)}, u32[]{:S(2)}) copy-start(s32[1,1,8]{2,1,0:T(1,128)} %param.12) | copy-start | bytes 100
  0.7 21.9 %copy-start = (bf16[1,1,8,256,256]{4,3,2,1,0:T(8,128)(2,1)S(1)}, bf16[1,1,8,256,256]{4,3,2,1,0:T(8,128)(2,1)}, u32[]{:S(2)}) copy-start(bf16[1,1,8,256,256]{4,3,2,1,0:T(8,128)(2,1)} %param.11) | copy-start | bytes 3145732
  0.7 21.9 %copy-start.1 = (f32[2,256,256]{2,1,0:T(8,128)S(1)}, f32[2,256,256]{2,1,0:T(8,128)}, u32[]{:S(2)}) copy-start(f32[2,256,256]{2,1,0:T(8,128)} %probe_ref.1) | copy-start | bytes 1572868

commit v9 on v8

--- a/solution.py
+++ b/solution.py
@@ -206,8 +206,8 @@
 def spread_kernel(
     phase_ref, absorb_ref, t_ref, own_ref,
     vol, part, inbox,
-    vol_sem, sum_send, sum_recv, beam_send, near_send, rim_send, out_send, row_send, corner_send,
-    t_recv,
+    vol_sem, sum_send, sum_recv, beam_send, near_send, near_recv, rim_send, rim_recv,
+    out_send, out_recv, own_recv, row_send, corner_send, corner_recv, t_recv,
 ):
     beams, rows_n, deep_n, _ = sizes()
     b, i, z, c = places()
@@ -270,8 +270,8 @@
     def cell(k, m):
         return t_ref.at[:, k, pl.ds(pl.multiple_of(m * h, h), h), :]
 
-    def arrived(k, m, check=None):
-        wait = remote(cell(1, m), cell(k, m), near_send, t_recv.at[k, m], col_1=1 - c).wait_recv
+    def arrived(m, check=None):
+        wait = remote(cell(1, m), cell(1, m), near_send, t_recv.at[m], col_1=1 - c).wait_recv
         if check is None:
             wait()
         else:
@@ -291,40 +291,42 @@
     by_row, direct = {0}, {2}
     singles = []
 
-    def single(check, slot, src, k, m, **where):
-        copy = remote(src, cell(k, m), corner_send.at[slot], t_recv.at[k, m], **where)
+    def single(check, slot, upper, src, dst, **where):
+        copy = remote(src, dst, corner_send.at[slot], corner_recv.at[upper], **where)
         pl.when(check)(copy.start)
         singles.append((check, copy))
 
     def tile(o, s):
         m, rim, upper, goal, alive, _ = spot(o, s)
         if o:
-            arrived(1, m)
-        far = remote(
-            cell(1, m), cell(2 - 2 * c, m), out_send, t_recv.at[2 - 2 * c, m], **outer
-        )
+            arrived(m)
+        landed = own_recv.at[s] if o in by_row else out_recv
+        far = remote(cell(1, m), cell(2 - 2 * c, m), out_send, landed, **outer)
         pl.when(has_out)(far.start)
-        side = remote(cell(1, m), cell(1, rim), row_send.at[upper], t_recv.at[1, rim], row=goal)
+        side = remote(cell(1, m), cell(1, rim), row_send.at[upper], t_recv.at[rim], row=goal)
         pl.when(alive)(side.start)
         if o in direct:
             single(
-                alive & has_out, o * subs + s, cell(1, m), 2 - 2 * c, rim, row=goal, **outer
+                alive & has_out, o * subs + s, upper, cell(1, m), cell(2 - 2 * c, rim),
+                row=goal, **outer,
             )
-        remote(cell(1, m), cell(2 * c, m), near_send, t_recv.at[2 * c, m], col_1=1 - c).start()
+        remote(cell(1, m), cell(2 * c, m), near_send, near_recv, col_1=1 - c).start()
 
     def corner(o, s):
-        m, rim, _, goal, alive, _ = spot(o, s)
-        arrived(2 * c, m, has_out)
-        if o in by_row:
-            single(alive & has_out, o * subs + s, cell(2 * c, m), 2 * c, rim, row=goal)
+        m, rim, upper, goal, alive, _ = spot(o, s)
+        here = cell(2 * c, m)
+        pl.when(has_out)(remote(here, here, out_send, own_recv.at[s], **outer).wait_recv)
+        single(alive & has_out, o * subs + s, upper, here, cell(2 * c, rim), row=goal)
 
     def edge(o, s):
         _, rim, upper, _, _, alive = spot(o, s)
-        arrived(1, rim, alive)
+        arrived(rim, alive)
         if o not in by_row and o not in direct:
-            single(alive & has_out, o * subs + s, cell(1, rim), 2 - 2 * c, rim, **outer)
+            single(
+                alive & has_out, o * subs + s, upper, cell(1, rim), cell(2 - 2 * c, rim), **outer
+            )
         copy = remote(
-            cell(1, rim), cell(2 * c, rim), rim_send.at[upper], t_recv.at[2 * c, rim], col_1=1 - c
+            cell(1, rim), cell(2 * c, rim), rim_send.at[upper], rim_recv.at[upper], col_1=1 - c
         )
         pl.when(alive)(copy.start)
 
@@ -346,7 +348,7 @@
         m = top * subs + b * subs + s
         for o in ring:
             remote(
-                cell(1, m), cell(1, m), beam_send, t_recv.at[1, m], beam=lax.rem(b + o, beams)
+                cell(1, m), cell(1, m), beam_send, t_recv.at[m], beam=lax.rem(b + o, beams)
             ).start()
         tile(0, s)
     events = []
@@ -356,23 +358,23 @@
     events += [(edge, o, s) for s in range(subs) for o in ring]
     for event, o, s in events:
         event(o, s)
-    for s in range(subs):
-        for o in range(beams):
-            m, rim, _, _, _, alive = spot(o, s)
-            if o:
-                corner(o, s)
-            arrived(2 - 2 * c, m)
-            arrived(2 - 2 * c, rim, alive)
-            arrived(2 * c, rim, alive & has_out)
+    most = part.at[pl.ds(1, beams - 1)]
+    some = part.at[pl.ds(0, top)]
+    total_of(part, near_send, near_recv).wait_recv()
+    pl.when(has_out)(total_of(most, out_send, out_recv).wait_recv)
+    for upper, source_here in enumerate((below, above)):
+        pl.when(source_here)(total_of(some, rim_send.at[upper], rim_recv.at[upper]).wait_recv)
+        pl.when(source_here & has_out)(
+            total_of(some, rim_send.at[upper], corner_recv.at[upper]).wait_recv
+        )
     for s in range(subs):
         total_of(part.at[pl.ds(1, beams - 1), s], sum_send.at[s], sum_recv.at[s]).wait_send()
-    total_of(part.at[pl.ds(1, beams - 1)], beam_send, beam_send).wait_send()
+    total_of(most, beam_send, beam_send).wait_send()
     total_of(part, near_send, near_send).wait_send()
     pl.when(has_out)(total_of(part, out_send, out_send).wait_send)
     for upper, (goal_here, source_here) in enumerate(((above, below), (below, above))):
-        like = part.at[pl.ds(0, top)]
-        pl.when(goal_here)(total_of(like, row_send.at[upper], row_send.at[upper]).wait_send)
-        pl.when(source_here)(total_of(like, rim_send.at[upper], rim_send.at[upper]).wait_send)
+        pl.when(goal_here)(total_of(some, row_send.at[upper], row_send.at[upper]).wait_send)
+        pl.when(source_here)(total_of(some, rim_send.at[upper], rim_send.at[upper]).wait_send)
     for check, copy in singles:
         pl.when(check)(copy.wait_send)
     tall = blocks * h
@@ -410,11 +412,16 @@
             dma((SUBS,)),
             dma,
             dma,
+            dma,
+            dma((2,)),
             dma((2,)),
             dma,
+            dma,
+            dma((SUBS,)),
             dma((2,)),
             dma((beams * SUBS,)),
-            dma((3, 2 * beams * SUBS)),
+            dma((2,)),
+            dma((2 * beams * SUBS,)),
         ],
         compiler_params=pltpu.CompilerParams(
             collective_id=0, has_side_effects=True, vmem_limit_bytes=VMEM_LIMIT
@@ -713,10 +720,23 @@
     for k in range(1, deep_n):
         total = total + z_in[k]
     probe_out[c, i, b] = total * scale
+    share = p_sum.shape[2]
+    own_piece = probe_out.at[c, i, b]
+    near_by = [o for o in range(1, plane) if o % rows_n != rows_n // 2]
+    far_off = [o for o in range(1, plane) if o % rows_n == rows_n // 2]
     spreads = group(
         5,
-        [(probe_out.at[c, i, b], probe_out.at[c, i, b], peer_xy(o)) for o in range(1, plane)],
-        p_in.at[pl.ds(0, (plane - 1) * p_sum.shape[2]), :],
+        [(own_piece, own_piece, peer_xy(o)) for o in near_by],
+        p_in.at[pl.ds(0, len(near_by) * share), :],
+    )
+    far_pieces = group(
+        8,
+        [
+            (own_piece, own_piece, dict(peer_xy(o), col_1=core))
+            for core in (c, 1 - c)
+            for o in far_off
+        ],
+        p_in.at[pl.ds(0, 2 * len(far_off) * share), :],
     )
     norms.wait_recv()
     pair = n_xy[0]
@@ -732,8 +752,18 @@
         n_zc.at[pl.ds(0, across - 1)],
     )
     spreads.wait_recv()
-    last = go(
-        remote(probe_out.at[c], probe_out.at[c], pair_send.at[1], pair_recv.at[1], col_1=1 - c)
+    last = group(
+        9,
+        [
+            (
+                probe_out.at[c, lax.rem(i + o, rows_n)],
+                probe_out.at[c, lax.rem(i + o, rows_n)],
+                dict(col_1=1 - c),
+            )
+            for o in range(rows_n)
+            if o != rows_n // 2
+        ],
+        probe_out.at[0, pl.ds(0, rows_n - 1)],
     )
     norms.wait_recv()
     pair = n_zc[0]
@@ -741,6 +771,7 @@
         pair = pair + n_zc[k]
     sums_ref[...] = pair
     grads.wait_recv()
+    far_pieces.wait_recv()
     last.wait_recv()
     for check, copy in finish:
         if check is None:
@@ -760,7 +791,7 @@
     f32 = functools.partial(pltpu.VMEM, dtype=jnp.float32)
     outs, sides = 2 * beams + 1, beams + 1
     sems = [(sides,), (sides,), (outs,), (outs,), (beams,), (beams,)]
-    sems += [(2, beams), (2, beams), (2,), (2,), (9,), (9,)]
+    sems += [(2, beams), (2, beams), (1,), (1,), (10,), (10,)]
     grad, probe_total, sums = pl.pallas_call(
         functools.partial(fold_kernel, 1.0 / positions),
         out_shape=[

time: 61.9 us -> 60.9 us (0.984)
  Pallas kernels: 61 us -> 60 us
    pallas_call x1, Pallas kernels: 30 us -> 29.2 us  [folded(): pl.pallas_call(functools.partial(fold_kernel, 1.0 / positions), out_shape...]
where the time goes in v9:
time: 60.9 us; the launch traced here: 60.8 us
  Pallas kernels  60 us (99%)
  between operations  0.73 us (1%)
    pallas_call x1, Pallas kernels, folded(): pl.pallas_call(functools.partial(fold_kernel, 1.0 / positions), out_shape...  29.2 us
    pallas_call x1, Pallas kernels, transmission(): pl.pallas_call(spread_kernel, out_shape=[jax.ShapeDtypeStruct((2, 3, 2 *...  21.6 us
    pallas_call x1, Pallas kernels, window_terms(): pl.pallas_call(window_kernel, grid_spec=grid_spec, out_shape=[jax.ShapeDt...  8.27 us

profile of v9, /device:TPU:1, one launch (start us, length us, event | category | flops | bytes accessed | tf_op | source)
XLA Modules:
  0.0 60.8 jit_solution(1578052846120631629)
XLA Ops:
  0.6 0.0 copy-start.2
  0.6 0.0 copy-start.4
  0.7 0.0 copy-start.3
  0.7 0.0 copy-start
  0.7 0.0 copy-start.1
  0.7 21.6 %spread.1 = (f32[2,3,512,128]{3,2,1,0:T(8,128)S(1)}, f32[2,64,128]{2,1,0:T(8,128)S(1)}) custom-call(bf16[16,256,128]{2,1,0:T(8,128)(2,1)} %phase_ref.1, bf16[16,256,128]{2,1,0:T(8,128)(2,1)} %absorb_ref.1), custom_call_target="tpu_custom_call" | custom-call | tf_op jit(solution)/shard_map/spread/pallas_call | solution.py:398
  22.3 0.0 copy-done.2
  22.3 0.0 copy-done.4
  22.3 0.0 copy-done.3
  22.3 0.0 copy-done
  22.3 0.0 copy-done.1
  22.4 8.3 %windows.1 = (f32[2,3,512,128]{3,2,1,0:T(8,128)S(1)}, f32[2,256,256]{2,1,0:T(8,128)S(1)}, f32[8,128]{1,0:T(8,128)S(1)}) custom-call(s32[8]{0:T(128)S(1)} %bitcast.7, s32[8]{0:T(128)S(1)} %bitcast.8, f32[2,3,512,128]{3,2,1,0:T(8,128)S(1)} %get-tuple-element.14.t_ref, f32[2,256,256]{2,1,0:T(8,128)S(1)} %copy-done.1, bf16[8,256,256]{2,1,0:T(8,128)(2,1)S(1)} %bitcast.5, ...), custom_call_target="tpu_custom_call" | custom-call | tf_op jit(solution)/shard_map/windows/pallas_call | solution.py:168
  30.6 29.2 %fold.1 = (f32[2,256,128]{2,1,0:T(8,128)S(1)}, f32[2,4,4,16,256]{4,3,2,1,0:T(8,128)S(1)}, f32[1,128]{1,0:T(1,128)S(1)}) custom-call(f32[2,3,512,128]{3,2,1,0:T(8,128)S(1)} %get-tuple-element.15.canvas_ref, f32[2,64,128]{2,1,0:T(8,128)S(1)} %get-tuple-element.16.own_ref, f32[2,256,256]{2,1,0:T(8,128)S(1)} %get-tuple-element.17.probe_ref, ...), custom_call_target="tpu_custom_call" | custom-call | tf_op jit(solution)/shard_map/fold/pallas_call | solution.py:795
  59.9 0.9 %finish.1 = (f32[2,256,128]{2,1,0:T(8,128)}, f32[2,256,256]{2,1,0:T(8,128)}, f32[1,1]{1,0:T(1,128)}) custom-call(f32[2,256,128]{2,1,0:T(8,128)S(1)} %get-tuple-element.19.grad_ref, f32[2,256,256]{2,1,0:T(8,128)S(1)} %bitcast.6, f32[1,128]{1,0:T(1,128)S(1)} %get-tuple-element.21.sums_ref), custom_call_target="tpu_custom_call" | custom-call | tf_op jit(solution)/shard_map/finish/pallas_call | solution.py:843
Async XLA Ops:
  0.6 21.7 %copy-start.2 = (bf16[2,256,256]{2,1,0:T(8,128)(2,1)S(1)}, bf16[2,256,256]{2,1,0:T(8,128)(2,1)}, u32[]{:S(2)}) copy-start(bf16[2,256,256]{2,1,0:T(8,128)(2,1)} %constant.13.table_ref) | copy-start | bytes 786436
  0.6 21.7 %copy-start.4 = (s32[1,1,8]{2,1,0:T(1,128)S(1)}, s32[1,1,8]{2,1,0:T(1,128)}, u32[]{:S(2)}) copy-start(s32[1,1,8]{2,1,0:T(1,128)} %param.13) | copy-start | bytes 100
  0.7 21.7 %copy-start.3 = (s32[1,1,8]{2,1,0:T(1,128)S(1)}, s32[1,1,8]{2,1,0:T(1,128)}, u32[]{:S(2)}) copy-start(s32[1,1,8]{2,1,0:T(1,128)} %param.12) | copy-start | bytes 100
  0.7 21.7 %copy-start = (bf16[1,1,8,256,256]{4,3,2,1,0:T(8,128)(2,1)S(1)}, bf16[1,1,8,256,256]{4,3,2,1,0:T(8,128)(2,1)}, u32[]{:S(2)}) copy-start(bf16[1,1,8,256,256]{4,3,2,1,0:T(8,128)(2,1)} %param.11) | copy-start | bytes 3145732
  0.7 21.7 %copy-start.1 = (f32[2,256,256]{2,1,0:T(8,128)S(1)}, f32[2,256,256]{2,1,0:T(8,128)}, u32[]{:S(2)}) copy-start(f32[2,256,256]{2,1,0:T(8,128)} %probe_ref.1) | copy-start | bytes 1572868

commit v10 on v9

--- a/solution.py
+++ b/solution.py
@@ -14,8 +14,8 @@
 MESH = pl.DeviceIdType.MESH
 LANES = 128
 CHUNK = 128
-BATCH = 4
-SUBS = 2
+BATCH = 8
+SUBS = 4
 VMEM_LIMIT = 20 << 20
 
 
@@ -466,6 +466,10 @@
     def peer_xy(o):
         return dict(beam=lax.rem(b + o // rows_n, beams), row=lax.rem(i + o % rows_n, rows_n))
 
+    def reach(o):
+        ob, oi = o // rows_n, o % rows_n
+        return -min(ob, beams - ob) - min(oi, rows_n - oi)
+
     def peer_zc(o):
         return dict(col_0=lax.rem(z + o // cores, deep_n), col_1=lax.rem(c + o % cores, cores))
 
@@ -702,7 +706,7 @@
     )
     norms = group(
         4,
-        [(n_xy.at[me_xy], n_xy.at[me_xy], peer_xy(o)) for o in range(1, plane)],
+        [(n_xy.at[me_xy], n_xy.at[me_xy], peer_xy(o)) for o in sorted(range(1, plane), key=reach)],
         n_xy.at[pl.ds(0, plane - 1)],
     )
 

time: 60.9 us -> 61.5 us (level); the launches traced: 60.8 us -> 62.2 us
  Pallas kernels: 60 us -> 61.4 us
    pallas_call x1, Pallas kernels: 29.2 us -> 31.1 us  [folded(): pl.pallas_call(functools.partial(fold_kernel, 1.0 / positions), out_shape...]
where the time goes in v10:
time: 61.5 us; the launch traced here: 62.2 us
  Pallas kernels  61.4 us (100%)
  between operations  0.73 us (1%)
    pallas_call x1, Pallas kernels, folded(): pl.pallas_call(functools.partial(fold_kernel, 1.0 / positions), out_shape...  31.1 us
    pallas_call x1, Pallas kernels, transmission(): pl.pallas_call(spread_kernel, out_shape=[jax.ShapeDtypeStruct((2, 3, 2 *...  21.3 us
    pallas_call x1, Pallas kernels, window_terms(): pl.pallas_call(window_kernel, grid_spec=grid_spec, out_shape=[jax.ShapeDt...  8.11 us

profile of v10, /device:TPU:1, one launch (start us, length us, event | category | flops | bytes accessed | tf_op | source)
XLA Modules:
  0.0 62.2 jit_solution(8837408275580063390)
XLA Ops:
  0.6 0.0 copy-start.2
  0.6 0.0 copy-start.4
  0.7 0.0 copy-start.3
  0.7 0.0 copy-start
  0.7 0.0 copy-start.1
  0.7 21.3 %spread.1 = (f32[2,3,512,128]{3,2,1,0:T(8,128)S(1)}, f32[2,64,128]{2,1,0:T(8,128)S(1)}) custom-call(bf16[16,256,128]{2,1,0:T(8,128)(2,1)} %phase_ref.1, bf16[16,256,128]{2,1,0:T(8,128)(2,1)} %absorb_ref.1), custom_call_target="tpu_custom_call" | custom-call | tf_op jit(solution)/shard_map/spread/pallas_call | solution.py:398
  22.0 0.0 copy-done.2
  22.0 0.0 copy-done.4
  22.0 0.0 copy-done.3
  22.0 0.0 copy-done
  22.0 0.0 copy-done.1
  22.0 8.1 %windows.1 = (f32[2,3,512,128]{3,2,1,0:T(8,128)S(1)}, f32[2,256,256]{2,1,0:T(8,128)S(1)}, f32[8,128]{1,0:T(8,128)S(1)}) custom-call(s32[8]{0:T(128)S(1)} %bitcast.7, s32[8]{0:T(128)S(1)} %bitcast.8, f32[2,3,512,128]{3,2,1,0:T(8,128)S(1)} %get-tuple-element.14.t_ref, f32[2,256,256]{2,1,0:T(8,128)S(1)} %copy-done.1, bf16[8,256,256]{2,1,0:T(8,128)(2,1)S(1)} %bitcast.5, ...), custom_call_target="tpu_custom_call" | custom-call | tf_op jit(solution)/shard_map/windows/pallas_call | solution.py:168
  30.2 31.1 %fold.1 = (f32[2,256,128]{2,1,0:T(8,128)S(1)}, f32[2,4,4,16,256]{4,3,2,1,0:T(8,128)S(1)}, f32[1,128]{1,0:T(1,128)S(1)}) custom-call(f32[2,3,512,128]{3,2,1,0:T(8,128)S(1)} %get-tuple-element.15.canvas_ref, f32[2,64,128]{2,1,0:T(8,128)S(1)} %get-tuple-element.16.own_ref, f32[2,256,256]{2,1,0:T(8,128)S(1)} %get-tuple-element.17.probe_ref, ...), custom_call_target="tpu_custom_call" | custom-call | tf_op jit(solution)/shard_map/fold/pallas_call | solution.py:799
  61.3 0.9 %finish.1 = (f32[2,256,128]{2,1,0:T(8,128)}, f32[2,256,256]{2,1,0:T(8,128)}, f32[1,1]{1,0:T(1,128)}) custom-call(f32[2,256,128]{2,1,0:T(8,128)S(1)} %get-tuple-element.19.grad_ref, f32[2,256,256]{2,1,0:T(8,128)S(1)} %bitcast.6, f32[1,128]{1,0:T(1,128)S(1)} %get-tuple-element.21.sums_ref), custom_call_target="tpu_custom_call" | custom-call | tf_op jit(solution)/shard_map/finish/pallas_call | solution.py:847
Async XLA Ops:
  0.6 21.4 %copy-start.2 = (bf16[2,256,256]{2,1,0:T(8,128)(2,1)S(1)}, bf16[2,256,256]{2,1,0:T(8,128)(2,1)}, u32[]{:S(2)}) copy-start(bf16[2,256,256]{2,1,0:T(8,128)(2,1)} %constant.13.table_ref) | copy-start | bytes 786436
  0.6 21.4 %copy-start.4 = (s32[1,1,8]{2,1,0:T(1,128)S(1)}, s32[1,1,8]{2,1,0:T(1,128)}, u32[]{:S(2)}) copy-start(s32[1,1,8]{2,1,0:T(1,128)} %param.13) | copy-start | bytes 100
  0.7 21.4 %copy-start.3 = (s32[1,1,8]{2,1,0:T(1,128)S(1)}, s32[1,1,8]{2,1,0:T(1,128)}, u32[]{:S(2)}) copy-start(s32[1,1,8]{2,1,0:T(1,128)} %param.12) | copy-start | bytes 100
  0.7 21.4 %copy-start = (bf16[1,1,8,256,256]{4,3,2,1,0:T(8,128)(2,1)S(1)}, bf16[1,1,8,256,256]{4,3,2,1,0:T(8,128)(2,1)}, u32[]{:S(2)}) copy-start(bf16[1,1,8,256,256]{4,3,2,1,0:T(8,128)(2,1)} %param.11) | copy-start | bytes 3145732
  0.7 21.4 %copy-start.1 = (f32[2,256,256]{2,1,0:T(8,128)S(1)}, f32[2,256,256]{2,1,0:T(8,128)}, u32[]{:S(2)}) copy-start(f32[2,256,256]{2,1,0:T(8,128)} %probe_ref.1) | copy-start | bytes 1572868
